TPU v7x, 32 devices: a whole 2x2x4 slice. The times are simulated.
32 devices in a mesh: row: 8 (over z, core), col: 4 (over y, x).
Axes of the slice: x: 2, y: 2, z: 4, core: 2. Of those that a mesh axis runs over, the one named last changes fastest.
Arguments:
- fine_residual: float32 [16, 3, 1572864], P(None, None, ('row', 'col')), may hold values from -6 to 6
- restriction: float32 [3, 3, 1572864], P(None, None, ('row', 'col')), may hold values from -1.25 to 1.25
- restriction_pattern: int32 [1572864], P(('row', 'col')), may hold values 0 or 1
- cell_aggregate: int32 [384, 512], P('row', 'col'), may hold values from 0 to 196607, as said below
- block_inverse: float32 [3, 3, 384, 512], P(None, None, 'row', 'col'), may hold values from -4 to 4, as said below
- off_blocks: float32 [4, 3, 3, 384, 512], P(None, None, None, 'row', 'col'), may hold values from -0.5 to 0.5
- operator_pattern: int32 [4, 384, 512], P(None, 'row', 'col'), may hold values 0 or 1
Outputs:
- coarse_solution: float32 [16, 3, 384, 512], P(None, None, 'row', 'col')
- fine_correction: float32 [16, 3, 1572864], P(None, None, ('row', 'col'))
Inputs may be any that keep to these rules, and one draw needn't show every extreme that they name: `cell_aggregate`: every aggregate number 0 to 196607 stands in exactly one coarse cell. Aggregate g = f * 6144 + a lies in the tile numbered a mod 32, where the tile of rows i * 48 to (i + 1) * 48 - 1 and columns j * 128 to (j + 1) * 128 - 1 is numbered i * 4 + j. `block_inverse`: each 3x3 block is the inverse of a cell's diagonal block.
All inputs are finite; a program needn't handle non-finite values. No bound on the sum of `restriction_pattern` or of `operator_pattern` on one device may be relied on, other than what follows from the above.
Results may differ from a plain program's by a relative error of at most 0.00002.
Values sent between devices are 32-bit elements; how exact they have to be, the bound alone decides.
No kernel may reach another device: no remote copies, remote signals or barrier semaphores. Data moves between devices by JAX's collectives and lax.ppermute only.
A program may use at most 128 MiB of HBM per device.

v0:
```python
import functools

import jax
import jax.numpy as jnp
from jax import lax
from jax.experimental import pallas as pl
from jax.experimental.pallas import tpu as pltpu
from jax.sharding import PartitionSpec as P

FPA = 8
ITERS = 4
LANES = 128
CHUNKS = 2
AXES = ("row", "col")


def vmem_spec():
    return pl.BlockSpec(memory_space=pltpu.VMEM)


class Sizes:
    def __init__(self, fine, loads, rows, cols, rows_n, cols_n):
        self.devices = rows_n * cols_n
        self.rows_n, self.cols_n = rows_n, cols_n
        self.fine = fine
        self.agg = fine // FPA
        self.blocks = self.agg // LANES
        self.loads = loads
        self.rows, self.cols = rows, cols
        self.q = loads // CHUNKS
        self.comps = 3 * self.q
        self.group = LANES // self.q
        self.groups = self.blocks // self.group
        self.low = LANES // self.devices
        self.per_peer = 3 * self.groups * self.low
        self.depth = ITERS - 1
        self.wide = rows + 2 * self.depth


def for_tiles(s, visit):
    for comp in range(3):
        for grp in range(s.groups):
            starts = []
            for low in range(s.low):
                slot = (comp * s.groups + grp) * s.low + low
                for first in range(0, s.devices, 8):
                    starts.append(first * s.per_peer + slot)
            visit(comp, grp, starts)


def store_tiles(s, out_ref, tile_of):
    def visit(comp, grp, starts):
        turned = tile_of(comp, grp).T
        for at, start in enumerate(starts):
            out_ref[pl.ds(start, 8, stride=s.per_peer), :] = turned[at * 8 : at * 8 + 8]

    for_tiles(s, visit)


def load_tiles(s, in_ref, take):
    def visit(comp, grp, starts):
        parts = [in_ref[pl.ds(start, 8, stride=s.per_peer), :] for start in starts]
        take(comp, grp, jnp.concatenate(parts, axis=0).T)

    for_tiles(s, visit)


def restrict_kernel(s, x_ref, rest_ref, pat_ref, out_ref, acc):
    step = pl.program_id(0)

    @pl.when(step == 0)
    def _():
        acc[...] = jnp.zeros_like(acc)

    def column(block, carry):
        at = pl.ds(pl.multiple_of(block * LANES, LANES), LANES)
        mask = pat_ref[0:1, at].astype(jnp.float32)
        value = [x_ref[comp, :, at] for comp in range(3)]
        for comp in range(3):
            total = acc[comp, :, at]
            for source in range(3):
                total = total + (rest_ref[comp, source : source + 1, at] * mask) * value[source]
            acc[comp, :, at] = total
        return carry

    lax.fori_loop(0, s.blocks, column, 0)

    @pl.when(step == FPA - 1)
    def _():
        def tile_of(comp, grp):
            parts = []
            for member in range(s.group):
                low = (grp * s.group + member) * LANES
                parts.append(acc[comp, :, low : low + LANES])
            return jnp.concatenate(parts, axis=0)

        store_tiles(s, out_ref, tile_of)


def restrict(s, residual, restriction, pattern, chunk):
    return pl.pallas_call(
        functools.partial(restrict_kernel, s),
        grid=(FPA,),
        in_specs=[
            pl.BlockSpec((3, s.q, s.agg), lambda p: (0, chunk, p)),
            pl.BlockSpec((3, 3, s.agg), lambda p: (0, 0, p)),
            pl.BlockSpec((1, s.agg), lambda p: (0, p)),
        ],
        out_specs=pl.BlockSpec((s.devices * s.per_peer, LANES), lambda p: (0, 0)),
        out_shape=jax.ShapeDtypeStruct((s.devices * s.per_peer, LANES), jnp.float32),
        scratch_shapes=[pltpu.VMEM((3, s.q, s.agg), jnp.float32)],
        name="restrict",
    )(residual, restriction, pattern)


def prolong_kernel(s, in_ref, rest_ref, pat_ref, out_ref, agg):
    step = pl.program_id(0)

    @pl.when(step == 0)
    def _():
        def take(comp, grp, turned):
            for member in range(s.group):
                low = (grp * s.group + member) * LANES
                agg[comp, :, low : low + LANES] = turned[member * s.q : (member + 1) * s.q]

        load_tiles(s, in_ref, take)

    def column(block, carry):
        at = pl.ds(pl.multiple_of(block * LANES, LANES), LANES)
        mask = pat_ref[0:1, at].astype(jnp.float32)
        value = [agg[comp, :, at] for comp in range(3)]
        for comp in range(3):
            total = (rest_ref[0, comp : comp + 1, at] * mask) * value[0]
            for source in range(1, 3):
                total = total + (rest_ref[source, comp : comp + 1, at] * mask) * value[source]
            out_ref[comp, :, at] = total
        return carry

    lax.fori_loop(0, s.blocks, column, 0)


def prolong(s, arrived, restriction, pattern, chunk, whole):
    kernel = functools.partial(prolong_kernel, s)
    specs = [
        vmem_spec(),
        pl.BlockSpec((3, 3, s.agg), lambda p: (0, 0, p)),
        pl.BlockSpec((1, s.agg), lambda p: (0, p)),
    ]
    args = [arrived, restriction, pattern]
    alias = {}
    body = kernel
    if whole is not None:
        specs.append(pl.BlockSpec(memory_space=pl.ANY))
        args.append(whole)
        alias = {3: 0}

        def body(in_ref, rest_ref, pat_ref, whole_ref, out_ref, agg):
            del whole_ref
            kernel(in_ref, rest_ref, pat_ref, out_ref, agg)

    return pl.pallas_call(
        body,
        grid=(FPA,),
        in_specs=specs,
        out_specs=pl.BlockSpec((3, s.q, s.agg), lambda p: (0, chunk, p)),
        out_shape=jax.ShapeDtypeStruct((3, s.loads, s.fine), jnp.float32),
        scratch_shapes=[pltpu.VMEM((3, s.q, s.agg), jnp.float32)],
        input_output_aliases=alias,
        name="prolong",
    )(*args)


def gather_rows(s, table_ref, row_ref, lane_ref, out_ref, count):
    def one(k, carry):
        rows = jnp.broadcast_to(row_ref[pl.ds(k, 1), :], (8, LANES))
        lanes = jnp.broadcast_to(lane_ref[pl.ds(k, 1), :], (8, LANES))
        parts = s.comps // 8
        total = [jnp.zeros((8, LANES), jnp.float32) for _ in range(parts)]
        for source in range(count):
            hit = rows == source
            for part in range(parts):
                moved = jnp.take_along_axis(
                    table_ref[source, part * 8 : part * 8 + 8, :],
                    lanes,
                    axis=1,
                    mode="promise_in_bounds",
                )
                total[part] = jnp.where(hit, moved, total[part])
        for part in range(parts):
            out_ref[k, part * 8 : part * 8 + 8, :] = total[part]
        return carry

    lax.fori_loop(0, count, one, 0)


def collect_kernel(s, in_ref, row_ref, lane_ref, out_ref, table):
    def take(comp, grp, turned):
        for member in range(s.group):
            block = grp * s.group + member
            table[block, comp * s.q : (comp + 1) * s.q, :] = turned[member * s.q : (member + 1) * s.q]

    load_tiles(s, in_ref, take)
    gather_rows(s, table, row_ref, lane_ref, out_ref, s.rows)


def collect(s, received, row, lane):
    return pl.pallas_call(
        functools.partial(collect_kernel, s),
        in_specs=[vmem_spec()] * 3,
        out_specs=vmem_spec(),
        out_shape=jax.ShapeDtypeStruct((s.rows, s.comps, LANES), jnp.float32),
        scratch_shapes=[pltpu.VMEM((s.blocks, s.comps, LANES), jnp.float32)],
        name="collect",
    )(received, row, lane)


PACK = 32
EDGE = LANES // PACK


def pack_kernel(s, body_ref, before_ref, after_ref, left_ref, right_ref):
    where = lax.broadcasted_iota(jnp.int32, (s.comps, LANES), 1) // EDGE
    packs = left_ref.shape[0]
    for pack in range(packs):
        left = jnp.zeros((s.comps, LANES), jnp.float32)
        right = jnp.zeros((s.comps, LANES), jnp.float32)
        for member in range(PACK):
            at = pack * PACK + member
            if at >= s.wide:
                break
            if at < s.depth:
                line = before_ref[at]
            elif at < s.depth + s.rows:
                line = body_ref[at - s.depth]
            else:
                line = after_ref[at - s.depth - s.rows]
            here = where == member
            left = jnp.where(here, pltpu.roll(line, member * EDGE, 1) if member else line, left)
            turn = (member + 1) * EDGE
            right = jnp.where(here, pltpu.roll(line, turn, 1) if turn < LANES else line, right)
        left_ref[pack] = left
        right_ref[pack] = right


def pack_edges(s, body, before, after):
    packs = -(-s.wide // PACK)
    shape = jax.ShapeDtypeStruct((packs, s.comps, LANES), jnp.float32)
    return pl.pallas_call(
        functools.partial(pack_kernel, s),
        in_specs=[vmem_spec()] * 3,
        out_specs=[vmem_spec()] * 2,
        out_shape=[shape, shape],
        name="pack_edges",
    )(body, before, after)


def sweeps_kernel(
    s, rhs_ref, before_ref, after_ref, left_ref, right_ref, coef_ref, row_ref, lane_ref,
    sol_ref, out_ref, wide, even, odd, final, back,
):
    lane = lax.broadcasted_iota(jnp.int32, (s.comps, LANES), 1)
    for at in range(s.wide):
        if at < s.depth:
            line = before_ref[at]
        elif at < s.depth + s.rows:
            line = rhs_ref[at - s.depth]
        else:
            line = after_ref[at - s.depth - s.rows]
        pack, member = divmod(at, PACK)
        past = right_ref[pack]
        if member:
            past = pltpu.roll(past, LANES - member * EDGE, 1)
        ahead = left_ref[pack]
        turn = (member + 1) * EDGE
        if turn < LANES:
            ahead = pltpu.roll(ahead, LANES - turn, 1)
        wide[at, :, 0:LANES] = line
        wide[at, :, LANES : 2 * LANES] = jnp.where(
            lane < s.depth, past, jnp.where(lane >= LANES - s.depth, ahead, 0.0)
        )

    q = s.q

    def coefficient(at, index, width):
        return coef_ref[at, index : index + 1, 0:width]

    def invert(at, total, width):
        fresh = []
        for comp in range(3):
            value = coefficient(at, comp * 3, width) * total[0]
            for source in range(1, 3):
                value = value + coefficient(at, comp * 3 + source, width) * total[source]
            fresh.append(value)
        return fresh

    def first(at, carry):
        total = [wide[at, comp * q : (comp + 1) * q, :] for comp in range(3)]
        fresh = invert(at, total, 2 * LANES)
        for comp in range(3):
            even[at, comp * q : (comp + 1) * q, :] = fresh[comp]
        return carry

    lax.fori_loop(0, s.wide, first, 0)

    def sweep(old, at, width):
        pieces = [[] for _ in range(4)]
        for source in range(3):
            part = slice(source * q, (source + 1) * q)
            pieces[0].append(old[at - 1, part, 0:width])
            pieces[1].append(old[at + 1, part, 0:width])
            here = old[at, part, :]
            pieces[2].append(pltpu.roll(here, 1, 1)[:, 0:width])
            pieces[3].append(pltpu.roll(here, 2 * LANES - 1, 1)[:, 0:width])
        total = []
        for comp in range(3):
            value = wide[at, comp * q : (comp + 1) * q, 0:width]
            for direction in range(4):
                for source in range(3):
                    index = 9 + (direction * 3 + comp) * 3 + source
                    value = value - coefficient(at, index, width) * pieces[direction][source]
            total.append(value)
        return invert(at, total, width)

    old, new = even, odd
    for inner in range(1, s.depth):
        def middle(at, carry, old=old, new=new):
            fresh = sweep(old, at, 2 * LANES)
            for comp in range(3):
                new[at, comp * q : (comp + 1) * q, :] = fresh[comp]
            return carry

        lax.fori_loop(inner, s.wide - inner, middle, 0)
        old, new = new, old

    def last(k, carry):
        fresh = sweep(old, k + s.depth, LANES)
        for comp in range(3):
            final[k, comp * q : (comp + 1) * q, :] = fresh[comp]
            for low in range(0, q, 8):
                start = (low * 3 + comp) * s.rows + k
                sol_ref[pl.ds(start, 8, stride=3 * s.rows), :] = fresh[comp][low : low + 8]
        return carry

    lax.fori_loop(0, s.rows, last, 0)

    gather_rows(s, final, row_ref, lane_ref, back, s.blocks)

    def tile_of(comp, grp):
        parts = []
        for member in range(s.group):
            parts.append(back[grp * s.group + member, comp * q : (comp + 1) * q, :])
        return jnp.concatenate(parts, axis=0)

    store_tiles(s, out_ref, tile_of)


def sweeps(s, rhs, before, after, left, right, coefs, row, lane):
    state = pltpu.VMEM((s.wide, s.comps, 2 * LANES), jnp.float32)
    tile = pltpu.VMEM((s.rows, s.comps, LANES), jnp.float32)
    return pl.pallas_call(
        functools.partial(sweeps_kernel, s),
        in_specs=[vmem_spec()] * 8,
        out_specs=[vmem_spec()] * 2,
        out_shape=[
            jax.ShapeDtypeStruct((s.q * 3 * s.rows, LANES), jnp.float32),
            jax.ShapeDtypeStruct((s.devices * s.per_peer, LANES), jnp.float32),
        ],
        scratch_shapes=[state, state, state, tile, tile],
        name="sweeps",
    )(rhs, before, after, left, right, coefs, row, lane)


def invert_kernel(count, slot_ref, out_ref):
    def some(at, carry):
        for step in range(8):
            k = at * 8 + step
            out_ref[slot_ref[k]] = k
        return carry

    lax.fori_loop(0, count // 8, some, 0)


def invert_permutation(slots):
    count = slots.shape[0]
    return pl.pallas_call(
        functools.partial(invert_kernel, count),
        in_specs=[pl.BlockSpec(memory_space=pltpu.SMEM)],
        out_specs=pl.BlockSpec(memory_space=pltpu.SMEM),
        out_shape=jax.ShapeDtypeStruct((count,), jnp.int32),
        name="invert_permutation",
    )(slots)


def ring(axis):
    count = lax.axis_size(axis)
    up = [(i, i + 1) for i in range(count - 1)]
    return up, [(j, i) for i, j in up]


def wide_coefficients(s, inverse, blocks, pattern):
    coupling = blocks * pattern.astype(jnp.float32)[:, None, None]
    coefs = jnp.concatenate([inverse.reshape(9, s.rows, s.cols), coupling.reshape(36, s.rows, s.cols)])
    coefs = coefs.transpose(1, 0, 2)
    up, down = ring("row")
    before = lax.ppermute(coefs[-s.depth :], "row", up)
    after = lax.ppermute(coefs[: s.depth], "row", down)
    coefs = jnp.concatenate([before, coefs, after])
    up, down = ring("col")
    ahead = lax.ppermute(coefs[..., -s.depth :].transpose(2, 1, 0), "col", up).transpose(2, 1, 0)
    past = lax.ppermute(coefs[..., : s.depth].transpose(2, 1, 0), "col", down).transpose(2, 1, 0)
    gap = jnp.zeros(coefs.shape[:2] + (LANES - 2 * s.depth,), jnp.float32)
    return jnp.concatenate([coefs, past, gap, ahead], axis=2)


def exchange(s, outgoing):
    blocks = outgoing.reshape(s.devices, s.per_peer, LANES)
    moved = lax.all_to_all(blocks, AXES, split_axis=0, concat_axis=0, tiled=True)
    return moved.reshape(s.devices * s.per_peer, LANES)


def body(
    fine_residual,
    restriction,
    restriction_pattern,
    cell_aggregate,
    block_inverse,
    off_blocks,
    operator_pattern,
):
    s = Sizes(
        fine_residual.shape[2],
        fine_residual.shape[0],
        cell_aggregate.shape[0],
        cell_aggregate.shape[1],
        lax.axis_size("row"),
        lax.axis_size("col"),
    )
    residual = fine_residual.transpose(1, 0, 2)
    pattern = restriction_pattern.reshape(1, -1)

    received = []
    for chunk in range(CHUNKS):
        received.append(exchange(s, restrict(s, residual, restriction, pattern, chunk)))

    owner = cell_aggregate // s.agg
    local = cell_aggregate % s.agg
    row = local // LANES
    lane = local % LANES // s.devices * s.devices + owner
    back = invert_permutation((row * LANES + lane).reshape(-1)).reshape(s.blocks, LANES)
    coefs = wide_coefficients(s, block_inverse, off_blocks, operator_pattern)

    row_up, row_down = ring("row")
    col_up, col_down = ring("col")
    solutions = []
    arrived = []
    for chunk in range(CHUNKS):
        rhs = collect(s, received[chunk], row, lane)
        before = lax.ppermute(rhs[-s.depth :], "row", row_up)
        after = lax.ppermute(rhs[: s.depth], "row", row_down)
        left, right = pack_edges(s, rhs, before, after)
        ahead = lax.ppermute(right, "col", col_up)
        past = lax.ppermute(left, "col", col_down)
        sol, outgoing = sweeps(s, rhs, before, after, ahead, past, coefs, back // LANES, back % LANES)
        solutions.append(sol.reshape(s.q, 3, s.rows, LANES))
        arrived.append(exchange(s, outgoing))
    correction = None
    for chunk in range(CHUNKS):
        correction = prolong(s, arrived[chunk], restriction, pattern, chunk, correction)
    return jnp.concatenate(solutions), correction.transpose(1, 0, 2)


def solution(mesh):
    in_specs = (
        P(None, None, AXES),
        P(None, None, AXES),
        P(AXES),
        P("row", "col"),
        P(None, None, "row", "col"),
        P(None, None, None, "row", "col"),
        P(None, "row", "col"),
    )
    out_specs = (P(None, None, "row", "col"), P(None, None, AXES))
    return jax.shard_map(body, mesh=mesh, in_specs=in_specs, out_specs=out_specs, check_vma=False)
```

profile of v0, /device:TPU:0, one launch (start us, length us, event | category | flops | bytes accessed | tf_op | source)
XLA Modules:
  0.0 239.6 jit_solution(16645252562114651994)
XLA Ops:
  0.6 9.0 %restrict.2 = f32[1152,128]{1,0:T(8,128)} custom-call(f32[3,16,49152]{2,1,0:T(8,128)} %bitcast.43, f32[3,3,49152]{2,1,0:T(4,128)} %rest_ref.7, s32[1,49152]{1,0:T(1,128)} %bitcast.49), custom_call_target="tpu_custom_call" | custom-call | tf_op jit(solution)/shard_map/restrict/pallas_call | solution.py:101
  9.7 2.0 reshape.51
  11.7 7.3 %all-to-all-start = ((f32[32,36,128]{2,1,0:T(8,128)}), f32[32,36,128]{2,1,0:T(8,128)S(1)}, u32[]{:S(2)}, u32[]{:S(2)}) async-start(f32[32,36,128]{2,1,0:T(8,128)} %reshape.51), calls=%async_computation | async-start | bytes 1310720 | tf_op jit(solution)/shard_map/all_to_all | solution.py:417
  19.6 2.2 collective-permute-start.4
  21.8 1.3 collective-permute-start.5
  23.1 0.7 add_bitcast_fusion
  23.8 9.0 %restrict.3 = f32[1152,128]{1,0:T(8,128)} custom-call(f32[3,16,49152]{2,1,0:T(8,128)} %bitcast.44, f32[3,3,49152]{2,1,0:T(4,128)} %rest_ref.7, s32[1,49152]{1,0:T(1,128)} %bitcast.50), custom_call_target="tpu_custom_call" | custom-call | tf_op jit(solution)/shard_map/restrict/pallas_call | solution.py:101
  32.8 12.1 %invert_permutation.1 = s32[6144]{0:T(1024)} custom-call(s32[6144]{0:T(1024)} %get-tuple-element.18.slot_ref), custom_call_target="tpu_custom_call" | custom-call | tf_op jit(solution)/shard_map/invert_permutation/pallas_call | solution.py:385
  44.9 1.9 reshape.58
  46.9 7.9 %all-to-all-start.1 = ((f32[32,36,128]{2,1,0:T(8,128)}), f32[32,36,128]{2,1,0:T(8,128)S(1)}, u32[]{:S(2)}, u32[]{:S(2)}) async-start(f32[32,36,128]{2,1,0:T(8,128)} %reshape.58), calls=%async_computation.1 | async-start | bytes 1310720 | tf_op jit(solution)/shard_map/all_to_all | solution.py:417
  55.0 1.5 slice_bitcast_fusion.1
  56.4 2.5 %copy.16 = f32[3,45,54]{2,1,0:T(8,128)} copy(f32[3,45,54]{0,1,2:T(8,128)} %get-tuple-element.20) | data formatting | bytes 58320 | tf_op jit(solution)/shard_map/transpose | solution.py:410
  59.6 3.8 %collective-permute-start.7 = (f32[3,45,54]{2,1,0:T(8,128)S(1)}, f32[3,45,54]{2,1,0:T(8,128)S(1)}, u32[]{:S(2)}, u32[]{:S(2)}) collective-permute-start(f32[3,45,54]{2,1,0:T(8,128)S(1)} %copy.18), channel_id=1, source_target_pairs={{0,1},{1,2},{2,3},{4,5},{5,6},{6,7},{8,9},{9,10},{10,11},{12,13},{... | collective-permute-start | bytes 87488 | tf_op jit(solution)/shard_map/ppermute | solution.py:409
  63.4 1.3 collective-permute-start.6
  64.7 1.9 reshape.52.in_ref
  66.7 12.8 %collect.2.body_ref.rhs_ref = f32[48,24,128]{2,1,0:T(8,128)} custom-call(f32[1152,128]{1,0:T(8,128)} %reshape.52.in_ref, s32[48,128]{1,0:T(8,128)} %get-tuple-element.30.row_ref, s32[48,128]{1,0:T(8,128)} %get-tuple-element.19.lane_ref), custom_call_target="tpu_custom_call" | custom-call | tf_op jit(solution)/shard_map/collect/pallas_call | solution.py:207
  79.5 1.4 fusion.12
  80.9 1.3 collective-permute-start.1
  82.2 3.0 %collective-permute-start = (f32[3,24,128]{2,1,0:T(8,128)}, f32[3,24,128]{2,1,0:T(8,128)S(1)}, u32[]{:S(2)}, u32[]{:S(2)}) collective-permute-start(f32[3,24,128]{2,1,0:T(8,128)} %get-tuple-element.25), channel_id=1, source_target_pairs={{0,4},{4,8},{8,12},{12,16},{16,20},{20,24},{24,28},{1,5},{5,9},{9,... | collective-permute-start | bytes 110600 | tf_op jit(solution)/shard_map/ppermute | solution.py:458
  86.0 1.6 copy.17
  87.5 1.7 copy.19
  90.5 2.1 pack_edges.2
  92.6 4.5 %collective-permute-start.2 = (f32[2,24,128]{2,1,0:T(8,128)}, f32[2,24,128]{2,1,0:T(8,128)S(1)}, u32[]{:S(2)}, u32[]{:S(2)}) collective-permute-start(f32[2,24,128]{2,1,0:T(8,128)} %get-tuple-element.10), channel_id=1, source_target_pairs={{0,1},{1,2},{2,3},{4,5},{5,6},{6,7},{8,9},{9,10},{10,11},{12,13},{... | collective-permute-start | bytes 73736 | tf_op jit(solution)/shard_map/ppermute | solution.py:461
  97.1 1.3 collective-permute-start.3
  98.4 3.3 %pad_maximum_fusion.coef_ref = f32[54,45,256]{2,1,0:T(8,128)} fusion(f32[54,45,3]{2,1,0:T(8,128)} %bitcast.47, f32[54,45,3]{2,1,0:T(8,128)S(1)} %bitcast.46, f32[3,45,128]{2,1,0:T(8,128)S(1)} %collective-permute-done.5, f32[48,45,128]{2,1,0:T(8,128)S(1)} %maximum_bitcast_fusion, f32[3,45,128]{2,1,0:T(8,128)S(1)} %collective-permute-done.4, f32[256]{0:T(256)S(1)} %pad.6.clone), kind=kLoop, calls=%fused_computation | loop fusion | flops 3110400 | bytes 3791824 | tf_op jit(solution)/shard_map/concatenate | solution.py:412
  101.8 1.8 collective-permute-done.3.right_ref
  104.2 28.3 %sweeps.2 = (f32[1152,128]{1,0:T(8,128)}, f32[1152,128]{1,0:T(8,128)}) custom-call(f32[48,24,128]{2,1,0:T(8,128)} %collect.2.body_ref.rhs_ref, f32[3,24,128]{2,1,0:T(8,128)} %copy-done.6, f32[3,24,128]{2,1,0:T(8,128)} %copy-done.5, f32[2,24,128]{2,1,0:T(8,128)} %copy-done.12, f32[2,24,128]{2,1,0:T(8,128)} %copy-done.13, ...), custom_call_target="tpu_custom_call" | custom-call | tf_op jit(solution)/shard_map/sweeps/pallas_call | solution.py:360
  132.5 1.9 reshape.63
  134.4 5.9 %all-to-all-start.3 = ((f32[32,36,128]{2,1,0:T(8,128)}), f32[32,36,128]{2,1,0:T(8,128)S(1)}, u32[]{:S(2)}, u32[]{:S(2)}) async-start(f32[32,36,128]{2,1,0:T(8,128)} %reshape.63), calls=%async_computation.3 | async-start | bytes 1310720 | tf_op jit(solution)/shard_map/all_to_all | solution.py:417
  140.4 0.9 reshape.59.in_ref
  141.2 12.9 %collect.3.body_ref.rhs_ref = f32[48,24,128]{2,1,0:T(8,128)} custom-call(f32[1152,128]{1,0:T(8,128)} %reshape.59.in_ref, s32[48,128]{1,0:T(8,128)} %get-tuple-element.30.row_ref, s32[48,128]{1,0:T(8,128)} %get-tuple-element.19.lane_ref), custom_call_target="tpu_custom_call" | custom-call | tf_op jit(solution)/shard_map/collect/pallas_call | solution.py:207
  154.1 0.8 fusion.13
  154.9 1.3 collective-permute-start.9
  156.1 3.0 %collective-permute-start.8 = (f32[3,24,128]{2,1,0:T(8,128)S(1)}, f32[3,24,128]{2,1,0:T(8,128)S(1)}, u32[]{:S(2)}, u32[]{:S(2)}) collective-permute-start(f32[3,24,128]{2,1,0:T(8,128)S(1)} %get-tuple-element.27), channel_id=1, source_target_pairs={{0,4},{4,8},{8,12},{12,16},{16,20},{20,24},{24,28},{1,5},{5,9},{9,... | collective-permute-start | bytes 110600 | tf_op jit(solution)/shard_map/ppermute | solution.py:458
  159.2 0.8 collective-permute-done.8.before_ref
  160.6 2.1 pack_edges.3
  162.8 3.7 %collective-permute-start.10 = (f32[2,24,128]{2,1,0:T(8,128)}, f32[2,24,128]{2,1,0:T(8,128)S(1)}, u32[]{:S(2)}, u32[]{:S(2)}) collective-permute-start(f32[2,24,128]{2,1,0:T(8,128)} %get-tuple-element.13), channel_id=1, source_target_pairs={{0,1},{1,2},{2,3},{4,5},{5,6},{6,7},{8,9},{9,10},{10,11},{12,13},{... | collective-permute-start | bytes 73736 | tf_op jit(solution)/shard_map/ppermute | solution.py:461
  166.4 1.3 collective-permute-start.11
  168.1 4.2 %collective-permute-done.11.right_ref = f32[2,24,128]{2,1,0:T(8,128)S(1)} collective-permute-done((f32[2,24,128]{2,1,0:T(8,128)}, f32[2,24,128]{2,1,0:T(8,128)S(1)}, u32[]{:S(2)}, u32[]{:S(2)}) %collective-permute-start.11) | collective-permute-done | bytes 24608 | tf_op jit(solution)/shard_map/ppermute | solution.py:462
  173.0 28.3 %sweeps.3 = (f32[1152,128]{1,0:T(8,128)}, f32[1152,128]{1,0:T(8,128)}) custom-call(f32[48,24,128]{2,1,0:T(8,128)} %collect.3.body_ref.rhs_ref, f32[3,24,128]{2,1,0:T(8,128)} %copy-done.8, f32[3,24,128]{2,1,0:T(8,128)} %copy-done.7, f32[2,24,128]{2,1,0:T(8,128)} %copy-done.14, f32[2,24,128]{2,1,0:T(8,128)} %copy-done.15, ...), custom_call_target="tpu_custom_call" | custom-call | tf_op jit(solution)/shard_map/sweeps/pallas_call | solution.py:360
  201.3 2.1 reshape.61
  203.4 7.7 %all-to-all-start.2 = ((f32[32,36,128]{2,1,0:T(8,128)}), f32[32,36,128]{2,1,0:T(8,128)S(1)}, u32[]{:S(2)}, u32[]{:S(2)}) async-start(f32[32,36,128]{2,1,0:T(8,128)} %reshape.61), calls=%async_computation.2 | async-start | bytes 1310720 | tf_op jit(solution)/shard_map/all_to_all | solution.py:417
  211.1 1.1 pad_maximum_fusion.2
  212.2 0.9 reshape.64.in_ref
  213.1 8.8 %prolong.2.whole_ref = f32[3,16,49152]{2,1,0:T(8,128)} custom-call(f32[1152,128]{1,0:T(8,128)} %reshape.64.in_ref, f32[3,3,49152]{2,1,0:T(4,128)} %rest_ref.7, s32[1,49152]{1,0:T(1,128)} %bitcast.51), custom_call_target="tpu_custom_call" | custom-call | tf_op jit(solution)/shard_map/prolong/pallas_call | solution.py:161
  221.9 8.1 %all-to-all-done.2 = f32[32,36,128]{2,1,0:T(8,128)S(1)} async-done(((f32[32,36,128]{2,1,0:T(8,128)}), f32[32,36,128]{2,1,0:T(8,128)S(1)}, u32[]{:S(2)}, u32[]{:S(2)}) %all-to-all-start.2) | async-done | bytes 589856 | tf_op jit(solution)/shard_map/all_to_all | solution.py:417
  230.0 0.9 reshape.62.in_ref
  230.8 8.8 %prolong.3 = f32[3,16,49152]{2,1,0:T(8,128)} custom-call(f32[1152,128]{1,0:T(8,128)} %reshape.62.in_ref, f32[3,3,49152]{2,1,0:T(4,128)} %rest_ref.7, s32[1,49152]{1,0:T(1,128)} %bitcast.52, f32[3,16,49152]{2,1,0:T(8,128)} %prolong.2.whole_ref), custom_call_target="tpu_custom_call", output_to_operand_aliasing={{}: (3, {})} | custom-call | tf_op jit(solution)/shard_map/prolong/pallas_call | solution.py:161
  (55 shorter events, 5.5 us)
Async XLA Ops:
  9.7 9.3 %copy-start.9 = (s32[4,48,128]{2,1,0:T(8,128)S(1)}, s32[4,48,128]{2,1,0:T(8,128)}, u32[]{:S(2)}) copy-start(s32[4,48,128]{2,1,0:T(8,128)} %param.13) | copy-start | bytes 294916
  9.7 9.4 %copy-start.4 = (f32[3,3,48,128]{3,2,1,0:T(8,128)S(1)}, f32[3,3,48,128]{3,2,1,0:T(8,128)}, u32[]{:S(2)}) copy-start(f32[3,3,48,128]{3,2,1,0:T(8,128)} %param.11) | copy-start | bytes 663556
  11.7 7.5 %copy-start.1 = (f32[4,3,3,48,128]{4,3,2,1,0:T(8,128)S(1)}, f32[4,3,3,48,128]{4,3,2,1,0:T(8,128)}, u32[]{:S(2)}) copy-start(f32[4,3,3,48,128]{4,3,2,1,0:T(8,128)} %param.12) | copy-start | bytes 2654212
  11.7 35.2 %all-to-all-start = ((f32[32,36,128]{2,1,0:T(8,128)}), f32[32,36,128]{2,1,0:T(8,128)S(1)}, u32[]{:S(2)}, u32[]{:S(2)}) async-start(f32[32,36,128]{2,1,0:T(8,128)} %reshape.51), calls=%async_computation | async-start | bytes 1310720 | tf_op jit(solution)/shard_map/all_to_all | solution.py:417
  19.5 3.6 %copy-start.11 = (s32[48,128]{1,0:T(8,128)S(1)}, s32[48,128]{1,0:T(8,128)}, u32[]{:S(2)}) copy-start(s32[48,128]{1,0:T(8,128)} %param.10) | copy-start | bytes 73732
  19.6 35.2 %collective-permute-start.4 = (f32[3,45,128]{2,1,0:T(8,128)S(1)}, f32[3,45,128]{2,1,0:T(8,128)S(1)}, u32[]{:S(2)}, u32[]{:S(2)}) collective-permute-start(f32[3,45,128]{2,1,0:T(8,128)S(1)} %get-tuple-element.22), channel_id=1, source_target_pairs={{0,4},{4,8},{8,12},{12,16},{16,20},{20,24},{24,28},{1,5},{5,9},{9,... | collective-permute-start | bytes 207368 | tf_op jit(solution)/shard_map/ppermute | solution.py:405
  21.8 33.0 %collective-permute-start.5 = (f32[3,45,128]{2,1,0:T(8,128)S(1)}, f32[3,45,128]{2,1,0:T(8,128)S(1)}, u32[]{:S(2)}, u32[]{:S(2)}) collective-permute-start(f32[3,45,128]{2,1,0:T(8,128)S(1)} %get-tuple-element.23), channel_id=1, source_target_pairs={{4,0},{8,4},{12,8},{16,12},{20,16},{24,20},{28,24},{5,1},{9,5},{13... | collective-permute-start | bytes 207368 | tf_op jit(solution)/shard_map/ppermute | solution.py:406
  46.9 8.0 %copy-start = (f32[32,36,128]{2,1,0:T(8,128)}, f32[32,36,128]{2,1,0:T(8,128)S(1)}, u32[]{:S(2)}) copy-start(f32[32,36,128]{2,1,0:T(8,128)S(1)} %all-to-all-done) | copy-start | bytes 1769476
  46.9 87.6 %all-to-all-start.1 = ((f32[32,36,128]{2,1,0:T(8,128)}), f32[32,36,128]{2,1,0:T(8,128)S(1)}, u32[]{:S(2)}, u32[]{:S(2)}) async-start(f32[32,36,128]{2,1,0:T(8,128)} %reshape.58), calls=%async_computation.1 | async-start | bytes 1310720 | tf_op jit(solution)/shard_map/all_to_all | solution.py:417
  59.6 25.6 %copy-start.10 = (s32[6144]{0:T(1024)S(1)}, s32[6144]{0:T(1024)}, u32[]{:S(2)}) copy-start(s32[6144]{0:T(1024)} %invert_permutation.1) | copy-start | bytes 73732
  59.6 27.9 %collective-permute-start.7 = (f32[3,45,54]{2,1,0:T(8,128)S(1)}, f32[3,45,54]{2,1,0:T(8,128)S(1)}, u32[]{:S(2)}, u32[]{:S(2)}) collective-permute-start(f32[3,45,54]{2,1,0:T(8,128)S(1)} %copy.18), channel_id=1, source_target_pairs={{0,1},{1,2},{2,3},{4,5},{5,6},{6,7},{8,9},{9,10},{10,11},{12,13},{... | collective-permute-start | bytes 87488 | tf_op jit(solution)/shard_map/ppermute | solution.py:409
  63.4 22.5 %collective-permute-start.6 = (f32[3,45,54]{2,1,0:T(8,128)}, f32[3,45,54]{2,1,0:T(8,128)}, u32[]{:S(2)}, u32[]{:S(2)}) collective-permute-start(f32[3,45,54]{2,1,0:T(8,128)} %copy.16), channel_id=1, source_target_pairs={{1,0},{2,1},{3,2},{5,4},{6,5},{7,6},{9,8},{10,9},{11,10},{13,12},{... | collective-permute-start | bytes 87488 | tf_op jit(solution)/shard_map/ppermute | solution.py:410
  80.9 8.4 %collective-permute-start.1 = (f32[3,24,128]{2,1,0:T(8,128)}, f32[3,24,128]{2,1,0:T(8,128)S(1)}, u32[]{:S(2)}, u32[]{:S(2)}) collective-permute-start(f32[3,24,128]{2,1,0:T(8,128)} %get-tuple-element.24), channel_id=1, source_target_pairs={{4,0},{8,4},{12,8},{16,12},{20,16},{24,20},{28,24},{5,1},{9,5},{13... | collective-permute-start | bytes 110600 | tf_op jit(solution)/shard_map/ppermute | solution.py:459
  82.2 7.1 %collective-permute-start = (f32[3,24,128]{2,1,0:T(8,128)}, f32[3,24,128]{2,1,0:T(8,128)S(1)}, u32[]{:S(2)}, u32[]{:S(2)}) collective-permute-start(f32[3,24,128]{2,1,0:T(8,128)} %get-tuple-element.25), channel_id=1, source_target_pairs={{0,4},{4,8},{8,12},{12,16},{16,20},{20,24},{24,28},{1,5},{5,9},{9,... | collective-permute-start | bytes 110600 | tf_op jit(solution)/shard_map/ppermute | solution.py:458
  89.3 0.6 copy-start.5
  89.9 0.6 copy-start.6
  92.6 9.2 %collective-permute-start.2 = (f32[2,24,128]{2,1,0:T(8,128)}, f32[2,24,128]{2,1,0:T(8,128)S(1)}, u32[]{:S(2)}, u32[]{:S(2)}) collective-permute-start(f32[2,24,128]{2,1,0:T(8,128)} %get-tuple-element.10), channel_id=1, source_target_pairs={{0,1},{1,2},{2,3},{4,5},{5,6},{6,7},{8,9},{9,10},{10,11},{12,13},{... | collective-permute-start | bytes 73736 | tf_op jit(solution)/shard_map/ppermute | solution.py:461
  97.1 6.4 %collective-permute-start.3 = (f32[2,24,128]{2,1,0:T(8,128)}, f32[2,24,128]{2,1,0:T(8,128)S(1)}, u32[]{:S(2)}, u32[]{:S(2)}) collective-permute-start(f32[2,24,128]{2,1,0:T(8,128)} %get-tuple-element.11), channel_id=1, source_target_pairs={{1,0},{2,1},{3,2},{5,4},{6,5},{7,6},{9,8},{10,9},{11,10},{13,12},{... | collective-permute-start | bytes 73736 | tf_op jit(solution)/shard_map/ppermute | solution.py:462
  101.8 1.8 copy-start.12
  103.6 0.6 copy-start.13
  134.4 68.9 %all-to-all-start.3 = ((f32[32,36,128]{2,1,0:T(8,128)}), f32[32,36,128]{2,1,0:T(8,128)S(1)}, u32[]{:S(2)}, u32[]{:S(2)}) async-start(f32[32,36,128]{2,1,0:T(8,128)} %reshape.63), calls=%async_computation.3 | async-start | bytes 1310720 | tf_op jit(solution)/shard_map/all_to_all | solution.py:417
  154.9 4.3 %collective-permute-start.9 = (f32[3,24,128]{2,1,0:T(8,128)S(1)}, f32[3,24,128]{2,1,0:T(8,128)S(1)}, u32[]{:S(2)}, u32[]{:S(2)}) collective-permute-start(f32[3,24,128]{2,1,0:T(8,128)S(1)} %get-tuple-element.26), channel_id=1, source_target_pairs={{4,0},{8,4},{12,8},{16,12},{20,16},{24,20},{28,24},{5,1},{9,5},{13... | collective-permute-start | bytes 110600 | tf_op jit(solution)/shard_map/ppermute | solution.py:459
  156.1 3.9 %collective-permute-start.8 = (f32[3,24,128]{2,1,0:T(8,128)S(1)}, f32[3,24,128]{2,1,0:T(8,128)S(1)}, u32[]{:S(2)}, u32[]{:S(2)}) collective-permute-start(f32[3,24,128]{2,1,0:T(8,128)S(1)} %get-tuple-element.27), channel_id=1, source_target_pairs={{0,4},{4,8},{8,12},{12,16},{16,20},{20,24},{24,28},{1,5},{5,9},{9,... | collective-permute-start | bytes 110600 | tf_op jit(solution)/shard_map/ppermute | solution.py:458
  159.2 0.8 copy-start.7
  160.0 0.6 copy-start.8
  162.8 5.4 %collective-permute-start.10 = (f32[2,24,128]{2,1,0:T(8,128)}, f32[2,24,128]{2,1,0:T(8,128)S(1)}, u32[]{:S(2)}, u32[]{:S(2)}) collective-permute-start(f32[2,24,128]{2,1,0:T(8,128)} %get-tuple-element.13), channel_id=1, source_target_pairs={{0,1},{1,2},{2,3},{4,5},{5,6},{6,7},{8,9},{9,10},{10,11},{12,13},{... | collective-permute-start | bytes 73736 | tf_op jit(solution)/shard_map/ppermute | solution.py:461
  166.4 5.9 %collective-permute-start.11 = (f32[2,24,128]{2,1,0:T(8,128)}, f32[2,24,128]{2,1,0:T(8,128)S(1)}, u32[]{:S(2)}, u32[]{:S(2)}) collective-permute-start(f32[2,24,128]{2,1,0:T(8,128)} %get-tuple-element.14), channel_id=1, source_target_pairs={{1,0},{2,1},{3,2},{5,4},{6,5},{7,6},{9,8},{10,9},{11,10},{13,12},{... | collective-permute-start | bytes 73736 | tf_op jit(solution)/shard_map/ppermute | solution.py:462
  168.1 4.2 %copy-start.14 = (f32[2,24,128]{2,1,0:T(8,128)}, f32[2,24,128]{2,1,0:T(8,128)S(1)}, u32[]{:S(2)}) copy-start(f32[2,24,128]{2,1,0:T(8,128)S(1)} %collective-permute-done.10.left_ref) | copy-start | bytes 73732
  172.4 0.6 copy-start.15
  201.3 9.8 %copy-start.2 = (f32[1152,128]{1,0:T(8,128)S(1)}, f32[1152,128]{1,0:T(8,128)}, u32[]{:S(2)}) copy-start(f32[1152,128]{1,0:T(8,128)} %get-tuple-element.12) | copy-start | bytes 1769476
  201.3 9.8 %copy-start.3 = (f32[1152,128]{1,0:T(8,128)S(1)}, f32[1152,128]{1,0:T(8,128)}, u32[]{:S(2)}) copy-start(f32[1152,128]{1,0:T(8,128)} %get-tuple-element.15) | copy-start | bytes 1769476
  203.4 26.6 %all-to-all-start.2 = ((f32[32,36,128]{2,1,0:T(8,128)}), f32[32,36,128]{2,1,0:T(8,128)S(1)}, u32[]{:S(2)}, u32[]{:S(2)}) async-start(f32[32,36,128]{2,1,0:T(8,128)} %reshape.61), calls=%async_computation.2 | async-start | bytes 1310720 | tf_op jit(solution)/shard_map/all_to_all | solution.py:417
where the time goes:
time: 242 us; the launch traced here: 240 us
  Pallas kernels  134 us (55%)
  starting transfers between devices  56.9 us (24%)
  local copies, waits for them, and re-layouts  26.2 us (11%)
  waiting for transfers between devices  15.4 us (6%)
  other arithmetic  6.02 us (2%)
    pallas_call x2, Pallas kernels, sweeps(): pl.pallas_call(functools.partial(sweeps_kernel, s), in_specs=[vmem_spec()...  56.6 us
    all_to_all x4, starting transfers between devices, exchange(): lax.all_to_all(blocks, AXES, split_axis=0, concat_axis=0, tiled=True)  28.9 us
    pallas_call x2, Pallas kernels, collect(): pl.pallas_call(functools.partial(collect_kernel, s), in_specs=[vmem_spec(...  25.7 us
    pallas_call x2, Pallas kernels, restrict(): pl.pallas_call(functools.partial(restrict_kernel, s), grid=(FPA,), in_spe...  18.1 us
    pallas_call x2, Pallas kernels, prolong(): pl.pallas_call(body, grid=(FPA,), in_specs=specs, out_specs=pl.BlockSpec(...  17.5 us
    pallas_call x1, Pallas kernels, invert_permutation(): pl.pallas_call(functools.partial(invert_kernel, count), in_specs=[pl.Bloc...  12.1 us
    ppermute x2, starting transfers between devices, body(): ahead = lax.ppermute(right, 'col', col_up)  8.2 us
    all_to_all x4, waiting for transfers between devices, exchange(): lax.all_to_all(blocks, AXES, split_axis=0, concat_axis=0, tiled=True)  8.13 us
  transfers between devices with their start and end apart: 16, of which 5 were waited for; matrix products, arithmetic and copies ran while one was open for 11% of the time, Pallas kernels for 49%

commit v1 on v0

--- a/solution.py
+++ b/solution.py
@@ -10,7 +10,8 @@
 FPA = 8
 ITERS = 4
 LANES = 128
-CHUNKS = 2
+CHUNKS = 1
+UNROLL = 4
 AXES = ("row", "col")
 
 
@@ -65,6 +66,15 @@
     for_tiles(s, visit)
 
 
+def each_column(s, visit):
+    def some(block, carry):
+        for step in range(UNROLL):
+            visit(pl.ds(pl.multiple_of((block * UNROLL + step) * LANES, LANES), LANES))
+        return carry
+
+    lax.fori_loop(0, s.blocks // UNROLL, some, 0)
+
+
 def restrict_kernel(s, x_ref, rest_ref, pat_ref, out_ref, acc):
     step = pl.program_id(0)
 
@@ -72,8 +82,7 @@
     def _():
         acc[...] = jnp.zeros_like(acc)
 
-    def column(block, carry):
-        at = pl.ds(pl.multiple_of(block * LANES, LANES), LANES)
+    def column(at):
         mask = pat_ref[0:1, at].astype(jnp.float32)
         value = [x_ref[comp, :, at] for comp in range(3)]
         for comp in range(3):
@@ -81,9 +90,8 @@
             for source in range(3):
                 total = total + (rest_ref[comp, source : source + 1, at] * mask) * value[source]
             acc[comp, :, at] = total
-        return carry
-
-    lax.fori_loop(0, s.blocks, column, 0)
+
+    each_column(s, column)
 
     @pl.when(step == FPA - 1)
     def _():
@@ -125,8 +133,7 @@
 
         load_tiles(s, in_ref, take)
 
-    def column(block, carry):
-        at = pl.ds(pl.multiple_of(block * LANES, LANES), LANES)
+    def column(at):
         mask = pat_ref[0:1, at].astype(jnp.float32)
         value = [agg[comp, :, at] for comp in range(3)]
         for comp in range(3):
@@ -134,9 +141,8 @@
             for source in range(1, 3):
                 total = total + (rest_ref[source, comp : comp + 1, at] * mask) * value[source]
             out_ref[comp, :, at] = total
-        return carry
-
-    lax.fori_loop(0, s.blocks, column, 0)
+
+    each_column(s, column)
 
 
 def prolong(s, arrived, restriction, pattern, chunk, whole):
@@ -170,48 +176,55 @@
     )(*args)
 
 
-def gather_rows(s, table_ref, row_ref, lane_ref, out_ref, count):
-    def one(k, carry):
-        rows = jnp.broadcast_to(row_ref[pl.ds(k, 1), :], (8, LANES))
-        lanes = jnp.broadcast_to(lane_ref[pl.ds(k, 1), :], (8, LANES))
-        parts = s.comps // 8
-        total = [jnp.zeros((8, LANES), jnp.float32) for _ in range(parts)]
-        for source in range(count):
-            hit = rows == source
-            for part in range(parts):
-                moved = jnp.take_along_axis(
-                    table_ref[source, part * 8 : part * 8 + 8, :],
-                    lanes,
-                    axis=1,
-                    mode="promise_in_bounds",
-                )
-                total[part] = jnp.where(hit, moved, total[part])
-        for part in range(parts):
-            out_ref[k, part * 8 : part * 8 + 8, :] = total[part]
-        return carry
-
-    lax.fori_loop(0, count, one, 0)
-
-
-def collect_kernel(s, in_ref, row_ref, lane_ref, out_ref, table):
+def collect_kernel(s, slot_ref, in_ref, out_ref, table, lines, even, odd):
     def take(comp, grp, turned):
         for member in range(s.group):
             block = grp * s.group + member
             table[block, comp * s.q : (comp + 1) * s.q, :] = turned[member * s.q : (member + 1) * s.q]
 
     load_tiles(s, in_ref, take)
-    gather_rows(s, table, row_ref, lane_ref, out_ref, s.rows)
-
-
-def collect(s, received, row, lane):
+    for block in range(s.blocks):
+        lines[block * LANES : (block + 1) * LANES, 0 : s.comps] = table[block].T
+
+    def fetch(row, held):
+        for lane in range(LANES):
+            slot = slot_ref[row * LANES + lane]
+            held[lane : lane + 1, :] = lines[pl.ds(slot, 1), :]
+
+    def place(row, held):
+        out_ref[row] = held[...].T[0 : s.comps]
+
+    fetch(0, even)
+
+    def two(k, carry):
+        row = 2 * k
+        fetch(row + 1, odd)
+        place(row, even)
+        fetch(jnp.minimum(row + 2, s.rows - 1), even)
+        place(row + 1, odd)
+        return carry
+
+    lax.fori_loop(0, s.rows // 2, two, 0)
+
+
+def line_scratch(s):
+    return [
+        pltpu.VMEM((s.blocks, s.comps, LANES), jnp.float32),
+        pltpu.VMEM((s.agg, LANES), jnp.float32),
+        pltpu.VMEM((LANES, LANES), jnp.float32),
+        pltpu.VMEM((LANES, LANES), jnp.float32),
+    ]
+
+
+def collect(s, received, slots):
     return pl.pallas_call(
         functools.partial(collect_kernel, s),
-        in_specs=[vmem_spec()] * 3,
+        in_specs=[pl.BlockSpec(memory_space=pltpu.SMEM), vmem_spec()],
         out_specs=vmem_spec(),
         out_shape=jax.ShapeDtypeStruct((s.rows, s.comps, LANES), jnp.float32),
-        scratch_shapes=[pltpu.VMEM((s.blocks, s.comps, LANES), jnp.float32)],
+        scratch_shapes=line_scratch(s),
         name="collect",
-    )(received, row, lane)
+    )(slots, received)
 
 
 PACK = 32
@@ -255,8 +268,8 @@
 
 
 def sweeps_kernel(
-    s, rhs_ref, before_ref, after_ref, left_ref, right_ref, coef_ref, row_ref, lane_ref,
-    sol_ref, out_ref, wide, even, odd, final, back,
+    s, slot_ref, rhs_ref, before_ref, after_ref, left_ref, right_ref, coef_ref,
+    sol_ref, out_ref, wide, even, odd, final, table, lines, ahead_lines, behind_lines,
 ):
     lane = lax.broadcasted_iota(jnp.int32, (s.comps, LANES), 1)
     for at in range(s.wide):
@@ -293,19 +306,23 @@
             fresh.append(value)
         return fresh
 
+    def span(comp, low):
+        return slice(comp * q + low, comp * q + low + 8)
+
     def first(at, carry):
-        total = [wide[at, comp * q : (comp + 1) * q, :] for comp in range(3)]
-        fresh = invert(at, total, 2 * LANES)
-        for comp in range(3):
-            even[at, comp * q : (comp + 1) * q, :] = fresh[comp]
+        for low in range(0, q, 8):
+            total = [wide[at, span(comp, low), :] for comp in range(3)]
+            fresh = invert(at, total, 2 * LANES)
+            for comp in range(3):
+                even[at, span(comp, low), :] = fresh[comp]
         return carry
 
     lax.fori_loop(0, s.wide, first, 0)
 
-    def sweep(old, at, width):
+    def sweep(old, at, low, width):
         pieces = [[] for _ in range(4)]
         for source in range(3):
-            part = slice(source * q, (source + 1) * q)
+            part = span(source, low)
             pieces[0].append(old[at - 1, part, 0:width])
             pieces[1].append(old[at + 1, part, 0:width])
             here = old[at, part, :]
@@ -313,7 +330,7 @@
             pieces[3].append(pltpu.roll(here, 2 * LANES - 1, 1)[:, 0:width])
         total = []
         for comp in range(3):
-            value = wide[at, comp * q : (comp + 1) * q, 0:width]
+            value = wide[at, span(comp, low), 0:width]
             for direction in range(4):
                 for source in range(3):
                     index = 9 + (direction * 3 + comp) * 3 + source
@@ -324,71 +341,71 @@
     old, new = even, odd
     for inner in range(1, s.depth):
         def middle(at, carry, old=old, new=new):
-            fresh = sweep(old, at, 2 * LANES)
-            for comp in range(3):
-                new[at, comp * q : (comp + 1) * q, :] = fresh[comp]
+            for low in range(0, q, 8):
+                fresh = sweep(old, at, low, 2 * LANES)
+                for comp in range(3):
+                    new[at, span(comp, low), :] = fresh[comp]
             return carry
 
         lax.fori_loop(inner, s.wide - inner, middle, 0)
         old, new = new, old
 
     def last(k, carry):
-        fresh = sweep(old, k + s.depth, LANES)
-        for comp in range(3):
-            final[k, comp * q : (comp + 1) * q, :] = fresh[comp]
-            for low in range(0, q, 8):
+        for low in range(0, q, 8):
+            fresh = sweep(old, k + s.depth, low, LANES)
+            for comp in range(3):
+                final[k, span(comp, low), :] = fresh[comp]
                 start = (low * 3 + comp) * s.rows + k
-                sol_ref[pl.ds(start, 8, stride=3 * s.rows), :] = fresh[comp][low : low + 8]
+                sol_ref[pl.ds(start, 8, stride=3 * s.rows), :] = fresh[comp]
         return carry
 
     lax.fori_loop(0, s.rows, last, 0)
 
-    gather_rows(s, final, row_ref, lane_ref, back, s.blocks)
+    def turn_line(row, held):
+        held[:, 0 : s.comps] = final[row].T
+
+    def send(row, held):
+        for lane in range(LANES):
+            slot = slot_ref[row * LANES + lane]
+            lines[pl.ds(slot, 1), :] = held[lane : lane + 1, :]
+
+    turn_line(0, ahead_lines)
+
+    def two(k, carry):
+        row = 2 * k
+        turn_line(row + 1, behind_lines)
+        send(row, ahead_lines)
+        turn_line(jnp.minimum(row + 2, s.rows - 1), ahead_lines)
+        send(row + 1, behind_lines)
+        return carry
+
+    lax.fori_loop(0, s.rows // 2, two, 0)
+    for block in range(s.blocks):
+        table[block] = lines[block * LANES : (block + 1) * LANES, :].T[0 : s.comps]
 
     def tile_of(comp, grp):
         parts = []
         for member in range(s.group):
-            parts.append(back[grp * s.group + member, comp * q : (comp + 1) * q, :])
+            parts.append(table[grp * s.group + member, comp * q : (comp + 1) * q, :])
         return jnp.concatenate(parts, axis=0)
 
     store_tiles(s, out_ref, tile_of)
 
 
-def sweeps(s, rhs, before, after, left, right, coefs, row, lane):
+def sweeps(s, slots, rhs, before, after, left, right, coefs):
     state = pltpu.VMEM((s.wide, s.comps, 2 * LANES), jnp.float32)
     tile = pltpu.VMEM((s.rows, s.comps, LANES), jnp.float32)
     return pl.pallas_call(
         functools.partial(sweeps_kernel, s),
-        in_specs=[vmem_spec()] * 8,
+        in_specs=[pl.BlockSpec(memory_space=pltpu.SMEM)] + [vmem_spec()] * 6,
         out_specs=[vmem_spec()] * 2,
         out_shape=[
             jax.ShapeDtypeStruct((s.q * 3 * s.rows, LANES), jnp.float32),
             jax.ShapeDtypeStruct((s.devices * s.per_peer, LANES), jnp.float32),
         ],
-        scratch_shapes=[state, state, state, tile, tile],
+        scratch_shapes=[state, state, state, tile] + line_scratch(s),
         name="sweeps",
-    )(rhs, before, after, left, right, coefs, row, lane)
-
-
-def invert_kernel(count, slot_ref, out_ref):
-    def some(at, carry):
-        for step in range(8):
-            k = at * 8 + step
-            out_ref[slot_ref[k]] = k
-        return carry
-
-    lax.fori_loop(0, count // 8, some, 0)
-
-
-def invert_permutation(slots):
-    count = slots.shape[0]
-    return pl.pallas_call(
-        functools.partial(invert_kernel, count),
-        in_specs=[pl.BlockSpec(memory_space=pltpu.SMEM)],
-        out_specs=pl.BlockSpec(memory_space=pltpu.SMEM),
-        out_shape=jax.ShapeDtypeStruct((count,), jnp.int32),
-        name="invert_permutation",
-    )(slots)
+    )(slots, rhs, before, after, left, right, coefs)
 
 
 def ring(axis):
@@ -446,7 +463,7 @@
     local = cell_aggregate % s.agg
     row = local // LANES
     lane = local % LANES // s.devices * s.devices + owner
-    back = invert_permutation((row * LANES + lane).reshape(-1)).reshape(s.blocks, LANES)
+    slots = (row * LANES + lane).reshape(-1)
     coefs = wide_coefficients(s, block_inverse, off_blocks, operator_pattern)
 
     row_up, row_down = ring("row")
@@ -454,19 +471,19 @@
     solutions = []
     arrived = []
     for chunk in range(CHUNKS):
-        rhs = collect(s, received[chunk], row, lane)
+        rhs = collect(s, received[chunk], slots)
         before = lax.ppermute(rhs[-s.depth :], "row", row_up)
         after = lax.ppermute(rhs[: s.depth], "row", row_down)
         left, right = pack_edges(s, rhs, before, after)
         ahead = lax.ppermute(right, "col", col_up)
         past = lax.ppermute(left, "col", col_down)
-        sol, outgoing = sweeps(s, rhs, before, after, ahead, past, coefs, back // LANES, back % LANES)
+        sol, outgoing = sweeps(s, slots, rhs, before, after, ahead, past, coefs)
         solutions.append(sol.reshape(s.q, 3, s.rows, LANES))
         arrived.append(exchange(s, outgoing))
     correction = None
     for chunk in range(CHUNKS):
         correction = prolong(s, arrived[chunk], restriction, pattern, chunk, correction)
-    return jnp.concatenate(solutions), correction.transpose(1, 0, 2)
+    return solutions[0] if CHUNKS == 1 else jnp.concatenate(solutions), correction.transpose(1, 0, 2)
 
 
 def solution(mesh):

time: 242 us -> 168 us (0.69)
  Pallas kernels: 134 us -> 61.2 us
  blocking collectives: 0 us -> 35.3 us
  starting transfers between devices: 56.9 us -> 26.7 us
  local copies, waits for them, and re-layouts: 26.2 us -> 10.2 us
  waiting for transfers between devices: 15.4 us -> 28.3 us
    pallas_call x5 -> x2, Pallas kernels: 94.4 us -> 39.4 us  [the longest x1 29 us: sweeps(): pl.pallas_call(functools.partial(sweeps_kernel, s), in_specs=[pl.BlockSpe...]
    all_to_all x0 -> x1, blocking collectives: none -> 35.3 us  [exchange(): lax.all_to_all(blocks, AXES, split_axis=0, concat_axis=0, tiled=True)]
    all_to_all x4 -> x1, starting transfers between devices: 28.9 us -> 7.45 us  [exchange(): lax.all_to_all(blocks, AXES, split_axis=0, concat_axis=0, tiled=True)]
    all_to_all x4 -> x1, waiting for transfers between devices: 8.13 us -> 21.9 us  [exchange(): lax.all_to_all(blocks, AXES, split_axis=0, concat_axis=0, tiled=True)]
    reshape x8 -> x0, local copies, waits for them, and re-layouts: 12.5 us -> none  [the longest x4 7.94 us: exchange(): blocks = outgoing.reshape(s.devices, s.per_peer, LANES)]
    pallas_call x2 -> x1, Pallas kernels: 17.5 us -> 9.2 us  [prolong(): pl.pallas_call(body, grid=(FPA,), in_specs=specs, out_specs=pl.BlockSpec(...]
    pallas_call x2 -> x1, Pallas kernels: 18.1 us -> 9.9 us  [restrict(): pl.pallas_call(functools.partial(restrict_kernel, s), grid=(FPA,), in_spe...]
    ppermute x2 -> x1, starting transfers between devices: 8.2 us -> 4.38 us  [body(): ahead = lax.ppermute(right, 'col', col_up)]
  transfers between devices with their start and end apart: 16 -> 9, of which waited for: 5 -> 4; matrix products, arithmetic and copies ran while one was open for 11% -> 7% of each run, Pallas kernels for 49% -> 0%
where the time goes in v1:
time: 168 us; the launch traced here: 167 us
  Pallas kernels  61.2 us (36%)
  blocking collectives  35.3 us (21%)
  waiting for transfers between devices  28.3 us (17%)
  starting transfers between devices  26.7 us (16%)
  local copies, waits for them, and re-layouts  10.2 us (6%)
  other arithmetic  4.27 us (3%)
    all_to_all x1, blocking collectives, exchange(): lax.all_to_all(blocks, AXES, split_axis=0, concat_axis=0, tiled=True)  35.3 us
    pallas_call x1, Pallas kernels, sweeps(): pl.pallas_call(functools.partial(sweeps_kernel, s), in_specs=[pl.BlockSpe...  29 us
    all_to_all x1, waiting for transfers between devices, exchange(): lax.all_to_all(blocks, AXES, split_axis=0, concat_axis=0, tiled=True)  21.9 us
    pallas_call x1, Pallas kernels, collect(): pl.pallas_call(functools.partial(collect_kernel, s), in_specs=[pl.BlockSp...  10.4 us
    pallas_call x1, Pallas kernels, restrict(): pl.pallas_call(functools.partial(restrict_kernel, s), grid=(FPA,), in_spe...  9.9 us
    pallas_call x1, Pallas kernels, prolong(): pl.pallas_call(body, grid=(FPA,), in_specs=specs, out_specs=pl.BlockSpec(...  9.2 us
    all_to_all x1, starting transfers between devices, exchange(): lax.all_to_all(blocks, AXES, split_axis=0, concat_axis=0, tiled=True)  7.45 us
    ppermute x1, starting transfers between devices, wide_coefficients(): lax.ppermute(coefs[..., -s.depth:].transpose(2, 1, 0), 'col', up)  4.54 us
  transfers between devices with their start and end apart: 9, of which 4 were waited for; matrix products, arithmetic and copies ran while one was open for 7% of the time, Pallas kernels for 0%

profile of v1, /device:TPU:0, one launch (start us, length us, event | category | flops | bytes accessed | tf_op | source)
XLA Modules:
  0.0 166.7 jit_solution(11876084585152096721)
XLA Ops:
  0.6 9.9 %restrict.1 = f32[2304,128]{1,0:T(8,128)} custom-call(f32[3,16,49152]{2,1,0:T(8,128)} %bitcast.20, f32[3,3,49152]{2,1,0:T(4,128)} %rest_ref.3, s32[1,49152]{1,0:T(1,128)} %bitcast.28), custom_call_target="tpu_custom_call" | custom-call | tf_op jit(solution)/shard_map/restrict/pallas_call | solution.py:109
  10.5 7.4 %all-to-all-start = ((f32[32,72,128]{2,1,0:T(8,128)}), f32[32,72,128]{2,1,0:T(8,128)}, u32[]{:S(2)}, u32[]{:S(2)}) async-start(f32[32,72,128]{2,1,0:T(8,128)} %bitcast.24), calls=%async_computation | async-start | bytes 2359296 | tf_op jit(solution)/shard_map/all_to_all | solution.py:434
  18.0 0.0 copy-done.5
  18.0 0.0 copy-done.4
  18.0 0.1 copy.13
  18.1 0.0 copy-done.1
  18.1 0.1 broadcast_multiply_fusion
  18.2 0.3 copy.14
  18.5 0.0 copy-start.8
  18.5 0.1 maximum_bitcast_fusion
  18.6 2.1 %collective-permute-start.4 = (f32[3,45,128]{2,1,0:T(8,128)S(1)}, f32[3,45,128]{2,1,0:T(8,128)S(1)}, u32[]{:S(2)}, u32[]{:S(2)}) collective-permute-start(f32[3,45,128]{2,1,0:T(8,128)S(1)} %get-tuple-element.12), channel_id=1, source_target_pairs={{0,4},{4,8},{8,12},{12,16},{16,20},{20,24},{24,28},{1,5},{5,9},{9,... | collective-permute-start | bytes 207368 | tf_op jit(solution)/shard_map/ppermute | solution.py:422
  20.7 1.3 collective-permute-start.5
  22.0 0.0 copy-done.8
  22.1 0.7 fusion.2.slot_ref
  22.7 0.0 collective-permute-done.4
  22.7 2.3 %collective-permute-done.5 = f32[3,45,128]{2,1,0:T(8,128)S(1)} collective-permute-done((f32[3,45,128]{2,1,0:T(8,128)S(1)}, f32[3,45,128]{2,1,0:T(8,128)S(1)}, u32[]{:S(2)}, u32[]{:S(2)}) %collective-permute-start.5) | collective-permute-done | bytes 69152 | tf_op jit(solution)/shard_map/ppermute | solution.py:423
  25.0 0.1 pad_maximum_fusion.1
  25.1 21.9 %all-to-all-done = f32[32,72,128]{2,1,0:T(8,128)} async-done(((f32[32,72,128]{2,1,0:T(8,128)}), f32[32,72,128]{2,1,0:T(8,128)}, u32[]{:S(2)}, u32[]{:S(2)}) %all-to-all-start) | async-done | bytes 1179680 | tf_op jit(solution)/shard_map/all_to_all | solution.py:434
  47.1 10.4 %collect.1.body_ref.rhs_ref = f32[48,48,128]{2,1,0:T(8,128)} custom-call(s32[6144]{0:T(1024)} %fusion.2.slot_ref, f32[2304,128]{1,0:T(8,128)} %bitcast.4.in_ref), custom_call_target="tpu_custom_call" | custom-call | tf_op jit(solution)/shard_map/collect/pallas_call | solution.py:220
  57.5 0.9 fusion.11
  58.4 1.3 collective-permute-start.1
  59.7 3.0 %collective-permute-start = (f32[3,48,128]{2,1,0:T(8,128)S(1)}, f32[3,48,128]{2,1,0:T(8,128)S(1)}, u32[]{:S(2)}, u32[]{:S(2)}) collective-permute-start(f32[3,48,128]{2,1,0:T(8,128)S(1)} %get-tuple-element.15), channel_id=1, source_target_pairs={{0,4},{4,8},{8,12},{12,16},{16,20},{20,24},{24,28},{1,5},{5,9},{9,... | collective-permute-start | bytes 221192 | tf_op jit(solution)/shard_map/ppermute | solution.py:475
  62.7 1.9 %slice_bitcast_fusion.1 = (f32[3,45,54]{0,1,2:T(8,128)}, f32[3,45,54]{0,1,2:T(8,128)}) fusion(f32[54,45,128]{2,1,0:T(8,128)S(1)} %pad_maximum_fusion.1), kind=kLoop, calls=%fused_computation.2 | loop fusion | bytes 116640 | tf_op jit(solution)/shard_map/transpose | solution.py:427
  64.7 2.0 %copy.15 = f32[3,45,54]{2,1,0:T(8,128)S(1)} copy(f32[3,45,54]{0,1,2:T(8,128)} %get-tuple-element.10) | data formatting | bytes 58320 | tf_op jit(solution)/shard_map/transpose | solution.py:427
  66.7 1.3 collective-permute-start.6
  68.0 0.0 copy-done
  68.0 0.6 copy.17
  68.6 4.5 %collective-permute-start.7 = (f32[3,45,54]{2,1,0:T(8,128)S(1)}, f32[3,45,54]{2,1,0:T(8,128)S(1)}, u32[]{:S(2)}, u32[]{:S(2)}) collective-permute-start(f32[3,45,54]{2,1,0:T(8,128)S(1)} %copy.17), channel_id=1, source_target_pairs={{0,1},{1,2},{2,3},{4,5},{5,6},{6,7},{8,9},{9,10},{10,11},{12,13},{... | collective-permute-start | bytes 87488 | tf_op jit(solution)/shard_map/ppermute | solution.py:426
  73.2 0.1 pad.4.clone
  73.2 0.0 collective-permute-done.6
  73.2 0.7 copy.16
  73.9 1.5 collective-permute-done.7
  75.5 1.7 %copy.18 = f32[3,45,54]{0,1,2:T(8,128)} copy(f32[3,45,54]{2,1,0:T(8,128)S(1)} %collective-permute-done.7) | data formatting | bytes 58320 | tf_op jit(solution)/shard_map/ppermute | solution.py:426
  77.1 0.0 collective-permute-done.1.after_ref
  77.1 0.0 collective-permute-done.before_ref
  77.1 0.6 copy-done.2
  77.8 0.6 copy-done.3
  78.4 2.7 %pack_edges.1 = (f32[2,48,128]{2,1,0:T(8,128)}, f32[2,48,128]{2,1,0:T(8,128)}) custom-call(f32[48,48,128]{2,1,0:T(8,128)} %collect.1.body_ref.rhs_ref, f32[3,48,128]{2,1,0:T(8,128)} %copy-done.3, f32[3,48,128]{2,1,0:T(8,128)} %copy-done.2), custom_call_target="tpu_custom_call" | custom-call | tf_op jit(solution)/shard_map/pack_edges/pallas_call | solution.py:261
  81.1 4.4 %collective-permute-start.2 = (f32[2,48,128]{2,1,0:T(8,128)}, f32[2,48,128]{2,1,0:T(8,128)S(1)}, u32[]{:S(2)}, u32[]{:S(2)}) collective-permute-start(f32[2,48,128]{2,1,0:T(8,128)} %get-tuple-element.6), channel_id=1, source_target_pairs={{0,1},{1,2},{2,3},{4,5},{5,6},{6,7},{8,9},{9,10},{10,11},{12,13},{... | collective-permute-start | bytes 147464 | tf_op jit(solution)/shard_map/ppermute | solution.py:478
  85.4 1.3 collective-permute-start.3
  86.7 3.3 %pad_maximum_fusion.coef_ref = f32[54,45,256]{2,1,0:T(8,128)} fusion(f32[54,45,3]{2,1,0:T(8,128)} %bitcast.23, f32[54,45,3]{2,1,0:T(8,128)S(1)} %bitcast.22, f32[3,45,128]{2,1,0:T(8,128)S(1)} %collective-permute-done.5, f32[48,45,128]{2,1,0:T(8,128)S(1)} %maximum_bitcast_fusion, f32[3,45,128]{2,1,0:T(8,128)S(1)} %collective-permute-done.4, f32[256]{0:T(256)S(1)} %pad.4.clone), kind=kLoop, calls=%fused_computation | loop fusion | flops 3110400 | bytes 3791824 | tf_op jit(solution)/shard_map/concatenate | solution.py:429
  90.1 0.0 collective-permute-done.2.left_ref
  90.1 2.5 %collective-permute-done.3.right_ref = f32[2,48,128]{2,1,0:T(8,128)S(1)} collective-permute-done((f32[2,48,128]{2,1,0:T(8,128)}, f32[2,48,128]{2,1,0:T(8,128)S(1)}, u32[]{:S(2)}, u32[]{:S(2)}) %collective-permute-start.3) | collective-permute-done | bytes 49184 | tf_op jit(solution)/shard_map/ppermute | solution.py:479
  92.6 0.0 copy-done.6
  92.6 0.6 copy-done.7
  93.2 29.0 %sweeps.1 = (f32[2304,128]{1,0:T(8,128)}, f32[2304,128]{1,0:T(8,128)}) custom-call(s32[6144]{0:T(1024)} %fusion.2.slot_ref, f32[48,48,128]{2,1,0:T(8,128)} %collect.1.body_ref.rhs_ref, f32[3,48,128]{2,1,0:T(8,128)} %copy-done.3, f32[3,48,128]{2,1,0:T(8,128)} %copy-done.2, f32[2,48,128]{2,1,0:T(8,128)} %copy-done.6, f32[2,48,128]{2,1,0:T(8,128)} %copy-done.7, ...), custom_call_target="tpu_custom_call" | custom-call | tf_op jit(solution)/shard_map/sweeps/pallas_call | solution.py:398
  122.2 35.3 %all_to_all.10 = f32[32,72,128]{2,1,0:T(8,128)} all-to-all(f32[32,72,128]{2,1,0:T(8,128)} %bitcast.27), channel_id=1, replica_groups=mesh['row'=8,'col'=4] {'row','col'}, dimensions={0} | all-to-all | bytes 2359296 | tf_op jit(solution)/shard_map/all_to_all | solution.py:434
  157.5 9.2 %prolong.1 = f32[3,16,49152]{2,1,0:T(8,128)} custom-call(f32[2304,128]{1,0:T(8,128)} %bitcast.25, f32[3,3,49152]{2,1,0:T(4,128)} %rest_ref.3, s32[1,49152]{1,0:T(1,128)} %bitcast.29), custom_call_target="tpu_custom_call" | custom-call | tf_op jit(solution)/shard_map/prolong/pallas_call | solution.py:167
  (11 shorter events, 0.0 us)
Async XLA Ops:
  10.5 7.5 %copy-start.5 = (s32[4,48,128]{2,1,0:T(8,128)S(1)}, s32[4,48,128]{2,1,0:T(8,128)}, u32[]{:S(2)}) copy-start(s32[4,48,128]{2,1,0:T(8,128)} %param.13) | copy-start | bytes 294916
  10.5 7.5 %copy-start.4 = (f32[3,3,48,128]{3,2,1,0:T(8,128)S(1)}, f32[3,3,48,128]{3,2,1,0:T(8,128)}, u32[]{:S(2)}) copy-start(f32[3,3,48,128]{3,2,1,0:T(8,128)} %param.11) | copy-start | bytes 663556
  10.5 7.6 %copy-start.1 = (f32[4,3,3,48,128]{4,3,2,1,0:T(8,128)S(1)}, f32[4,3,3,48,128]{4,3,2,1,0:T(8,128)}, u32[]{:S(2)}) copy-start(f32[4,3,3,48,128]{4,3,2,1,0:T(8,128)} %param.12) | copy-start | bytes 2654212
  10.5 36.5 %all-to-all-start = ((f32[32,72,128]{2,1,0:T(8,128)}), f32[32,72,128]{2,1,0:T(8,128)}, u32[]{:S(2)}, u32[]{:S(2)}) async-start(f32[32,72,128]{2,1,0:T(8,128)} %bitcast.24), calls=%async_computation | async-start | bytes 2359296 | tf_op jit(solution)/shard_map/all_to_all | solution.py:434
  18.5 3.5 %copy-start.8 = (s32[48,128]{1,0:T(8,128)S(1)}, s32[48,128]{1,0:T(8,128)}, u32[]{:S(2)}) copy-start(s32[48,128]{1,0:T(8,128)} %param.10) | copy-start | bytes 73732
  18.6 4.1 %collective-permute-start.4 = (f32[3,45,128]{2,1,0:T(8,128)S(1)}, f32[3,45,128]{2,1,0:T(8,128)S(1)}, u32[]{:S(2)}, u32[]{:S(2)}) collective-permute-start(f32[3,45,128]{2,1,0:T(8,128)S(1)} %get-tuple-element.12), channel_id=1, source_target_pairs={{0,4},{4,8},{8,12},{12,16},{16,20},{20,24},{24,28},{1,5},{5,9},{9,... | collective-permute-start | bytes 207368 | tf_op jit(solution)/shard_map/ppermute | solution.py:422
  20.7 4.3 %collective-permute-start.5 = (f32[3,45,128]{2,1,0:T(8,128)S(1)}, f32[3,45,128]{2,1,0:T(8,128)S(1)}, u32[]{:S(2)}, u32[]{:S(2)}) collective-permute-start(f32[3,45,128]{2,1,0:T(8,128)S(1)} %get-tuple-element.13), channel_id=1, source_target_pairs={{4,0},{8,4},{12,8},{16,12},{20,16},{24,20},{28,24},{5,1},{9,5},{13... | collective-permute-start | bytes 207368 | tf_op jit(solution)/shard_map/ppermute | solution.py:423
  58.4 18.7 %collective-permute-start.1 = (f32[3,48,128]{2,1,0:T(8,128)S(1)}, f32[3,48,128]{2,1,0:T(8,128)S(1)}, u32[]{:S(2)}, u32[]{:S(2)}) collective-permute-start(f32[3,48,128]{2,1,0:T(8,128)S(1)} %get-tuple-element.14), channel_id=1, source_target_pairs={{4,0},{8,4},{12,8},{16,12},{20,16},{24,20},{28,24},{5,1},{9,5},{13... | collective-permute-start | bytes 221192 | tf_op jit(solution)/shard_map/ppermute | solution.py:476
  59.7 17.4 %collective-permute-start = (f32[3,48,128]{2,1,0:T(8,128)S(1)}, f32[3,48,128]{2,1,0:T(8,128)S(1)}, u32[]{:S(2)}, u32[]{:S(2)}) collective-permute-start(f32[3,48,128]{2,1,0:T(8,128)S(1)} %get-tuple-element.15), channel_id=1, source_target_pairs={{0,4},{4,8},{8,12},{12,16},{16,20},{20,24},{24,28},{1,5},{5,9},{9,... | collective-permute-start | bytes 221192 | tf_op jit(solution)/shard_map/ppermute | solution.py:475
  64.7 3.3 %copy-start = (f32[3,45,54]{0,1,2:T(8,128)S(1)}, f32[3,45,54]{0,1,2:T(8,128)}, u32[]{:S(2)}) copy-start(f32[3,45,54]{0,1,2:T(8,128)} %get-tuple-element.11) | copy-start | bytes 87484
  66.7 6.6 %collective-permute-start.6 = (f32[3,45,54]{2,1,0:T(8,128)S(1)}, f32[3,45,54]{2,1,0:T(8,128)S(1)}, u32[]{:S(2)}, u32[]{:S(2)}) collective-permute-start(f32[3,45,54]{2,1,0:T(8,128)S(1)} %copy.15), channel_id=1, source_target_pairs={{1,0},{2,1},{3,2},{5,4},{6,5},{7,6},{9,8},{10,9},{11,10},{13,12},{... | collective-permute-start | bytes 87488 | tf_op jit(solution)/shard_map/ppermute | solution.py:427
  68.6 6.9 %collective-permute-start.7 = (f32[3,45,54]{2,1,0:T(8,128)S(1)}, f32[3,45,54]{2,1,0:T(8,128)S(1)}, u32[]{:S(2)}, u32[]{:S(2)}) collective-permute-start(f32[3,45,54]{2,1,0:T(8,128)S(1)} %copy.17), channel_id=1, source_target_pairs={{0,1},{1,2},{2,3},{4,5},{5,6},{6,7},{8,9},{9,10},{10,11},{12,13},{... | collective-permute-start | bytes 87488 | tf_op jit(solution)/shard_map/ppermute | solution.py:426
  77.1 0.6 copy-start.2
  77.8 0.6 copy-start.3
  81.1 9.0 %collective-permute-start.2 = (f32[2,48,128]{2,1,0:T(8,128)}, f32[2,48,128]{2,1,0:T(8,128)S(1)}, u32[]{:S(2)}, u32[]{:S(2)}) collective-permute-start(f32[2,48,128]{2,1,0:T(8,128)} %get-tuple-element.6), channel_id=1, source_target_pairs={{0,1},{1,2},{2,3},{4,5},{5,6},{6,7},{8,9},{9,10},{10,11},{12,13},{... | collective-permute-start | bytes 147464 | tf_op jit(solution)/shard_map/ppermute | solution.py:478
  85.4 7.2 %collective-permute-start.3 = (f32[2,48,128]{2,1,0:T(8,128)}, f32[2,48,128]{2,1,0:T(8,128)S(1)}, u32[]{:S(2)}, u32[]{:S(2)}) collective-permute-start(f32[2,48,128]{2,1,0:T(8,128)} %get-tuple-element.7), channel_id=1, source_target_pairs={{1,0},{2,1},{3,2},{5,4},{6,5},{7,6},{9,8},{10,9},{11,10},{13,12},{... | collective-permute-start | bytes 147464 | tf_op jit(solution)/shard_map/ppermute | solution.py:479
  90.1 2.5 %copy-start.6 = (f32[2,48,128]{2,1,0:T(8,128)}, f32[2,48,128]{2,1,0:T(8,128)S(1)}, u32[]{:S(2)}) copy-start(f32[2,48,128]{2,1,0:T(8,128)S(1)} %collective-permute-done.2.left_ref) | copy-start | bytes 147460
  92.6 0.6 copy-start.7

commit v2 on v1

--- a/solution.py
+++ b/solution.py
@@ -17,6 +17,17 @@
 
 def vmem_spec():
     return pl.BlockSpec(memory_space=pltpu.VMEM)
+
+
+KERNEL = pltpu.CompilerParams(vmem_limit_bytes=30 * 1024 * 1024)
+
+
+def in_vmem(x):
+    return pltpu.with_memory_space_constraint(x, pltpu.VMEM)
+
+
+def vmem_result(*shape):
+    return pltpu.VMEM(shape, jnp.float32)
 
 
 class Sizes:
@@ -75,105 +86,106 @@
     lax.fori_loop(0, s.blocks // UNROLL, some, 0)
 
 
-def restrict_kernel(s, x_ref, rest_ref, pat_ref, out_ref, acc):
-    step = pl.program_id(0)
-
-    @pl.when(step == 0)
-    def _():
-        acc[...] = jnp.zeros_like(acc)
-
-    def column(at):
-        mask = pat_ref[0:1, at].astype(jnp.float32)
-        value = [x_ref[comp, :, at] for comp in range(3)]
-        for comp in range(3):
-            total = acc[comp, :, at]
-            for source in range(3):
-                total = total + (rest_ref[comp, source : source + 1, at] * mask) * value[source]
-            acc[comp, :, at] = total
-
-    each_column(s, column)
-
-    @pl.when(step == FPA - 1)
-    def _():
-        def tile_of(comp, grp):
-            parts = []
-            for member in range(s.group):
-                low = (grp * s.group + member) * LANES
-                parts.append(acc[comp, :, low : low + LANES])
-            return jnp.concatenate(parts, axis=0)
-
-        store_tiles(s, out_ref, tile_of)
+def restrict_kernel(s, chunk, x_hbm, rest_hbm, pat_hbm, out_ref, x_ref, rest_ref, pat_ref, acc, sems):
+    loads = pl.ds(chunk * s.q, s.q)
+    copies = []
+    for part in range(FPA):
+        at = pl.ds(part * s.agg, s.agg)
+        group = (
+            pltpu.make_async_copy(rest_hbm.at[:, :, at], rest_ref.at[part], sems.at[part, 0]),
+            pltpu.make_async_copy(pat_hbm.at[:, at], pat_ref.at[part], sems.at[part, 1]),
+            pltpu.make_async_copy(x_hbm.at[:, loads, at], x_ref.at[part], sems.at[part, 2]),
+        )
+        for copy in group:
+            copy.start()
+        copies.append(group)
+
+    for part in range(FPA):
+        for copy in copies[part]:
+            copy.wait()
+
+        def column(at, part=part):
+            mask = pat_ref[part, 0:1, at].astype(jnp.float32)
+            value = [x_ref[part, comp, :, at] for comp in range(3)]
+            for comp in range(3):
+                total = (rest_ref[part, comp, 0:1, at] * mask) * value[0]
+                for source in range(1, 3):
+                    total = total + (rest_ref[part, comp, source : source + 1, at] * mask) * value[source]
+                acc[comp, :, at] = total if part == 0 else acc[comp, :, at] + total
+
+        each_column(s, column)
+
+    def tile_of(comp, grp):
+        parts = []
+        for member in range(s.group):
+            low = (grp * s.group + member) * LANES
+            parts.append(acc[comp, :, low : low + LANES])
+        return jnp.concatenate(parts, axis=0)
+
+    store_tiles(s, out_ref, tile_of)
 
 
 def restrict(s, residual, restriction, pattern, chunk):
     return pl.pallas_call(
-        functools.partial(restrict_kernel, s),
-        grid=(FPA,),
-        in_specs=[
-            pl.BlockSpec((3, s.q, s.agg), lambda p: (0, chunk, p)),
-            pl.BlockSpec((3, 3, s.agg), lambda p: (0, 0, p)),
-            pl.BlockSpec((1, s.agg), lambda p: (0, p)),
+        functools.partial(restrict_kernel, s, chunk),
+        in_specs=[pl.BlockSpec(memory_space=pltpu.HBM)] * 3,
+        out_specs=vmem_spec(),
+        out_shape=vmem_result(s.devices * s.per_peer, LANES),
+        scratch_shapes=[
+            pltpu.VMEM((FPA, 3, s.q, s.agg), jnp.float32),
+            pltpu.VMEM((FPA, 3, 3, s.agg), jnp.float32),
+            pltpu.VMEM((FPA, 1, s.agg), jnp.int32),
+            pltpu.VMEM((3, s.q, s.agg), jnp.float32),
+            pltpu.SemaphoreType.DMA((FPA, 3)),
         ],
-        out_specs=pl.BlockSpec((s.devices * s.per_peer, LANES), lambda p: (0, 0)),
-        out_shape=jax.ShapeDtypeStruct((s.devices * s.per_peer, LANES), jnp.float32),
-        scratch_shapes=[pltpu.VMEM((3, s.q, s.agg), jnp.float32)],
         name="restrict",
-    )(residual, restriction, pattern)
-
-
-def prolong_kernel(s, in_ref, rest_ref, pat_ref, out_ref, agg):
-    step = pl.program_id(0)
-
-    @pl.when(step == 0)
-    def _():
-        def take(comp, grp, turned):
-            for member in range(s.group):
-                low = (grp * s.group + member) * LANES
-                agg[comp, :, low : low + LANES] = turned[member * s.q : (member + 1) * s.q]
-
-        load_tiles(s, in_ref, take)
-
-    def column(at):
-        mask = pat_ref[0:1, at].astype(jnp.float32)
-        value = [agg[comp, :, at] for comp in range(3)]
-        for comp in range(3):
-            total = (rest_ref[0, comp : comp + 1, at] * mask) * value[0]
-            for source in range(1, 3):
-                total = total + (rest_ref[source, comp : comp + 1, at] * mask) * value[source]
-            out_ref[comp, :, at] = total
-
-    each_column(s, column)
-
-
-def prolong(s, arrived, restriction, pattern, chunk, whole):
-    kernel = functools.partial(prolong_kernel, s)
-    specs = [
-        vmem_spec(),
-        pl.BlockSpec((3, 3, s.agg), lambda p: (0, 0, p)),
-        pl.BlockSpec((1, s.agg), lambda p: (0, p)),
-    ]
-    args = [arrived, restriction, pattern]
-    alias = {}
-    body = kernel
-    if whole is not None:
-        specs.append(pl.BlockSpec(memory_space=pl.ANY))
-        args.append(whole)
-        alias = {3: 0}
-
-        def body(in_ref, rest_ref, pat_ref, whole_ref, out_ref, agg):
-            del whole_ref
-            kernel(in_ref, rest_ref, pat_ref, out_ref, agg)
-
+        compiler_params=KERNEL,
+    )(*(pltpu.with_memory_space_constraint(x, pltpu.HBM) for x in (residual, restriction, pattern)))
+
+
+def prolong_kernel(s, in_ref, rest_ref, pat_ref, out_hbm, agg, out_ref, sems):
+    def take(comp, grp, turned):
+        for member in range(s.group):
+            low = (grp * s.group + member) * LANES
+            agg[comp, :, low : low + LANES] = turned[member * s.q : (member + 1) * s.q]
+
+    load_tiles(s, in_ref, take)
+    copies = []
+    for part in range(FPA):
+        def column(at, part=part):
+            there = pl.ds(pl.multiple_of(at.start + part * s.agg, LANES), LANES)
+            mask = pat_ref[0:1, there].astype(jnp.float32)
+            value = [agg[comp, :, at] for comp in range(3)]
+            for comp in range(3):
+                total = (rest_ref[0, comp : comp + 1, there] * mask) * value[0]
+                for source in range(1, 3):
+                    total = total + (rest_ref[source, comp : comp + 1, there] * mask) * value[source]
+                out_ref[part, comp, :, at] = total
+
+        each_column(s, column)
+        copy = pltpu.make_async_copy(
+            out_ref.at[part], out_hbm.at[:, :, pl.ds(part * s.agg, s.agg)], sems.at[part]
+        )
+        copy.start()
+        copies.append(copy)
+    for copy in copies:
+        copy.wait()
+
+
+def prolong(s, arrived, restriction, pattern):
     return pl.pallas_call(
-        body,
-        grid=(FPA,),
-        in_specs=specs,
-        out_specs=pl.BlockSpec((3, s.q, s.agg), lambda p: (0, chunk, p)),
+        functools.partial(prolong_kernel, s),
+        in_specs=[vmem_spec()] * 3,
+        out_specs=pl.BlockSpec(memory_space=pltpu.HBM),
         out_shape=jax.ShapeDtypeStruct((3, s.loads, s.fine), jnp.float32),
-        scratch_shapes=[pltpu.VMEM((3, s.q, s.agg), jnp.float32)],
-        input_output_aliases=alias,
+        scratch_shapes=[
+            pltpu.VMEM((3, s.q, s.agg), jnp.float32),
+            pltpu.VMEM((FPA, 3, s.q, s.agg), jnp.float32),
+            pltpu.SemaphoreType.DMA((FPA,)),
+        ],
         name="prolong",
-    )(*args)
+        compiler_params=KERNEL,
+    )(in_vmem(arrived), in_vmem(restriction), in_vmem(pattern))
 
 
 def collect_kernel(s, slot_ref, in_ref, out_ref, table, lines, even, odd):
@@ -221,10 +233,11 @@
         functools.partial(collect_kernel, s),
         in_specs=[pl.BlockSpec(memory_space=pltpu.SMEM), vmem_spec()],
         out_specs=vmem_spec(),
-        out_shape=jax.ShapeDtypeStruct((s.rows, s.comps, LANES), jnp.float32),
+        out_shape=vmem_result(s.rows, s.comps, LANES),
         scratch_shapes=line_scratch(s),
         name="collect",
-    )(slots, received)
+        compiler_params=KERNEL,
+    )(slots, in_vmem(received))
 
 
 PACK = 32
@@ -257,14 +270,15 @@
 
 def pack_edges(s, body, before, after):
     packs = -(-s.wide // PACK)
-    shape = jax.ShapeDtypeStruct((packs, s.comps, LANES), jnp.float32)
+    shape = vmem_result(packs, s.comps, LANES)
     return pl.pallas_call(
         functools.partial(pack_kernel, s),
         in_specs=[vmem_spec()] * 3,
         out_specs=[vmem_spec()] * 2,
         out_shape=[shape, shape],
         name="pack_edges",
-    )(body, before, after)
+        compiler_params=KERNEL,
+    )(body, in_vmem(before), in_vmem(after))
 
 
 def sweeps_kernel(
@@ -401,11 +415,12 @@
         out_specs=[vmem_spec()] * 2,
         out_shape=[
             jax.ShapeDtypeStruct((s.q * 3 * s.rows, LANES), jnp.float32),
-            jax.ShapeDtypeStruct((s.devices * s.per_peer, LANES), jnp.float32),
+            vmem_result(s.devices * s.per_peer, LANES),
         ],
         scratch_shapes=[state, state, state, tile] + line_scratch(s),
         name="sweeps",
-    )(slots, rhs, before, after, left, right, coefs)
+        compiler_params=KERNEL,
+    )(slots, rhs, *map(in_vmem, (before, after, left, right, coefs)))
 
 
 def ring(axis):
@@ -471,6 +486,7 @@
     solutions = []
     arrived = []
     for chunk in range(CHUNKS):
+        received[chunk], coefs = lax.optimization_barrier((received[chunk], coefs))
         rhs = collect(s, received[chunk], slots)
         before = lax.ppermute(rhs[-s.depth :], "row", row_up)
         after = lax.ppermute(rhs[: s.depth], "row", row_down)
@@ -480,9 +496,7 @@
         sol, outgoing = sweeps(s, slots, rhs, before, after, ahead, past, coefs)
         solutions.append(sol.reshape(s.q, 3, s.rows, LANES))
         arrived.append(exchange(s, outgoing))
-    correction = None
-    for chunk in range(CHUNKS):
-        correction = prolong(s, arrived[chunk], restriction, pattern, chunk, correction)
+    correction = prolong(s, arrived[0], restriction, pattern)
     return solutions[0] if CHUNKS == 1 else jnp.concatenate(solutions), correction.transpose(1, 0, 2)
 
 

time: 168 us -> 155 us (0.923)
  Pallas kernels: 61.2 us -> 49.2 us
  blocking collectives: 35.3 us -> 45.2 us
  waiting for transfers between devices: 28.3 us -> 18.5 us
  starting transfers between devices: 26.7 us -> 32.4 us
  local copies, waits for them, and re-layouts: 10.2 us -> 5.55 us
    all_to_all x1, waiting for transfers between devices: 21.9 us -> 4.26 us  [exchange(): lax.all_to_all(blocks, AXES, split_axis=0, concat_axis=0, tiled=True)]
    all_to_all x1, blocking collectives: 35.3 us -> 45.2 us  [exchange(): lax.all_to_all(blocks, AXES, split_axis=0, concat_axis=0, tiled=True)]
    pallas_call x2, Pallas kernels: 19.1 us -> 11.9 us  [the longest x1 6.91 us: restrict(): pl.pallas_call(functools.partial(restrict_kernel, s, chunk), in_specs=[pl...]
    ppermute x1, starting transfers between devices: 3.03 us -> 10.1 us  [body(): before = lax.ppermute(rhs[-s.depth:], 'row', row_up)]
    ppermute x1, waiting for transfers between devices: 0.01 us -> 5.17 us  [wide_coefficients(): lax.ppermute(coefs[..., :s.depth].transpose(2, 1, 0), 'col', down)]
    transpose x2, local copies, waits for them, and re-layouts: 3.93 us -> 1.04 us  [wide_coefficients(): coefs[..., :s.depth].transpose(2, 1, 0)]
    ppermute x1, waiting for transfers between devices: 2.53 us -> 4.72 us  [body(): past = lax.ppermute(left, 'col', col_down)]
    pallas_call x1, Pallas kernels: 2.68 us -> 0.74 us  [pack_edges(): pl.pallas_call(functools.partial(pack_kernel, s), in_specs=[vmem_spec()]...]
  transfers between devices with their start and end apart: 9 -> 9, of which waited for: 4 -> 6; matrix products, arithmetic and copies ran while one was open for 7% -> 5% of each run, Pallas kernels for 0% -> 0%
where the time goes in v2:
time: 155 us
  Pallas kernels  49.2 us (32%)
  blocking collectives  45.2 us (29%)
  starting transfers between devices  32.4 us (21%)
  waiting for transfers between devices  18.5 us (12%)
  local copies, waits for them, and re-layouts  5.55 us (4%)
  other arithmetic  2.91 us (2%)
    all_to_all x1, blocking collectives, exchange(): lax.all_to_all(blocks, AXES, split_axis=0, concat_axis=0, tiled=True)  45.2 us
    pallas_call x1, Pallas kernels, sweeps(): pl.pallas_call(functools.partial(sweeps_kernel, s), in_specs=[pl.BlockSpe...  27.2 us
    ppermute x1, starting transfers between devices, body(): before = lax.ppermute(rhs[-s.depth:], 'row', row_up)  10.1 us
    pallas_call x1, Pallas kernels, collect(): pl.pallas_call(functools.partial(collect_kernel, s), in_specs=[pl.BlockSp...  9.39 us
    all_to_all x1, starting transfers between devices, exchange(): lax.all_to_all(blocks, AXES, split_axis=0, concat_axis=0, tiled=True)  7.45 us
    pallas_call x1, Pallas kernels, restrict(): pl.pallas_call(functools.partial(restrict_kernel, s, chunk), in_specs=[pl...  6.91 us
    ppermute x1, waiting for transfers between devices, wide_coefficients(): lax.ppermute(coefs[..., :s.depth].transpose(2, 1, 0), 'col', down)  5.17 us
    pallas_call x1, Pallas kernels, prolong(): pl.pallas_call(functools.partial(prolong_kernel, s), in_specs=[vmem_spec(...  5.03 us
  transfers between devices with their start and end apart: 9, of which 6 were waited for; matrix products, arithmetic and copies ran while one was open for 5% of the time, Pallas kernels for 0%

profile of v2, /device:TPU:0, one launch (start us, length us, event | category | flops | bytes accessed | tf_op | source)
XLA Modules:
  0.0 154.7 jit_solution(7636645891294663466)
XLA Ops:
  0.6 6.9 %restrict.1 = f32[2304,128]{1,0:T(8,128)} custom-call(f32[3,16,49152]{2,1,0:T(8,128)} %bitcast.24, f32[3,3,49152]{2,1,0:T(4,128)} %rest_ref.1, s32[1,49152]{1,0:T(1,128)} %bitcast.22), custom_call_target="tpu_custom_call" | custom-call | tf_op jit(solution)/shard_map/restrict/pallas_call | solution.py:129
  7.5 0.0 copy-start.5
  7.6 0.0 copy-start.4
  7.6 0.0 copy-start.3
  7.6 7.4 %all-to-all-start = ((f32[32,72,128]{2,1,0:T(8,128)}), f32[32,72,128]{2,1,0:T(8,128)}, u32[]{:S(2)}, u32[]{:S(2)}) async-start(f32[32,72,128]{2,1,0:T(8,128)} %bitcast.3), calls=%async_computation | async-start | bytes 2359296 | tf_op jit(solution)/shard_map/all_to_all | solution.py:449
  15.0 0.0 copy-done.5
  15.1 0.0 copy-done.4
  15.1 0.1 copy.13
  15.2 0.0 copy-done.3
  15.2 0.1 broadcast_multiply_fusion
  15.3 0.3 copy.14
  15.6 0.1 maximum_bitcast_fusion
  15.7 0.0 copy-start.2
  15.7 2.1 %collective-permute-start = (f32[3,45,128]{2,1,0:T(8,128)S(1)}, f32[3,45,128]{2,1,0:T(8,128)S(1)}, u32[]{:S(2)}, u32[]{:S(2)}) collective-permute-start(f32[3,45,128]{2,1,0:T(8,128)S(1)} %get-tuple-element.18), channel_id=1, source_target_pairs={{0,4},{4,8},{8,12},{12,16},{16,20},{20,24},{24,28},{1,5},{5,9},{9,... | collective-permute-start | bytes 207368 | tf_op jit(solution)/shard_map/ppermute | solution.py:437
  17.8 1.3 collective-permute-start.1
  19.1 0.0 collective-permute-done
  19.1 3.0 %collective-permute-done.1 = f32[3,45,128]{2,1,0:T(8,128)S(1)} collective-permute-done((f32[3,45,128]{2,1,0:T(8,128)S(1)}, f32[3,45,128]{2,1,0:T(8,128)S(1)}, u32[]{:S(2)}, u32[]{:S(2)}) %collective-permute-start.1) | collective-permute-done | bytes 69152 | tf_op jit(solution)/shard_map/ppermute | solution.py:438
  22.1 0.1 pad_maximum_fusion.1
  22.2 0.4 slice_bitcast_fusion.1
  22.6 0.0 copy-start.6
  22.6 0.6 copy.15
  23.2 0.6 copy.17
  23.9 3.4 %collective-permute-start.3 = (f32[3,45,54]{2,1,0:T(8,128)S(1)}, f32[3,45,54]{2,1,0:T(8,128)S(1)}, u32[]{:S(2)}, u32[]{:S(2)}) collective-permute-start(f32[3,45,54]{2,1,0:T(8,128)S(1)} %copy.17), channel_id=1, source_target_pairs={{0,1},{1,2},{2,3},{4,5},{5,6},{6,7},{8,9},{9,10},{10,11},{12,13},{... | collective-permute-start | bytes 87488 | tf_op jit(solution)/shard_map/ppermute | solution.py:441
  27.3 1.3 collective-permute-start.2
  28.6 0.0 copy-done.6
  28.6 0.1 fusion.2.slot_ref
  28.6 0.1 pad.4.clone
  28.7 5.2 %collective-permute-done.2 = f32[3,45,54]{2,1,0:T(8,128)S(1)} collective-permute-done((f32[3,45,54]{2,1,0:T(8,128)S(1)}, f32[3,45,54]{2,1,0:T(8,128)S(1)}, u32[]{:S(2)}, u32[]{:S(2)}) %collective-permute-start.2) | collective-permute-done | bytes 29192 | tf_op jit(solution)/shard_map/ppermute | solution.py:442
  33.9 1.7 %copy.16 = f32[3,45,54]{0,1,2:T(8,128)} copy(f32[3,45,54]{2,1,0:T(8,128)S(1)} %collective-permute-done.2) | data formatting | bytes 58320 | tf_op jit(solution)/shard_map/ppermute | solution.py:442
  35.6 0.0 collective-permute-done.3
  35.6 1.7 %copy.18 = f32[3,45,54]{0,1,2:T(8,128)} copy(f32[3,45,54]{2,1,0:T(8,128)S(1)} %collective-permute-done.3) | data formatting | bytes 58320 | tf_op jit(solution)/shard_map/ppermute | solution.py:441
  37.3 2.6 %pad_maximum_fusion.coef_ref = f32[54,45,256]{2,1,0:T(8,128)S(1)} fusion(f32[54,45,3]{2,1,0:T(8,128)} %bitcast.27, f32[54,45,3]{2,1,0:T(8,128)} %bitcast.26, f32[3,45,128]{2,1,0:T(8,128)S(1)} %collective-permute-done.1, f32[48,45,128]{2,1,0:T(8,128)} %copy-done.2, f32[3,45,128]{2,1,0:T(8,128)S(1)} %collective-permute-done, f32[256]{0:T(256)S(1)} %pad.4.clone), kind=kLoop, calls=%fused_computation | loop fusion | flops 3110400 | bytes 3791824 | tf_op jit(solution)/shard_map/concatenate | solution.py:444
  39.8 4.3 %all-to-all-done = f32[32,72,128]{2,1,0:T(8,128)} async-done(((f32[32,72,128]{2,1,0:T(8,128)}), f32[32,72,128]{2,1,0:T(8,128)}, u32[]{:S(2)}, u32[]{:S(2)}) %all-to-all-start) | async-done | bytes 1179680 | tf_op jit(solution)/shard_map/all_to_all | solution.py:449
  44.1 9.4 %collect.1.body_ref.rhs_ref = f32[48,48,128]{2,1,0:T(8,128)S(1)} custom-call(s32[6144]{0:T(1024)S(1)} %fusion.2.slot_ref, f32[2304,128]{1,0:T(8,128)} %bitcast.4.in_ref), custom_call_target="tpu_custom_call" | custom-call | tf_op jit(solution)/shard_map/collect/pallas_call | solution.py:232
  53.5 1.3 collective-permute-start.5
  54.8 10.1 %collective-permute-start.4 = (f32[3,48,128]{2,1,0:T(8,128)S(1)}, f32[3,48,128]{2,1,0:T(8,128)S(1)}, u32[]{:S(2)}, u32[]{:S(2)}) collective-permute-start(f32[3,48,128]{2,1,0:T(8,128)S(1)} %get-tuple-element.17), channel_id=1, source_target_pairs={{0,4},{4,8},{8,12},{12,16},{16,20},{20,24},{24,28},{1,5},{5,9},{9,... | collective-permute-start | bytes 221192 | tf_op jit(solution)/shard_map/ppermute | solution.py:491
  64.9 0.0 collective-permute-done.5.after_ref
  64.9 0.9 collective-permute-done.4.before_ref
  65.8 0.7 pack_edges.1
  66.5 4.3 %collective-permute-start.6 = (f32[2,48,128]{2,1,0:T(8,128)S(1)}, f32[2,48,128]{2,1,0:T(8,128)S(1)}, u32[]{:S(2)}, u32[]{:S(2)}) collective-permute-start(f32[2,48,128]{2,1,0:T(8,128)S(1)} %get-tuple-element.9), channel_id=1, source_target_pairs={{0,1},{1,2},{2,3},{4,5},{5,6},{6,7},{8,9},{9,10},{10,11},{12,13},{... | collective-permute-start | bytes 147464 | tf_op jit(solution)/shard_map/ppermute | solution.py:494
  70.8 1.3 collective-permute-start.7
  72.1 0.4 collective-permute-done.6.left_ref
  72.6 4.7 %collective-permute-done.7.right_ref = f32[2,48,128]{2,1,0:T(8,128)S(1)} collective-permute-done((f32[2,48,128]{2,1,0:T(8,128)S(1)}, f32[2,48,128]{2,1,0:T(8,128)S(1)}, u32[]{:S(2)}, u32[]{:S(2)}) %collective-permute-start.7) | collective-permute-done | bytes 49184 | tf_op jit(solution)/shard_map/ppermute | solution.py:495
  77.3 27.2 %sweeps.1 = (f32[2304,128]{1,0:T(8,128)}, f32[2304,128]{1,0:T(8,128)S(1)}) custom-call(s32[6144]{0:T(1024)S(1)} %fusion.2.slot_ref, f32[48,48,128]{2,1,0:T(8,128)S(1)} %collect.1.body_ref.rhs_ref, f32[3,48,128]{2,1,0:T(8,128)S(1)} %collective-permute-done.4.before_ref, f32[3,48,128]{2,1,0:T(8,128)S(1)} %collective-permute-done.5.after_ref, ...), custom_call_target="tpu_custom_call" | custom-call | tf_op jit(solution)/shard_map/sweeps/pallas_call | solution.py:412
  104.5 0.0 copy-start
  104.5 45.2 %all_to_all.10 = f32[32,72,128]{2,1,0:T(8,128)S(1)} all-to-all(f32[32,72,128]{2,1,0:T(8,128)S(1)} %bitcast.21), channel_id=1, replica_groups=mesh['row'=8,'col'=4] {'row','col'}, dimensions={0} | all-to-all | bytes 2359296 | tf_op jit(solution)/shard_map/all_to_all | solution.py:449
  149.7 0.0 copy-done.1
  149.7 5.0 %prolong.1 = f32[3,16,49152]{2,1,0:T(8,128)} custom-call(f32[2304,128]{1,0:T(8,128)S(1)} %bitcast.20, f32[3,3,49152]{2,1,0:T(4,128)S(1)} %copy-done, s32[1,49152]{1,0:T(1,128)S(1)} %bitcast.23), custom_call_target="tpu_custom_call" | custom-call | tf_op jit(solution)/shard_map/prolong/pallas_call | solution.py:176
  (7 shorter events, 0.0 us)
Async XLA Ops:
  7.5 7.5 %copy-start.5 = (s32[4,48,128]{2,1,0:T(8,128)S(1)}, s32[4,48,128]{2,1,0:T(8,128)}, u32[]{:S(2)}) copy-start(s32[4,48,128]{2,1,0:T(8,128)} %param.13) | copy-start | bytes 294916
  7.6 7.5 %copy-start.4 = (f32[3,3,48,128]{3,2,1,0:T(8,128)S(1)}, f32[3,3,48,128]{3,2,1,0:T(8,128)}, u32[]{:S(2)}) copy-start(f32[3,3,48,128]{3,2,1,0:T(8,128)} %param.11) | copy-start | bytes 663556
  7.6 7.6 %copy-start.3 = (f32[4,3,3,48,128]{4,3,2,1,0:T(8,128)S(1)}, f32[4,3,3,48,128]{4,3,2,1,0:T(8,128)}, u32[]{:S(2)}) copy-start(f32[4,3,3,48,128]{4,3,2,1,0:T(8,128)} %param.12) | copy-start | bytes 2654212
  7.6 36.5 %all-to-all-start = ((f32[32,72,128]{2,1,0:T(8,128)}), f32[32,72,128]{2,1,0:T(8,128)}, u32[]{:S(2)}, u32[]{:S(2)}) async-start(f32[32,72,128]{2,1,0:T(8,128)} %bitcast.3), calls=%async_computation | async-start | bytes 2359296 | tf_op jit(solution)/shard_map/all_to_all | solution.py:449
  15.7 6.4 %copy-start.2 = (f32[48,45,128]{2,1,0:T(8,128)}, f32[48,45,128]{2,1,0:T(8,128)S(1)}, u32[]{:S(2)}) copy-start(f32[48,45,128]{2,1,0:T(8,128)S(1)} %maximum_bitcast_fusion) | copy-start | bytes 3317764
  15.7 3.4 %collective-permute-start = (f32[3,45,128]{2,1,0:T(8,128)S(1)}, f32[3,45,128]{2,1,0:T(8,128)S(1)}, u32[]{:S(2)}, u32[]{:S(2)}) collective-permute-start(f32[3,45,128]{2,1,0:T(8,128)S(1)} %get-tuple-element.18), channel_id=1, source_target_pairs={{0,4},{4,8},{8,12},{12,16},{16,20},{20,24},{24,28},{1,5},{5,9},{9,... | collective-permute-start | bytes 207368 | tf_op jit(solution)/shard_map/ppermute | solution.py:437
  17.8 4.3 %collective-permute-start.1 = (f32[3,45,128]{2,1,0:T(8,128)S(1)}, f32[3,45,128]{2,1,0:T(8,128)S(1)}, u32[]{:S(2)}, u32[]{:S(2)}) collective-permute-start(f32[3,45,128]{2,1,0:T(8,128)S(1)} %get-tuple-element.19), channel_id=1, source_target_pairs={{4,0},{8,4},{12,8},{16,12},{20,16},{24,20},{28,24},{5,1},{9,5},{13... | collective-permute-start | bytes 207368 | tf_op jit(solution)/shard_map/ppermute | solution.py:438
  22.6 5.9 %copy-start.6 = (s32[48,128]{1,0:T(8,128)S(1)}, s32[48,128]{1,0:T(8,128)}, u32[]{:S(2)}) copy-start(s32[48,128]{1,0:T(8,128)} %param.10) | copy-start | bytes 73732
  23.9 11.7 %collective-permute-start.3 = (f32[3,45,54]{2,1,0:T(8,128)S(1)}, f32[3,45,54]{2,1,0:T(8,128)S(1)}, u32[]{:S(2)}, u32[]{:S(2)}) collective-permute-start(f32[3,45,54]{2,1,0:T(8,128)S(1)} %copy.17), channel_id=1, source_target_pairs={{0,1},{1,2},{2,3},{4,5},{5,6},{6,7},{8,9},{9,10},{10,11},{12,13},{... | collective-permute-start | bytes 87488 | tf_op jit(solution)/shard_map/ppermute | solution.py:441
  27.3 6.6 %collective-permute-start.2 = (f32[3,45,54]{2,1,0:T(8,128)S(1)}, f32[3,45,54]{2,1,0:T(8,128)S(1)}, u32[]{:S(2)}, u32[]{:S(2)}) collective-permute-start(f32[3,45,54]{2,1,0:T(8,128)S(1)} %copy.15), channel_id=1, source_target_pairs={{1,0},{2,1},{3,2},{5,4},{6,5},{7,6},{9,8},{10,9},{11,10},{13,12},{... | collective-permute-start | bytes 87488 | tf_op jit(solution)/shard_map/ppermute | solution.py:442
  53.5 11.4 %collective-permute-start.5 = (f32[3,48,128]{2,1,0:T(8,128)S(1)}, f32[3,48,128]{2,1,0:T(8,128)S(1)}, u32[]{:S(2)}, u32[]{:S(2)}) collective-permute-start(f32[3,48,128]{2,1,0:T(8,128)S(1)} %get-tuple-element.16), channel_id=1, source_target_pairs={{4,0},{8,4},{12,8},{16,12},{20,16},{24,20},{28,24},{5,1},{9,5},{13... | collective-permute-start | bytes 221192 | tf_op jit(solution)/shard_map/ppermute | solution.py:492
  54.8 11.0 %collective-permute-start.4 = (f32[3,48,128]{2,1,0:T(8,128)S(1)}, f32[3,48,128]{2,1,0:T(8,128)S(1)}, u32[]{:S(2)}, u32[]{:S(2)}) collective-permute-start(f32[3,48,128]{2,1,0:T(8,128)S(1)} %get-tuple-element.17), channel_id=1, source_target_pairs={{0,4},{4,8},{8,12},{12,16},{16,20},{20,24},{24,28},{1,5},{5,9},{9,... | collective-permute-start | bytes 221192 | tf_op jit(solution)/shard_map/ppermute | solution.py:491
  66.5 6.0 %collective-permute-start.6 = (f32[2,48,128]{2,1,0:T(8,128)S(1)}, f32[2,48,128]{2,1,0:T(8,128)S(1)}, u32[]{:S(2)}, u32[]{:S(2)}) collective-permute-start(f32[2,48,128]{2,1,0:T(8,128)S(1)} %get-tuple-element.9), channel_id=1, source_target_pairs={{0,1},{1,2},{2,3},{4,5},{5,6},{6,7},{8,9},{9,10},{10,11},{12,13},{... | collective-permute-start | bytes 147464 | tf_op jit(solution)/shard_map/ppermute | solution.py:494
  70.8 6.5 %collective-permute-start.7 = (f32[2,48,128]{2,1,0:T(8,128)S(1)}, f32[2,48,128]{2,1,0:T(8,128)S(1)}, u32[]{:S(2)}, u32[]{:S(2)}) collective-permute-start(f32[2,48,128]{2,1,0:T(8,128)S(1)} %get-tuple-element.10), channel_id=1, source_target_pairs={{1,0},{2,1},{3,2},{5,4},{6,5},{7,6},{9,8},{10,9},{11,10},{13,12},{... | collective-permute-start | bytes 147464 | tf_op jit(solution)/shard_map/ppermute | solution.py:495
  77.3 72.4 %copy-start.1 = (s32[49152]{0:T(1024)S(1)}, s32[49152]{0:T(1024)}, u32[]{:S(2)}) copy-start(s32[49152]{0:T(1024)} %param.9) | copy-start | bytes 589828
  104.5 45.2 %copy-start = (f32[3,3,49152]{2,1,0:T(4,128)S(1)}, f32[3,3,49152]{2,1,0:T(4,128)}, u32[]{:S(2)}) copy-start(f32[3,3,49152]{2,1,0:T(4,128)} %rest_ref.1) | copy-start | bytes 5308420

commit v3 on v2

--- a/solution.py
+++ b/solution.py
@@ -244,28 +244,43 @@
 EDGE = LANES // PACK
 
 
-def pack_kernel(s, body_ref, before_ref, after_ref, left_ref, right_ref):
-    where = lax.broadcasted_iota(jnp.int32, (s.comps, LANES), 1) // EDGE
-    packs = left_ref.shape[0]
-    for pack in range(packs):
-        left = jnp.zeros((s.comps, LANES), jnp.float32)
-        right = jnp.zeros((s.comps, LANES), jnp.float32)
-        for member in range(PACK):
-            at = pack * PACK + member
-            if at >= s.wide:
-                break
-            if at < s.depth:
-                line = before_ref[at]
-            elif at < s.depth + s.rows:
-                line = body_ref[at - s.depth]
+def pack_lines(line_of, count, left_ref, right_ref):
+    for pack in range(left_ref.shape[0]):
+        left = right = None
+        for member in range(min(PACK, count - pack * PACK)):
+            line = line_of(pack * PACK + member)
+            head = pltpu.roll(line, member * EDGE, 1) if member else line
+            turn = (member + 1) * EDGE
+            tail = pltpu.roll(line, turn, 1) if turn < LANES else line
+            if left is None:
+                here = lax.broadcasted_iota(jnp.int32, line.shape, 1) // EDGE
+                left, right = head, tail
             else:
-                line = after_ref[at - s.depth - s.rows]
-            here = where == member
-            left = jnp.where(here, pltpu.roll(line, member * EDGE, 1) if member else line, left)
-            turn = (member + 1) * EDGE
-            right = jnp.where(here, pltpu.roll(line, turn, 1) if turn < LANES else line, right)
+                left = jnp.where(here == member, head, left)
+                right = jnp.where(here == member, tail, right)
         left_ref[pack] = left
         right_ref[pack] = right
+
+
+def beyond(past, ahead, member, depth):
+    if member:
+        past = pltpu.roll(past, LANES - member * EDGE, 1)
+    turn = (member + 1) * EDGE
+    if turn < LANES:
+        ahead = pltpu.roll(ahead, LANES - turn, 1)
+    lane = lax.broadcasted_iota(jnp.int32, past.shape, 1)
+    return jnp.where(lane < depth, past, jnp.where(lane >= LANES - depth, ahead, 0.0))
+
+
+def pack_kernel(s, body_ref, before_ref, after_ref, left_ref, right_ref):
+    def line_of(at):
+        if at < s.depth:
+            return before_ref[at]
+        if at < s.depth + s.rows:
+            return body_ref[at - s.depth]
+        return after_ref[at - s.depth - s.rows]
+
+    pack_lines(line_of, s.wide, left_ref, right_ref)
 
 
 def pack_edges(s, body, before, after):
@@ -281,11 +296,81 @@
     )(body, in_vmem(before), in_vmem(after))
 
 
+COEFS = 48
+
+
+def prepare_kernel(s, inv_ref, off_ref, pat_ref, body_ref, top_ref, bottom_ref, left_ref, right_ref, flat):
+    rows = s.rows
+    flat[0 : 9 * rows, :] = inv_ref[...]
+    for direction in range(4):
+        mask = pat_ref[direction * rows : (direction + 1) * rows, :].astype(jnp.float32)
+        for entry in range(9):
+            at = direction * 9 + entry
+            flat[(9 + at) * rows : (10 + at) * rows, :] = off_ref[at * rows : (at + 1) * rows, :] * mask
+    flat[45 * rows : COEFS * rows, :] = jnp.zeros(((COEFS - 45) * rows, LANES), jnp.float32)
+
+    def one(row, carry):
+        for low in range(0, COEFS, 8):
+            body_ref[row, low : low + 8, :] = flat[pl.ds(low * rows + row, 8, stride=rows), :]
+        return carry
+
+    lax.fori_loop(0, rows, one, 0)
+    top_ref[...] = body_ref[0 : s.depth]
+    bottom_ref[...] = body_ref[rows - s.depth : rows]
+    pack_lines(lambda at: body_ref[at], rows, left_ref, right_ref)
+
+
+def prepare(s, inverse, blocks, pattern):
+    packs = vmem_result(-(-s.rows // PACK), COEFS, LANES)
+    edge = vmem_result(s.depth, COEFS, LANES)
+    return pl.pallas_call(
+        functools.partial(prepare_kernel, s),
+        in_specs=[vmem_spec()] * 3,
+        out_specs=[vmem_spec()] * 5,
+        out_shape=[vmem_result(s.rows, COEFS, LANES), edge, edge, packs, packs],
+        scratch_shapes=[pltpu.VMEM((COEFS * s.rows, LANES), jnp.float32)],
+        name="prepare",
+        compiler_params=KERNEL,
+    )(inverse.reshape(-1, LANES), blocks.reshape(-1, LANES), pattern.reshape(-1, LANES))
+
+
+def widen_kernel(
+    s, body_ref, before_ref, after_ref, past_ref, ahead_ref,
+    before_past_ref, before_ahead_ref, after_past_ref, after_ahead_ref, out_ref,
+):
+    last = (s.rows - s.depth) % PACK
+    for at in range(s.wide):
+        row = at - s.depth
+        if row < 0:
+            line = before_ref[at]
+            side = beyond(before_past_ref[0], before_ahead_ref[0], last + at, s.depth)
+        elif row < s.rows:
+            line = body_ref[row]
+            side = beyond(past_ref[row // PACK], ahead_ref[row // PACK], row % PACK, s.depth)
+        else:
+            line = after_ref[row - s.rows]
+            side = beyond(after_past_ref[0], after_ahead_ref[0], row - s.rows, s.depth)
+        out_ref[at, :, 0:LANES] = line
+        out_ref[at, :, LANES : 2 * LANES] = side
+
+
+def widen(s, *parts):
+    return pl.pallas_call(
+        functools.partial(widen_kernel, s),
+        in_specs=[vmem_spec()] * 9,
+        out_specs=vmem_spec(),
+        out_shape=vmem_result(s.wide, COEFS, 2 * LANES),
+        name="widen",
+        compiler_params=KERNEL,
+    )(*map(in_vmem, parts))
+
+
 def sweeps_kernel(
-    s, slot_ref, rhs_ref, before_ref, after_ref, left_ref, right_ref, coef_ref,
-    sol_ref, out_ref, wide, even, odd, final, table, lines, ahead_lines, behind_lines,
+    s, slot_ref, rhs_ref, before_ref, after_ref, past_ref, ahead_ref, coef_ref,
+    sol_ref, out_ref, wide, even, odd, table, lines, ahead_lines, behind_lines,
 ):
-    lane = lax.broadcasted_iota(jnp.int32, (s.comps, LANES), 1)
+    q = s.q
+    halves = range(0, q, 8)
     for at in range(s.wide):
         if at < s.depth:
             line = before_ref[at]
@@ -294,106 +379,117 @@
         else:
             line = after_ref[at - s.depth - s.rows]
         pack, member = divmod(at, PACK)
-        past = right_ref[pack]
-        if member:
-            past = pltpu.roll(past, LANES - member * EDGE, 1)
-        ahead = left_ref[pack]
-        turn = (member + 1) * EDGE
-        if turn < LANES:
-            ahead = pltpu.roll(ahead, LANES - turn, 1)
         wide[at, :, 0:LANES] = line
-        wide[at, :, LANES : 2 * LANES] = jnp.where(
-            lane < s.depth, past, jnp.where(lane >= LANES - s.depth, ahead, 0.0)
-        )
-
-    q = s.q
-
-    def coefficient(at, index, width):
-        return coef_ref[at, index : index + 1, 0:width]
-
-    def invert(at, total, width):
+        wide[at, :, LANES : 2 * LANES] = beyond(past_ref[pack], ahead_ref[pack], member, s.depth)
+
+    lane = lax.broadcasted_iota(jnp.int32, (8, LANES), 1)
+    is_first = lane == 0
+    is_last = lane == LANES - 1
+    columns = (slice(0, LANES), slice(LANES, 2 * LANES))
+
+    def span(comp, low):
+        return slice(comp * q + low, comp * q + low + 8)
+
+    def invert(at, total, column):
         fresh = []
         for comp in range(3):
-            value = coefficient(at, comp * 3, width) * total[0]
-            for source in range(1, 3):
-                value = value + coefficient(at, comp * 3 + source, width) * total[source]
+            value = [None] * len(halves)
+            for source in range(3):
+                index = comp * 3 + source
+                factor = coef_ref[at, index : index + 1, column]
+                for half in range(len(halves)):
+                    term = factor * total[source][half]
+                    value[half] = term if source == 0 else value[half] + term
             fresh.append(value)
         return fresh
 
-    def span(comp, low):
-        return slice(comp * q + low, comp * q + low + 8)
+    def put(target, at, fresh, column):
+        for comp in range(3):
+            for half, low in enumerate(halves):
+                target[at, span(comp, low), column] = fresh[comp][half]
 
     def first(at, carry):
-        for low in range(0, q, 8):
-            total = [wide[at, span(comp, low), :] for comp in range(3)]
-            fresh = invert(at, total, 2 * LANES)
+        for column in columns:
+            total = [[wide[at, span(comp, low), column] for low in halves] for comp in range(3)]
+            put(even, at, invert(at, total, column), column)
+        return carry
+
+    lax.fori_loop(0, s.wide, first, 0)
+
+    def turned(old, at):
+        west = ([], [])
+        east = ([], [])
+        for comp in range(3):
+            for side in west + east:
+                side.append([])
+            for low in halves:
+                here = [old[at, span(comp, low), column] for column in columns]
+                up = [pltpu.roll(x, 1, 1) for x in here]
+                down = [pltpu.roll(x, LANES - 1, 1) for x in here]
+                for v in range(2):
+                    west[v][-1].append(jnp.where(is_first, up[1 - v], up[v]))
+                    east[v][-1].append(jnp.where(is_last, down[1 - v], down[v]))
+        return west, east
+
+    def sweep(old, at, count):
+        west, east = turned(old, at)
+        result = []
+        for v in range(count):
+            column = columns[v]
+            pieces = []
+            for where in (at - 1, at + 1):
+                pieces.append([[old[where, span(comp, low), column] for low in halves] for comp in range(3)])
+            pieces += [west[v], east[v]]
+            total = []
             for comp in range(3):
-                even[at, span(comp, low), :] = fresh[comp]
-        return carry
-
-    lax.fori_loop(0, s.wide, first, 0)
-
-    def sweep(old, at, low, width):
-        pieces = [[] for _ in range(4)]
-        for source in range(3):
-            part = span(source, low)
-            pieces[0].append(old[at - 1, part, 0:width])
-            pieces[1].append(old[at + 1, part, 0:width])
-            here = old[at, part, :]
-            pieces[2].append(pltpu.roll(here, 1, 1)[:, 0:width])
-            pieces[3].append(pltpu.roll(here, 2 * LANES - 1, 1)[:, 0:width])
-        total = []
-        for comp in range(3):
-            value = wide[at, span(comp, low), 0:width]
-            for direction in range(4):
-                for source in range(3):
-                    index = 9 + (direction * 3 + comp) * 3 + source
-                    value = value - coefficient(at, index, width) * pieces[direction][source]
-            total.append(value)
-        return invert(at, total, width)
+                value = [wide[at, span(comp, low), column] for low in halves]
+                for direction in range(4):
+                    for source in range(3):
+                        index = 9 + (direction * 3 + comp) * 3 + source
+                        factor = coef_ref[at, index : index + 1, column]
+                        for half in range(len(halves)):
+                            value[half] = value[half] - factor * pieces[direction][source][half]
+                total.append(value)
+            result.append(invert(at, total, column))
+        return result
 
     old, new = even, odd
     for inner in range(1, s.depth):
-        def middle(at, carry, old=old, new=new):
-            for low in range(0, q, 8):
-                fresh = sweep(old, at, low, 2 * LANES)
-                for comp in range(3):
-                    new[at, span(comp, low), :] = fresh[comp]
+        def middle(k, carry, old=old, new=new, inner=inner):
+            for step in range(2):
+                at = inner + 2 * k + step
+                for column, fresh in zip(columns, sweep(old, at, 2)):
+                    put(new, at, fresh, column)
             return carry
 
-        lax.fori_loop(inner, s.wide - inner, middle, 0)
+        lax.fori_loop(0, (s.wide - 2 * inner) // 2, middle, 0)
         old, new = new, old
 
-    def last(k, carry):
-        for low in range(0, q, 8):
-            fresh = sweep(old, k + s.depth, low, LANES)
-            for comp in range(3):
-                final[k, span(comp, low), :] = fresh[comp]
-                start = (low * 3 + comp) * s.rows + k
-                sol_ref[pl.ds(start, 8, stride=3 * s.rows), :] = fresh[comp]
-        return carry
-
-    lax.fori_loop(0, s.rows, last, 0)
-
-    def turn_line(row, held):
-        held[:, 0 : s.comps] = final[row].T
+    def finish(row, held):
+        (fresh,) = sweep(old, row + s.depth, 1)
+        put(sol_ref, row, fresh, columns[0])
+        parts = [fresh[comp][half] for comp in range(3) for half in range(len(halves))]
+        held[:, 0 : s.comps] = jnp.concatenate(parts, axis=0).T
 
     def send(row, held):
-        for lane in range(LANES):
-            slot = slot_ref[row * LANES + lane]
-            lines[pl.ds(slot, 1), :] = held[lane : lane + 1, :]
-
-    turn_line(0, ahead_lines)
+        for column in range(LANES):
+            slot = slot_ref[row * LANES + column]
+            lines[pl.ds(slot, 1), :] = held[column : column + 1, :]
+
+    finish(0, ahead_lines)
+    finish(1, behind_lines)
 
     def two(k, carry):
         row = 2 * k
-        turn_line(row + 1, behind_lines)
         send(row, ahead_lines)
-        turn_line(jnp.minimum(row + 2, s.rows - 1), ahead_lines)
         send(row + 1, behind_lines)
+        finish(row + 2, ahead_lines)
+        finish(row + 3, behind_lines)
         return carry
 
-    lax.fori_loop(0, s.rows // 2, two, 0)
+    lax.fori_loop(0, s.rows // 2 - 1, two, 0)
+    send(s.rows - 2, ahead_lines)
+    send(s.rows - 1, behind_lines)
     for block in range(s.blocks):
         table[block] = lines[block * LANES : (block + 1) * LANES, :].T[0 : s.comps]
 
@@ -406,21 +502,20 @@
     store_tiles(s, out_ref, tile_of)
 
 
-def sweeps(s, slots, rhs, before, after, left, right, coefs):
+def sweeps(s, slots, rhs, before, after, past, ahead, coefs):
     state = pltpu.VMEM((s.wide, s.comps, 2 * LANES), jnp.float32)
-    tile = pltpu.VMEM((s.rows, s.comps, LANES), jnp.float32)
     return pl.pallas_call(
         functools.partial(sweeps_kernel, s),
         in_specs=[pl.BlockSpec(memory_space=pltpu.SMEM)] + [vmem_spec()] * 6,
         out_specs=[vmem_spec()] * 2,
         out_shape=[
-            jax.ShapeDtypeStruct((s.q * 3 * s.rows, LANES), jnp.float32),
+            vmem_result(s.rows, s.comps, LANES),
             vmem_result(s.devices * s.per_peer, LANES),
         ],
-        scratch_shapes=[state, state, state, tile] + line_scratch(s),
+        scratch_shapes=[state, state, state] + line_scratch(s),
         name="sweeps",
         compiler_params=KERNEL,
-    )(slots, rhs, *map(in_vmem, (before, after, left, right, coefs)))
+    )(slots, rhs, *map(in_vmem, (before, after, past, ahead)), coefs)
 
 
 def ring(axis):
@@ -429,19 +524,31 @@
     return up, [(j, i) for i, j in up]
 
 
+def shifted(x, down, right):
+    rows, cols = lax.axis_size("row"), lax.axis_size("col")
+    pairs = []
+    for i in range(rows):
+        for j in range(cols):
+            if 0 <= i + down < rows and 0 <= j + right < cols:
+                pairs.append((i * cols + j, (i + down) * cols + j + right))
+    return lax.ppermute(x, AXES, pairs)
+
+
 def wide_coefficients(s, inverse, blocks, pattern):
-    coupling = blocks * pattern.astype(jnp.float32)[:, None, None]
-    coefs = jnp.concatenate([inverse.reshape(9, s.rows, s.cols), coupling.reshape(36, s.rows, s.cols)])
-    coefs = coefs.transpose(1, 0, 2)
-    up, down = ring("row")
-    before = lax.ppermute(coefs[-s.depth :], "row", up)
-    after = lax.ppermute(coefs[: s.depth], "row", down)
-    coefs = jnp.concatenate([before, coefs, after])
-    up, down = ring("col")
-    ahead = lax.ppermute(coefs[..., -s.depth :].transpose(2, 1, 0), "col", up).transpose(2, 1, 0)
-    past = lax.ppermute(coefs[..., : s.depth].transpose(2, 1, 0), "col", down).transpose(2, 1, 0)
-    gap = jnp.zeros(coefs.shape[:2] + (LANES - 2 * s.depth,), jnp.float32)
-    return jnp.concatenate([coefs, past, gap, ahead], axis=2)
+    body, top, bottom, left, right = prepare(s, inverse, blocks, pattern)
+    head, tail = slice(0, 1), slice(-1, None)
+    return widen(
+        s,
+        body,
+        shifted(bottom, 1, 0),
+        shifted(top, -1, 0),
+        shifted(left, 0, -1),
+        shifted(right, 0, 1),
+        shifted(left[tail], 1, -1),
+        shifted(right[tail], 1, 1),
+        shifted(left[head], -1, -1),
+        shifted(right[head], -1, 1),
+    )
 
 
 def exchange(s, outgoing):
@@ -493,8 +600,8 @@
         left, right = pack_edges(s, rhs, before, after)
         ahead = lax.ppermute(right, "col", col_up)
         past = lax.ppermute(left, "col", col_down)
-        sol, outgoing = sweeps(s, slots, rhs, before, after, ahead, past, coefs)
-        solutions.append(sol.reshape(s.q, 3, s.rows, LANES))
+        sol, outgoing = sweeps(s, slots, rhs, before, after, past, ahead, coefs)
+        solutions.append(sol.reshape(s.rows, 3, s.q, LANES).transpose(2, 1, 0, 3))
         arrived.append(exchange(s, outgoing))
     correction = prolong(s, arrived[0], restriction, pattern)
     return solutions[0] if CHUNKS == 1 else jnp.concatenate(solutions), correction.transpose(1, 0, 2)

time: 155 us -> 142 us (0.916)
  blocking collectives: 45.2 us -> 0 us
  waiting for transfers between devices: 18.5 us -> 41.1 us
  starting transfers between devices: 32.4 us -> 52.5 us
  Pallas kernels: 49.2 us -> 40.9 us
  other arithmetic: 2.91 us -> 0.07 us
    all_to_all x1 -> x0, blocking collectives: 45.2 us -> none  [exchange(): lax.all_to_all(blocks, AXES, split_axis=0, concat_axis=0, tiled=True)]
    all_to_all x1 -> x2, waiting for transfers between devices: 4.26 us -> 26.3 us  [exchange(): lax.all_to_all(blocks, AXES, split_axis=0, concat_axis=0, tiled=True)]
    ppermute x4 -> x8, starting transfers between devices: 8.04 us -> 23.9 us  [shifted(): return lax.ppermute(x, AXES, pairs)]
    pallas_call x1, Pallas kernels: 27.2 us -> 16.4 us  [sweeps(): pl.pallas_call(functools.partial(sweeps_kernel, s), in_specs=[pl.BlockSpe...]
    all_to_all x1 -> x2, starting transfers between devices: 7.45 us -> 15.9 us  [exchange(): lax.all_to_all(blocks, AXES, split_axis=0, concat_axis=0, tiled=True)]
    ppermute x1, waiting for transfers between devices: 4.72 us -> 0.13 us  [body(): past = lax.ppermute(left, 'col', col_down)]
    ppermute x1, starting transfers between devices: 10.1 us -> 5.55 us  [body(): before = lax.ppermute(rhs[-s.depth:], 'row', row_up)]
    ppermute x4 -> x8, waiting for transfers between devices: 8.16 us -> 12.3 us  [shifted(): return lax.ppermute(x, AXES, pairs)]
  transfers between devices with their start and end apart: 9 -> 14, of which waited for: 6 -> 5; matrix products, arithmetic and copies ran while one was open for 5% -> 2% of each run, Pallas kernels for 0% -> 2%
where the time goes in v3:
time: 142 us; the launch traced here: 141 us
  starting transfers between devices  52.5 us (37%)
  waiting for transfers between devices  41.1 us (29%)
  Pallas kernels  40.9 us (29%)
  local copies, waits for them, and re-layouts  5.83 us (4%)
    all_to_all x2, waiting for transfers between devices, exchange(): lax.all_to_all(blocks, AXES, split_axis=0, concat_axis=0, tiled=True)  26.3 us
    ppermute x8, starting transfers between devices, shifted(): return lax.ppermute(x, AXES, pairs)  23.9 us
    pallas_call x1, Pallas kernels, sweeps(): pl.pallas_call(functools.partial(sweeps_kernel, s), in_specs=[pl.BlockSpe...  16.4 us
    all_to_all x2, starting transfers between devices, exchange(): lax.all_to_all(blocks, AXES, split_axis=0, concat_axis=0, tiled=True)  15.9 us
    ppermute x8, waiting for transfers between devices, shifted(): return lax.ppermute(x, AXES, pairs)  12.3 us
    pallas_call x1, Pallas kernels, collect(): pl.pallas_call(functools.partial(collect_kernel, s), in_specs=[pl.BlockSp...  9.39 us
    pallas_call x1, Pallas kernels, restrict(): pl.pallas_call(functools.partial(restrict_kernel, s, chunk), in_specs=[pl...  6.91 us
    ppermute x1, starting transfers between devices, body(): before = lax.ppermute(rhs[-s.depth:], 'row', row_up)  5.55 us
  transfers between devices with their start and end apart: 14, of which 5 were waited for; matrix products, arithmetic and copies ran while one was open for 2% of the time, Pallas kernels for 2%

profile of v3, /device:TPU:0, one launch (start us, length us, event | category | flops | bytes accessed | tf_op | source)
XLA Modules:
  0.0 141.5 jit_solution(14516640941826299869)
XLA Ops:
  0.6 6.9 %restrict.1 = f32[2304,128]{1,0:T(8,128)} custom-call(f32[3,16,49152]{2,1,0:T(8,128)} %bitcast.24, f32[3,3,49152]{2,1,0:T(4,128)} %rest_ref.1, s32[1,49152]{1,0:T(1,128)} %bitcast.20), custom_call_target="tpu_custom_call" | custom-call | tf_op jit(solution)/shard_map/restrict/pallas_call | solution.py:129
  7.5 0.0 copy-start.3
  7.6 0.0 copy-start.5
  7.6 0.0 copy-start.6
  7.6 7.4 %all-to-all-start = ((f32[32,72,128]{2,1,0:T(8,128)}), f32[32,72,128]{2,1,0:T(8,128)}, u32[]{:S(2)}, u32[]{:S(2)}) async-start(f32[32,72,128]{2,1,0:T(8,128)} %bitcast.3), calls=%async_computation | async-start | bytes 2359296 | tf_op jit(solution)/shard_map/all_to_all | solution.py:556
  15.0 0.0 copy-start.7
  15.0 0.0 copy-done.3
  15.1 0.0 copy-done.5
  15.1 1.6 %prepare.1 = (f32[48,48,128]{2,1,0:T(8,128)S(1)}, f32[3,48,128]{2,1,0:T(8,128)S(1)}, f32[3,48,128]{2,1,0:T(8,128)S(1)}, f32[2,48,128]{2,1,0:T(8,128)S(1)}, f32[2,48,128]{2,1,0:T(8,128)S(1)}) custom-call(f32[432,128]{1,0:T(8,128)S(1)} %bitcast.22, f32[1728,128]{1,0:T(8,128)S(1)} %bitcast.19, s32[192,128]{1,0:T(8,128)S(1)} %bitcast.23), custom_call_target="tpu_custom_call" | custom-call | tf_op jit(solution)/shard_map/prepare/pallas_call | solution.py:326
  16.7 1.3 collective-permute-start.6
  18.0 0.7 collective-permute-start.4
  18.7 0.7 collective-permute-start.7
  19.4 1.3 collective-permute-start.2
  20.7 6.2 %collective-permute-start.3 = (f32[2,48,128]{2,1,0:T(8,128)S(1)}, f32[2,48,128]{2,1,0:T(8,128)S(1)}, u32[]{:S(2)}, u32[]{:S(2)}) collective-permute-start(f32[2,48,128]{2,1,0:T(8,128)S(1)} %get-tuple-element.17), channel_id=1, source_target_pairs={{0,1},{1,2},{2,3},{4,5},{5,6},{6,7},{8,9},{9,10},{10,11},{12,13},{... | collective-permute-start | bytes 147464 | tf_op jit(solution)/shard_map/ppermute | solution.py:534
  26.9 0.0 collective-permute-done.6.after_past_ref
  26.9 8.1 %collective-permute-start.5 = (f32[1,48,128]{2,1,0:T(8,128)S(1)}, f32[1,48,128]{2,1,0:T(8,128)S(1)}, u32[]{:S(2)}, u32[]{:S(2)}) collective-permute-start(f32[1,48,128]{2,1,0:T(8,128)S(1)} %get-tuple-element.27), channel_id=1, source_target_pairs={{0,5},{1,6},{2,7},{4,9},{5,10},{6,11},{8,13},{9,14},{10,15},{12,17... | collective-permute-start | bytes 73736 | tf_op jit(solution)/shard_map/ppermute | solution.py:534
  35.0 0.0 collective-permute-done.4.before_past_ref
  35.0 4.5 %collective-permute-start = (f32[3,48,128]{2,1,0:T(8,128)S(1)}, f32[3,48,128]{2,1,0:T(8,128)S(1)}, u32[]{:S(2)}, u32[]{:S(2)}) collective-permute-start(f32[3,48,128]{2,1,0:T(8,128)S(1)} %get-tuple-element.14), channel_id=1, source_target_pairs={{0,4},{1,5},{2,6},{3,7},{4,8},{5,9},{6,10},{7,11},{8,12},{9,13},{1... | collective-permute-start | bytes 221192 | tf_op jit(solution)/shard_map/ppermute | solution.py:534
  39.5 0.0 collective-permute-done.7.after_ahead_ref
  39.5 1.3 collective-permute-start.1
  40.8 0.1 fusion.2.slot_ref
  40.9 0.0 collective-permute-done.5.before_ahead_ref
  40.9 0.0 collective-permute-done.2.past_ref
  40.9 0.0 collective-permute-done.3.ahead_ref
  40.9 0.0 collective-permute-done.before_ref
  40.9 12.3 %collective-permute-done.1.after_ref = f32[3,48,128]{2,1,0:T(8,128)S(1)} collective-permute-done((f32[3,48,128]{2,1,0:T(8,128)S(1)}, f32[3,48,128]{2,1,0:T(8,128)S(1)}, u32[]{:S(2)}, u32[]{:S(2)}) %collective-permute-start.1) | collective-permute-done | bytes 73760 | tf_op jit(solution)/shard_map/ppermute | solution.py:534
  53.2 0.7 widen.1.coef_ref
  53.9 0.0 all-to-all-done
  53.9 9.4 %collect.1.body_ref.rhs_ref = f32[48,48,128]{2,1,0:T(8,128)S(1)} custom-call(s32[6144]{0:T(1024)S(1)} %fusion.2.slot_ref, f32[2304,128]{1,0:T(8,128)} %bitcast.4.in_ref), custom_call_target="tpu_custom_call" | custom-call | tf_op jit(solution)/shard_map/collect/pallas_call | solution.py:232
  63.4 1.3 collective-permute-start.9
  64.7 5.6 %collective-permute-start.8 = (f32[3,48,128]{2,1,0:T(8,128)S(1)}, f32[3,48,128]{2,1,0:T(8,128)S(1)}, u32[]{:S(2)}, u32[]{:S(2)}) collective-permute-start(f32[3,48,128]{2,1,0:T(8,128)S(1)} %get-tuple-element.25), channel_id=1, source_target_pairs={{0,4},{4,8},{8,12},{12,16},{16,20},{20,24},{24,28},{1,5},{5,9},{9,... | collective-permute-start | bytes 221192 | tf_op jit(solution)/shard_map/ppermute | solution.py:598
  70.2 0.0 collective-permute-done.9.after_ref
  70.2 0.9 collective-permute-done.8.before_ref
  71.1 0.8 pack_edges.1
  71.9 1.3 collective-permute-start.10
  73.2 4.5 %collective-permute-start.11 = (f32[2,48,128]{2,1,0:T(8,128)S(1)}, f32[2,48,128]{2,1,0:T(8,128)S(1)}, u32[]{:S(2)}, u32[]{:S(2)}) collective-permute-start(f32[2,48,128]{2,1,0:T(8,128)S(1)} %get-tuple-element.20), channel_id=1, source_target_pairs={{0,1},{1,2},{2,3},{4,5},{5,6},{6,7},{8,9},{9,10},{10,11},{12,13},{... | collective-permute-start | bytes 147464 | tf_op jit(solution)/shard_map/ppermute | solution.py:601
  77.7 0.1 collective-permute-done.10.past_ref
  77.9 1.6 %collective-permute-done.11.ahead_ref = f32[2,48,128]{2,1,0:T(8,128)S(1)} collective-permute-done((f32[2,48,128]{2,1,0:T(8,128)S(1)}, f32[2,48,128]{2,1,0:T(8,128)S(1)}, u32[]{:S(2)}, u32[]{:S(2)}) %collective-permute-start.11) | collective-permute-done | bytes 49184 | tf_op jit(solution)/shard_map/ppermute | solution.py:601
  79.5 16.4 %sweeps.1 = (f32[48,48,128]{2,1,0:T(8,128)S(1)}, f32[2304,128]{1,0:T(8,128)S(1)}) custom-call(s32[6144]{0:T(1024)S(1)} %fusion.2.slot_ref, f32[48,48,128]{2,1,0:T(8,128)S(1)} %collect.1.body_ref.rhs_ref, f32[3,48,128]{2,1,0:T(8,128)S(1)} %collective-permute-done.8.before_ref, f32[3,48,128]{2,1,0:T(8,128)S(1)} %collective-permute-done.9.after_ref, ...), custom_call_target="tpu_custom_call" | custom-call | tf_op jit(solution)/shard_map/sweeps/pallas_call | solution.py:507
  95.9 0.0 copy-start.1
  95.9 1.0 copy-done.1
  96.9 1.0 copy-done.2
  97.9 8.5 %all-to-all-start.1 = ((f32[32,72,128]{2,1,0:T(8,128)}), f32[32,72,128]{2,1,0:T(8,128)S(1)}, u32[]{:S(2)}, u32[]{:S(2)}) async-start(f32[32,72,128]{2,1,0:T(8,128)} %bitcast.18), calls=%async_computation.1 | async-start | bytes 2359296 | tf_op jit(solution)/shard_map/all_to_all | solution.py:556
  106.4 0.0 copy-start
  106.4 2.8 %copy.11 = f32[48,3,16,128]{3,0,1,2:T(8,128)} copy(f32[48,3,16,128]{3,2,1,0:T(8,128)} %bitcast.17) | data formatting | bytes 2359296 | tf_op jit(solution)/shard_map/reshape | solution.py:604
  109.3 26.3 %all-to-all-done.1 = f32[32,72,128]{2,1,0:T(8,128)S(1)} async-done(((f32[32,72,128]{2,1,0:T(8,128)}), f32[32,72,128]{2,1,0:T(8,128)S(1)}, u32[]{:S(2)}, u32[]{:S(2)}) %all-to-all-start.1) | async-done | bytes 1179680 | tf_op jit(solution)/shard_map/all_to_all | solution.py:556
  135.5 0.9 copy-done.4
  136.4 5.0 %prolong.1 = f32[3,16,49152]{2,1,0:T(8,128)} custom-call(f32[2304,128]{1,0:T(8,128)S(1)} %bitcast.16, f32[3,3,49152]{2,1,0:T(4,128)S(1)} %copy-done, s32[1,49152]{1,0:T(1,128)S(1)} %bitcast.21), custom_call_target="tpu_custom_call" | custom-call | tf_op jit(solution)/shard_map/prolong/pallas_call | solution.py:176
  (8 shorter events, 0.0 us)
Async XLA Ops:
  7.5 7.5 %copy-start.3 = (f32[4,3,3,48,128]{4,3,2,1,0:T(8,128)S(1)}, f32[4,3,3,48,128]{4,3,2,1,0:T(8,128)}, u32[]{:S(2)}) copy-start(f32[4,3,3,48,128]{4,3,2,1,0:T(8,128)} %param.12) | copy-start | bytes 2654212
  7.6 7.5 %copy-start.5 = (f32[3,3,48,128]{3,2,1,0:T(8,128)S(1)}, f32[3,3,48,128]{3,2,1,0:T(8,128)}, u32[]{:S(2)}) copy-start(f32[3,3,48,128]{3,2,1,0:T(8,128)} %param.11) | copy-start | bytes 663556
  7.6 7.5 %copy-start.6 = (s32[4,48,128]{2,1,0:T(8,128)S(1)}, s32[4,48,128]{2,1,0:T(8,128)}, u32[]{:S(2)}) copy-start(s32[4,48,128]{2,1,0:T(8,128)} %param.13) | copy-start | bytes 294916
  7.6 46.4 %all-to-all-start = ((f32[32,72,128]{2,1,0:T(8,128)}), f32[32,72,128]{2,1,0:T(8,128)}, u32[]{:S(2)}, u32[]{:S(2)}) async-start(f32[32,72,128]{2,1,0:T(8,128)} %bitcast.3), calls=%async_computation | async-start | bytes 2359296 | tf_op jit(solution)/shard_map/all_to_all | solution.py:556
  15.0 25.8 %copy-start.7 = (s32[48,128]{1,0:T(8,128)S(1)}, s32[48,128]{1,0:T(8,128)}, u32[]{:S(2)}) copy-start(s32[48,128]{1,0:T(8,128)} %param.10) | copy-start | bytes 73732
  16.7 10.2 %collective-permute-start.6 = (f32[1,48,128]{2,1,0:T(8,128)S(1)}, f32[1,48,128]{2,1,0:T(8,128)S(1)}, u32[]{:S(2)}, u32[]{:S(2)}) collective-permute-start(f32[1,48,128]{2,1,0:T(8,128)S(1)} %get-tuple-element.28), channel_id=1, source_target_pairs={{5,0},{6,1},{7,2},{9,4},{10,5},{11,6},{13,8},{14,9},{15,10},{17,12... | collective-permute-start | bytes 73736 | tf_op jit(solution)/shard_map/ppermute | solution.py:534
  18.0 17.0 %collective-permute-start.4 = (f32[1,48,128]{2,1,0:T(8,128)S(1)}, f32[1,48,128]{2,1,0:T(8,128)S(1)}, u32[]{:S(2)}, u32[]{:S(2)}) collective-permute-start(f32[1,48,128]{2,1,0:T(8,128)S(1)} %get-tuple-element.29), channel_id=1, source_target_pairs={{1,4},{2,5},{3,6},{5,8},{6,9},{7,10},{9,12},{10,13},{11,14},{13,16... | collective-permute-start | bytes 73736 | tf_op jit(solution)/shard_map/ppermute | solution.py:534
  18.7 20.8 %collective-permute-start.7 = (f32[1,48,128]{2,1,0:T(8,128)S(1)}, f32[1,48,128]{2,1,0:T(8,128)S(1)}, u32[]{:S(2)}, u32[]{:S(2)}) collective-permute-start(f32[1,48,128]{2,1,0:T(8,128)S(1)} %get-tuple-element.26), channel_id=1, source_target_pairs={{4,1},{5,2},{6,3},{8,5},{9,6},{10,7},{12,9},{13,10},{14,11},{16,13... | collective-permute-start | bytes 73736 | tf_op jit(solution)/shard_map/ppermute | solution.py:534
  19.4 21.5 %collective-permute-start.2 = (f32[2,48,128]{2,1,0:T(8,128)S(1)}, f32[2,48,128]{2,1,0:T(8,128)S(1)}, u32[]{:S(2)}, u32[]{:S(2)}) collective-permute-start(f32[2,48,128]{2,1,0:T(8,128)S(1)} %get-tuple-element.16), channel_id=1, source_target_pairs={{1,0},{2,1},{3,2},{5,4},{6,5},{7,6},{9,8},{10,9},{11,10},{13,12},{... | collective-permute-start | bytes 147464 | tf_op jit(solution)/shard_map/ppermute | solution.py:534
  20.7 20.2 %collective-permute-start.3 = (f32[2,48,128]{2,1,0:T(8,128)S(1)}, f32[2,48,128]{2,1,0:T(8,128)S(1)}, u32[]{:S(2)}, u32[]{:S(2)}) collective-permute-start(f32[2,48,128]{2,1,0:T(8,128)S(1)} %get-tuple-element.17), channel_id=1, source_target_pairs={{0,1},{1,2},{2,3},{4,5},{5,6},{6,7},{8,9},{9,10},{10,11},{12,13},{... | collective-permute-start | bytes 147464 | tf_op jit(solution)/shard_map/ppermute | solution.py:534
  26.9 13.9 %collective-permute-start.5 = (f32[1,48,128]{2,1,0:T(8,128)S(1)}, f32[1,48,128]{2,1,0:T(8,128)S(1)}, u32[]{:S(2)}, u32[]{:S(2)}) collective-permute-start(f32[1,48,128]{2,1,0:T(8,128)S(1)} %get-tuple-element.27), channel_id=1, source_target_pairs={{0,5},{1,6},{2,7},{4,9},{5,10},{6,11},{8,13},{9,14},{10,15},{12,17... | collective-permute-start | bytes 73736 | tf_op jit(solution)/shard_map/ppermute | solution.py:534
  35.0 5.9 %collective-permute-start = (f32[3,48,128]{2,1,0:T(8,128)S(1)}, f32[3,48,128]{2,1,0:T(8,128)S(1)}, u32[]{:S(2)}, u32[]{:S(2)}) collective-permute-start(f32[3,48,128]{2,1,0:T(8,128)S(1)} %get-tuple-element.14), channel_id=1, source_target_pairs={{0,4},{1,5},{2,6},{3,7},{4,8},{5,9},{6,10},{7,11},{8,12},{9,13},{1... | collective-permute-start | bytes 221192 | tf_op jit(solution)/shard_map/ppermute | solution.py:534
  39.5 13.7 %collective-permute-start.1 = (f32[3,48,128]{2,1,0:T(8,128)S(1)}, f32[3,48,128]{2,1,0:T(8,128)S(1)}, u32[]{:S(2)}, u32[]{:S(2)}) collective-permute-start(f32[3,48,128]{2,1,0:T(8,128)S(1)} %get-tuple-element.15), channel_id=1, source_target_pairs={{4,0},{5,1},{6,2},{7,3},{8,4},{9,5},{10,6},{11,7},{12,8},{13,9},{1... | collective-permute-start | bytes 221192 | tf_op jit(solution)/shard_map/ppermute | solution.py:534
  63.4 6.9 %collective-permute-start.9 = (f32[3,48,128]{2,1,0:T(8,128)S(1)}, f32[3,48,128]{2,1,0:T(8,128)S(1)}, u32[]{:S(2)}, u32[]{:S(2)}) collective-permute-start(f32[3,48,128]{2,1,0:T(8,128)S(1)} %get-tuple-element.24), channel_id=1, source_target_pairs={{4,0},{8,4},{12,8},{16,12},{20,16},{24,20},{28,24},{5,1},{9,5},{13... | collective-permute-start | bytes 221192 | tf_op jit(solution)/shard_map/ppermute | solution.py:599
  64.7 6.5 %collective-permute-start.8 = (f32[3,48,128]{2,1,0:T(8,128)S(1)}, f32[3,48,128]{2,1,0:T(8,128)S(1)}, u32[]{:S(2)}, u32[]{:S(2)}) collective-permute-start(f32[3,48,128]{2,1,0:T(8,128)S(1)} %get-tuple-element.25), channel_id=1, source_target_pairs={{0,4},{4,8},{8,12},{12,16},{16,20},{20,24},{24,28},{1,5},{5,9},{9,... | collective-permute-start | bytes 221192 | tf_op jit(solution)/shard_map/ppermute | solution.py:598
  71.9 6.0 %collective-permute-start.10 = (f32[2,48,128]{2,1,0:T(8,128)S(1)}, f32[2,48,128]{2,1,0:T(8,128)S(1)}, u32[]{:S(2)}, u32[]{:S(2)}) collective-permute-start(f32[2,48,128]{2,1,0:T(8,128)S(1)} %get-tuple-element.19), channel_id=1, source_target_pairs={{1,0},{2,1},{3,2},{5,4},{6,5},{7,6},{9,8},{10,9},{11,10},{13,12},{... | collective-permute-start | bytes 147464 | tf_op jit(solution)/shard_map/ppermute | solution.py:602
  73.2 6.3 %collective-permute-start.11 = (f32[2,48,128]{2,1,0:T(8,128)S(1)}, f32[2,48,128]{2,1,0:T(8,128)S(1)}, u32[]{:S(2)}, u32[]{:S(2)}) collective-permute-start(f32[2,48,128]{2,1,0:T(8,128)S(1)} %get-tuple-element.20), channel_id=1, source_target_pairs={{0,1},{1,2},{2,3},{4,5},{5,6},{6,7},{8,9},{9,10},{10,11},{12,13},{... | collective-permute-start | bytes 147464 | tf_op jit(solution)/shard_map/ppermute | solution.py:601
  95.9 1.0 copy-start.1
  96.9 1.0 copy-start.2
  97.9 37.6 %all-to-all-start.1 = ((f32[32,72,128]{2,1,0:T(8,128)}), f32[32,72,128]{2,1,0:T(8,128)S(1)}, u32[]{:S(2)}, u32[]{:S(2)}) async-start(f32[32,72,128]{2,1,0:T(8,128)} %bitcast.18), calls=%async_computation.1 | async-start | bytes 2359296 | tf_op jit(solution)/shard_map/all_to_all | solution.py:556
  106.4 29.1 %copy-start = (f32[3,3,49152]{2,1,0:T(4,128)S(1)}, f32[3,3,49152]{2,1,0:T(4,128)}, u32[]{:S(2)}) copy-start(f32[3,3,49152]{2,1,0:T(4,128)} %rest_ref.1) | copy-start | bytes 5308420
  135.5 0.9 copy-start.4

commit v4 on v3

v4 whole, which is shorter than its diff:
```python
import functools
import math

import jax
import jax.numpy as jnp
from jax import lax
from jax.experimental import pallas as pl
from jax.experimental.pallas import tpu as pltpu
from jax.sharding import PartitionSpec as P

FPA = 8
ITERS = 4
LANES = 128
UNROLL = 4
AXES = ("row", "col")


def vmem_spec():
    return pl.BlockSpec(memory_space=pltpu.VMEM)


KERNEL = pltpu.CompilerParams(vmem_limit_bytes=30 * 1024 * 1024)


def in_vmem(x):
    return pltpu.with_memory_space_constraint(x, pltpu.VMEM)


def in_hbm(x):
    return pltpu.with_memory_space_constraint(x, pltpu.HBM)


def vmem_result(*shape):
    return pltpu.VMEM(shape, jnp.float32)


class Sizes:
    def __init__(self, fine, loads, rows, cols, rows_n, cols_n):
        self.devices = rows_n * cols_n
        self.rows_n, self.cols_n = rows_n, cols_n
        self.fine = fine
        self.agg = fine // FPA
        self.blocks = self.agg // LANES
        self.loads = loads
        self.rows, self.cols = rows, cols
        self.q = loads
        self.comps = 3 * self.q
        self.group = LANES // math.gcd(self.comps, LANES)
        self.groups = self.blocks // self.group
        self.tiles = self.group * self.comps // LANES
        self.low = LANES // self.devices
        self.per_peer = self.tiles * self.groups * self.low
        self.depth = ITERS - 1
        self.wide = rows + 2 * self.depth


def starts(s, grp, tile):
    for low in range(s.low):
        slot = (grp * s.tiles + tile) * s.low + low
        for first in range(0, s.devices, 8):
            yield low * s.devices + first, first * s.per_peer + slot


def pieces(s, grp):
    for member in range(s.group):
        done = 0
        while done < s.comps:
            at = member * s.comps + done
            size = min(s.comps - done, LANES - at % LANES)
            yield at // LANES, at % LANES, member, done, size
            done += size


def store_tiles(s, out_ref, rows_of):
    for grp in range(s.groups):
        rows = jnp.concatenate([rows_of(grp * s.group + member) for member in range(s.group)], axis=0)
        for tile in range(s.tiles):
            turned = rows[tile * LANES : (tile + 1) * LANES].T
            for lane, start in starts(s, grp, tile):
                out_ref[pl.ds(start, 8, stride=s.per_peer), :] = turned[lane : lane + 8]


def load_tiles(s, in_ref, take):
    for grp in range(s.groups):
        turned = []
        for tile in range(s.tiles):
            parts = [in_ref[pl.ds(start, 8, stride=s.per_peer), :] for _, start in starts(s, grp, tile)]
            turned.append(jnp.concatenate(parts, axis=0).T)
        rows = jnp.concatenate(turned, axis=0)
        for member in range(s.group):
            take(grp * s.group + member, rows[member * s.comps : (member + 1) * s.comps])


def turn(x, by):
    return pltpu.roll(x, by % LANES, 1) if by % LANES else x


def lines_from_tiles(s, in_ref, lines):
    where = lax.broadcasted_iota(jnp.int32, (8, LANES), 1)
    for grp in range(s.groups):
        runs = [dict(starts(s, grp, tile)) for tile in range(s.tiles)]
        for lane in runs[0]:
            held = [in_ref[pl.ds(run[lane], 8, stride=s.per_peer), :] for run in runs]
            made = {}
            for tile, low, member, done, size in pieces(s, grp):
                part = turn(held[tile], done - low)
                made[member] = jnp.where(where >= done, part, made[member]) if member in made else part
            for member, line in made.items():
                row = (grp * s.group + member) * LANES + lane
                lines[row : row + 8, :] = line


def tiles_from_lines(s, lines, out_ref):
    where = lax.broadcasted_iota(jnp.int32, (8, LANES), 1)
    for grp in range(s.groups):
        runs = [dict(starts(s, grp, tile)) for tile in range(s.tiles)]
        for lane in runs[0]:
            held = []
            for member in range(s.group):
                row = (grp * s.group + member) * LANES + lane
                held.append(lines[row : row + 8, :])
            made = {}
            for tile, low, member, done, size in pieces(s, grp):
                part = turn(held[member], low - done)
                made[tile] = jnp.where(where >= low, part, made[tile]) if tile in made else part
            for tile, value in made.items():
                out_ref[pl.ds(runs[tile][lane], 8, stride=s.per_peer), :] = value


def each_column(s, visit):
    def some(block, carry):
        for step in range(UNROLL):
            visit(pl.ds(pl.multiple_of((block * UNROLL + step) * LANES, LANES), LANES))
        return carry

    lax.fori_loop(0, s.blocks // UNROLL, some, 0)


def restrict_kernel(s, x_hbm, rest_hbm, pat_hbm, out_ref, x_ref, rest_ref, pat_ref, acc, sems):
    copies = []
    for part in range(FPA):
        at = pl.ds(part * s.agg, s.agg)
        group = (
            pltpu.make_async_copy(rest_hbm.at[:, :, at], rest_ref.at[part], sems.at[part, 0]),
            pltpu.make_async_copy(pat_hbm.at[:, at], pat_ref.at[part], sems.at[part, 1]),
            pltpu.make_async_copy(x_hbm.at[:, :, at], x_ref.at[part], sems.at[part, 2]),
        )
        for copy in group:
            copy.start()
        copies.append(group)

    for part in range(FPA):
        for copy in copies[part]:
            copy.wait()

        def column(at, part=part):
            mask = pat_ref[part, 0:1, at].astype(jnp.float32)
            value = [x_ref[part, comp, :, at] for comp in range(3)]
            for comp in range(3):
                total = (rest_ref[part, comp, 0:1, at] * mask) * value[0]
                for source in range(1, 3):
                    total = total + (rest_ref[part, comp, source : source + 1, at] * mask) * value[source]
                acc[comp, :, at] = total if part == 0 else acc[comp, :, at] + total

        each_column(s, column)

    def rows_of(block):
        return jnp.concatenate([acc[comp, :, block * LANES : (block + 1) * LANES] for comp in range(3)], axis=0)

    store_tiles(s, out_ref, rows_of)


def restrict(s, residual, restriction, pattern):
    return pl.pallas_call(
        functools.partial(restrict_kernel, s),
        in_specs=[pl.BlockSpec(memory_space=pltpu.HBM)] * 3,
        out_specs=vmem_spec(),
        out_shape=vmem_result(s.devices * s.per_peer, LANES),
        scratch_shapes=[
            pltpu.VMEM((FPA, 3, s.q, s.agg), jnp.float32),
            pltpu.VMEM((FPA, 3, 3, s.agg), jnp.float32),
            pltpu.VMEM((FPA, 1, s.agg), jnp.int32),
            pltpu.VMEM((3, s.q, s.agg), jnp.float32),
            pltpu.SemaphoreType.DMA((FPA, 3)),
        ],
        name="restrict",
        compiler_params=KERNEL,
    )(*map(in_hbm, (residual, restriction, pattern)))


def prolong_kernel(s, in_ref, rest_ref, pat_hbm, out_hbm, agg, out_ref, pat_ref, sems):
    fetch = pltpu.make_async_copy(pat_hbm, pat_ref, sems.at[FPA])
    fetch.start()

    def take(block, rows):
        for comp in range(3):
            agg[comp, :, block * LANES : (block + 1) * LANES] = rows[comp * s.q : (comp + 1) * s.q]

    load_tiles(s, in_ref, take)
    fetch.wait()
    copies = []
    for part in range(FPA):
        def column(at, part=part):
            there = pl.ds(pl.multiple_of(at.start + part * s.agg, LANES), LANES)
            mask = pat_ref[0:1, there].astype(jnp.float32)
            value = [agg[comp, :, at] for comp in range(3)]
            for comp in range(3):
                total = (rest_ref[0, comp : comp + 1, there] * mask) * value[0]
                for source in range(1, 3):
                    total = total + (rest_ref[source, comp : comp + 1, there] * mask) * value[source]
                out_ref[part, comp, :, at] = total

        each_column(s, column)
        copy = pltpu.make_async_copy(
            out_ref.at[part], out_hbm.at[:, :, pl.ds(part * s.agg, s.agg)], sems.at[part]
        )
        copy.start()
        copies.append(copy)
    for copy in copies:
        copy.wait()


def prolong(s, arrived, restriction, pattern):
    return pl.pallas_call(
        functools.partial(prolong_kernel, s),
        in_specs=[vmem_spec()] * 2 + [pl.BlockSpec(memory_space=pltpu.HBM)],
        out_specs=pl.BlockSpec(memory_space=pltpu.HBM),
        out_shape=jax.ShapeDtypeStruct((3, s.loads, s.fine), jnp.float32),
        scratch_shapes=[
            pltpu.VMEM((3, s.q, s.agg), jnp.float32),
            pltpu.VMEM((FPA, 3, s.q, s.agg), jnp.float32),
            pltpu.VMEM((1, s.fine), jnp.int32),
            pltpu.SemaphoreType.DMA((FPA + 1,)),
        ],
        name="prolong",
        compiler_params=KERNEL,
    )(in_vmem(arrived), in_vmem(restriction), in_hbm(pattern))


def fetch_row(slot_ref, lines, row, held):
    for lane in range(LANES):
        slot = slot_ref[row * LANES + lane]
        held[lane : lane + 1, :] = lines[pl.ds(slot, 1), :]


def edges_kernel(s, slot_ref, in_ref, coef_ref, lines, top_ref, bottom_ref, *held):
    lines_from_tiles(s, in_ref, lines)
    places = []
    for at in range(s.depth):
        places += [(at, top_ref, at), (s.rows - s.depth + at, bottom_ref, at)]
    for (row, _, _), buffer in zip(places, held):
        fetch_row(slot_ref, lines, row, buffer)
    for (row, target, at), buffer in zip(places, held):
        target[at, 0 : s.comps, :] = buffer[...].T[0 : s.comps]
        target[at, s.comps :, :] = coef_ref[row]


def edges(s, received, slots, coefs):
    edge = vmem_result(s.depth, s.comps + COEFS, LANES)
    return pl.pallas_call(
        functools.partial(edges_kernel, s),
        in_specs=[pl.BlockSpec(memory_space=pltpu.SMEM)] + [vmem_spec()] * 2,
        out_specs=[vmem_spec()] * 3,
        out_shape=[vmem_result(s.agg, LANES), edge, edge],
        scratch_shapes=[pltpu.VMEM((LANES, LANES), jnp.float32)] * (2 * s.depth),
        name="edges",
        compiler_params=KERNEL,
    )(slots, in_vmem(received), coefs)


def collect_kernel(s, slot_ref, lines, top_ref, bottom_ref, out_ref, even, odd):
    for at in range(s.depth):
        out_ref[at] = top_ref[at, 0 : s.comps]
        out_ref[s.rows - s.depth + at] = bottom_ref[at, 0 : s.comps]

    def place(row, held):
        out_ref[row] = held[...].T[0 : s.comps]

    fetch_row(slot_ref, lines, s.depth, even)
    last = s.rows - s.depth - 1

    def two(k, carry):
        row = s.depth + 2 * k
        fetch_row(slot_ref, lines, row + 1, odd)
        place(row, even)
        fetch_row(slot_ref, lines, jnp.minimum(row + 2, last), even)
        place(row + 1, odd)
        return carry

    lax.fori_loop(0, (s.rows - 2 * s.depth) // 2, two, 0)


def collect(s, slots, lines, top, bottom):
    return pl.pallas_call(
        functools.partial(collect_kernel, s),
        in_specs=[pl.BlockSpec(memory_space=pltpu.SMEM)] + [vmem_spec()] * 3,
        out_specs=vmem_spec(),
        out_shape=vmem_result(s.rows, s.comps, LANES),
        scratch_shapes=[pltpu.VMEM((LANES, LANES), jnp.float32)] * 2,
        name="collect",
        compiler_params=KERNEL,
    )(slots, lines, top, bottom)


PACK = 32
EDGE = LANES // PACK


def pack_lines(line_of, count, left_ref, right_ref, span):
    for pack in range(left_ref.shape[0]):
        left = right = None
        for member in range(min(PACK, count - pack * PACK)):
            line = line_of(pack * PACK + member)
            head = pltpu.roll(line, member * EDGE, 1) if member else line
            turn = (member + 1) * EDGE
            tail = pltpu.roll(line, turn, 1) if turn < LANES else line
            if left is None:
                here = lax.broadcasted_iota(jnp.int32, line.shape, 1) // EDGE
                left, right = head, tail
            else:
                left = jnp.where(here == member, head, left)
                right = jnp.where(here == member, tail, right)
        left_ref[pack, span, :] = left
        right_ref[pack, span, :] = right


def beyond(past, ahead, member, depth):
    if member:
        past = pltpu.roll(past, LANES - member * EDGE, 1)
    turn = (member + 1) * EDGE
    if turn < LANES:
        ahead = pltpu.roll(ahead, LANES - turn, 1)
    lane = lax.broadcasted_iota(jnp.int32, past.shape, 1)
    return jnp.where(lane < depth, past, jnp.where(lane >= LANES - depth, ahead, 0.0))


def pack_kernel(s, body_ref, coef_ref, before_ref, after_ref, left_ref, right_ref):
    for own_ref, span in ((body_ref, slice(0, s.comps)), (coef_ref, slice(s.comps, s.comps + COEFS))):
        def line_of(at, own_ref=own_ref, span=span):
            if at < s.depth:
                return before_ref[at, span, :]
            if at < s.depth + s.rows:
                return own_ref[at - s.depth]
            return after_ref[at - s.depth - s.rows, span, :]

        pack_lines(line_of, s.wide, left_ref, right_ref, span)


def pack_edges(s, body, coefs, before, after):
    packs = -(-s.wide // PACK)
    shape = vmem_result(packs, s.comps + COEFS, LANES)
    return pl.pallas_call(
        functools.partial(pack_kernel, s),
        in_specs=[vmem_spec()] * 4,
        out_specs=[vmem_spec()] * 2,
        out_shape=[shape, shape],
        name="pack_edges",
        compiler_params=KERNEL,
    )(body, coefs, in_vmem(before), in_vmem(after))


COEFS = 48


def prepare_kernel(s, inv_ref, off_ref, pat_ref, body_ref, flat):
    rows = s.rows
    flat[0 : 9 * rows, :] = inv_ref[...]
    for direction in range(4):
        mask = pat_ref[direction * rows : (direction + 1) * rows, :].astype(jnp.float32)
        for entry in range(9):
            at = direction * 9 + entry
            flat[(9 + at) * rows : (10 + at) * rows, :] = off_ref[at * rows : (at + 1) * rows, :] * mask
    flat[45 * rows : COEFS * rows, :] = jnp.zeros(((COEFS - 45) * rows, LANES), jnp.float32)

    def one(row, carry):
        for low in range(0, COEFS, 8):
            body_ref[row, low : low + 8, :] = flat[pl.ds(low * rows + row, 8, stride=rows), :]
        return carry

    lax.fori_loop(0, rows, one, 0)


def prepare(s, inverse, blocks, pattern):
    return pl.pallas_call(
        functools.partial(prepare_kernel, s),
        in_specs=[vmem_spec()] * 3,
        out_specs=vmem_spec(),
        out_shape=vmem_result(s.rows, COEFS, LANES),
        scratch_shapes=[pltpu.VMEM((COEFS * s.rows, LANES), jnp.float32)],
        name="prepare",
        compiler_params=KERNEL,
    )(inverse.reshape(-1, LANES), blocks.reshape(-1, LANES), pattern.reshape(-1, LANES))


def sweeps_kernel(
    s, slot_ref, rhs_ref, own_ref, before_ref, after_ref, past_ref, ahead_ref,
    sol_hbm, out_ref, wide, coef_ref, even, odd, sol_ref, lines, ahead_lines, behind_lines, sem,
):
    q = s.q
    halves = range(0, q, 8)
    for held, inner_ref, part in (
        (wide, rhs_ref, slice(0, s.comps)),
        (coef_ref, own_ref, slice(s.comps, s.comps + COEFS)),
    ):
        for at in range(s.wide):
            if at < s.depth:
                line = before_ref[at, part, :]
            elif at < s.depth + s.rows:
                line = inner_ref[at - s.depth]
            else:
                line = after_ref[at - s.depth - s.rows, part, :]
            pack, member = divmod(at, PACK)
            held[at, :, 0:LANES] = line
            held[at, :, LANES : 2 * LANES] = beyond(
                past_ref[pack, part, :], ahead_ref[pack, part, :], member, s.depth
            )

    lane = lax.broadcasted_iota(jnp.int32, (8, LANES), 1)
    is_first = lane == 0
    is_last = lane == LANES - 1
    columns = (slice(0, LANES), slice(LANES, 2 * LANES))

    def span(comp, low):
        return slice(comp * q + low, comp * q + low + 8)

    def invert(at, total, column):
        fresh = []
        for comp in range(3):
            value = [None] * len(halves)
            for source in range(3):
                index = comp * 3 + source
                factor = coef_ref[at, index : index + 1, column]
                for half in range(len(halves)):
                    term = factor * total[source][half]
                    value[half] = term if source == 0 else value[half] + term
            fresh.append(value)
        return fresh

    def put(target, at, fresh, column):
        for comp in range(3):
            for half, low in enumerate(halves):
                target[at, span(comp, low), column] = fresh[comp][half]

    def first(at, carry):
        for column in columns:
            total = [[wide[at, span(comp, low), column] for low in halves] for comp in range(3)]
            put(even, at, invert(at, total, column), column)
        return carry

    lax.fori_loop(0, s.wide, first, 0)

    def turned(old, at):
        west = ([], [])
        east = ([], [])
        for comp in range(3):
            for side in west + east:
                side.append([])
            for low in halves:
                here = [old[at, span(comp, low), column] for column in columns]
                up = [pltpu.roll(x, 1, 1) for x in here]
                down = [pltpu.roll(x, LANES - 1, 1) for x in here]
                for v in range(2):
                    west[v][-1].append(jnp.where(is_first, up[1 - v], up[v]))
                    east[v][-1].append(jnp.where(is_last, down[1 - v], down[v]))
        return west, east

    def sweep(old, at, count):
        west, east = turned(old, at)
        result = []
        for v in range(count):
            column = columns[v]
            pieces = []
            for where in (at - 1, at + 1):
                pieces.append([[old[where, span(comp, low), column] for low in halves] for comp in range(3)])
            pieces += [west[v], east[v]]
            total = []
            for comp in range(3):
                value = [wide[at, span(comp, low), column] for low in halves]
                for direction in range(4):
                    for source in range(3):
                        index = 9 + (direction * 3 + comp) * 3 + source
                        factor = coef_ref[at, index : index + 1, column]
                        for half in range(len(halves)):
                            value[half] = value[half] - factor * pieces[direction][source][half]
                total.append(value)
            result.append(invert(at, total, column))
        return result

    old, new = even, odd
    for inner in range(1, s.depth):
        def middle(k, carry, old=old, new=new, inner=inner):
            for step in range(2):
                at = inner + 2 * k + step
                for column, fresh in zip(columns, sweep(old, at, 2)):
                    put(new, at, fresh, column)
            return carry

        lax.fori_loop(0, (s.wide - 2 * inner) // 2, middle, 0)
        old, new = new, old

    def finish(row, held):
        (fresh,) = sweep(old, row + s.depth, 1)
        put(sol_ref, row, fresh, columns[0])
        parts = [fresh[comp][half] for comp in range(3) for half in range(len(halves))]
        held[:, 0 : s.comps] = jnp.concatenate(parts, axis=0).T

    def send(row, held):
        for column in range(LANES):
            slot = slot_ref[row * LANES + column]
            lines[pl.ds(slot, 1), :] = held[column : column + 1, :]

    finish(0, ahead_lines)
    finish(1, behind_lines)

    def two(k, carry):
        row = 2 * k
        send(row, ahead_lines)
        send(row + 1, behind_lines)
        finish(row + 2, ahead_lines)
        finish(row + 3, behind_lines)
        return carry

    lax.fori_loop(0, s.rows // 2 - 1, two, 0)
    copy = pltpu.make_async_copy(sol_ref, sol_hbm, sem)
    copy.start()
    send(s.rows - 2, ahead_lines)
    send(s.rows - 1, behind_lines)
    tiles_from_lines(s, lines, out_ref)
    copy.wait()


def sweeps(s, slots, rhs, coefs, before, after, past, ahead):
    state = pltpu.VMEM((s.wide, s.comps, 2 * LANES), jnp.float32)
    return pl.pallas_call(
        functools.partial(sweeps_kernel, s),
        in_specs=[pl.BlockSpec(memory_space=pltpu.SMEM)] + [vmem_spec()] * 6,
        out_specs=[pl.BlockSpec(memory_space=pltpu.HBM), vmem_spec()],
        out_shape=[
            jax.ShapeDtypeStruct((s.rows, s.comps, LANES), jnp.float32),
            jax.ShapeDtypeStruct((s.devices * s.per_peer, LANES), jnp.float32),
        ],
        scratch_shapes=[
            state,
            pltpu.VMEM((s.wide, COEFS, 2 * LANES), jnp.float32),
            state,
            state,
            pltpu.VMEM((s.rows, s.comps, LANES), jnp.float32),
            pltpu.VMEM((s.agg, LANES), jnp.float32),
            pltpu.VMEM((LANES, LANES), jnp.float32),
            pltpu.VMEM((LANES, LANES), jnp.float32),
            pltpu.SemaphoreType.DMA,
        ],
        name="sweeps",
        compiler_params=KERNEL,
    )(slots, rhs, coefs, *map(in_vmem, (before, after, past, ahead)))


def ring(axis):
    count = lax.axis_size(axis)
    up = [(i, i + 1) for i in range(count - 1)]
    return up, [(j, i) for i, j in up]


def exchange(s, outgoing):
    blocks = outgoing.reshape(s.devices, s.per_peer, LANES)
    moved = lax.all_to_all(blocks, AXES, split_axis=0, concat_axis=0, tiled=True)
    return moved.reshape(s.devices * s.per_peer, LANES)


def body(
    fine_residual,
    restriction,
    restriction_pattern,
    cell_aggregate,
    block_inverse,
    off_blocks,
    operator_pattern,
):
    s = Sizes(
        fine_residual.shape[2],
        fine_residual.shape[0],
        cell_aggregate.shape[0],
        cell_aggregate.shape[1],
        lax.axis_size("row"),
        lax.axis_size("col"),
    )
    residual = fine_residual.transpose(1, 0, 2)
    pattern = restriction_pattern.reshape(1, -1)

    outgoing = restrict(s, residual, restriction, pattern)
    received = exchange(s, outgoing)
    owner = cell_aggregate // s.agg
    local = cell_aggregate % s.agg
    slots = (local // s.devices * s.devices + owner).reshape(-1)
    coefs = prepare(s, block_inverse, off_blocks, operator_pattern)

    up, down = ring("row")
    lines, top, bottom = edges(s, received, slots, coefs)
    before = lax.ppermute(bottom, "row", up)
    after = lax.ppermute(top, "row", down)
    rhs = collect(s, slots, lines, top, bottom)
    left, right = pack_edges(s, rhs, coefs, before, after)
    up, down = ring("col")
    ahead = lax.ppermute(right, "col", up)
    past = lax.ppermute(left, "col", down)
    solved, outgoing = sweeps(s, slots, rhs, coefs, before, after, past, ahead)
    correction = prolong(s, exchange(s, outgoing), restriction, pattern)
    coarse = solved.reshape(s.rows, 3, s.loads, LANES).transpose(2, 1, 0, 3)
    return coarse, correction.transpose(1, 0, 2)


def solution(mesh):
    in_specs = (
        P(None, None, AXES),
        P(None, None, AXES),
        P(AXES),
        P("row", "col"),
        P(None, None, "row", "col"),
        P(None, None, None, "row", "col"),
        P(None, "row", "col"),
    )
    out_specs = (P(None, None, "row", "col"), P(None, None, AXES))
    return jax.shard_map(body, mesh=mesh, in_specs=in_specs, out_specs=out_specs, check_vma=False)
```

time: 142 us -> 127 us (0.89)
  starting transfers between devices: 52.5 us -> 22.3 us
  waiting for transfers between devices: 41.1 us -> 56.3 us
    all_to_all x2, waiting for transfers between devices: 26.3 us -> 53.5 us  [exchange(): lax.all_to_all(blocks, AXES, split_axis=0, concat_axis=0, tiled=True)]
    ppermute x12 -> x4, starting transfers between devices: 36.6 us -> 10.2 us  [the longest x1 4.55 us: body(): ahead = lax.ppermute(right, 'col', up)]
    ppermute x12 -> x4, waiting for transfers between devices: 14.9 us -> 2.84 us  [the longest x1 1.74 us: body(): ahead = lax.ppermute(right, 'col', up)]
    all_to_all x2, starting transfers between devices: 15.9 us -> 12.1 us  [exchange(): lax.all_to_all(blocks, AXES, split_axis=0, concat_axis=0, tiled=True)]
    pallas_call x1, Pallas kernels: 9.39 us -> 6.79 us  [collect(): pl.pallas_call(functools.partial(collect_kernel, s), in_specs=[pl.BlockSp...]
    pallas_call x2, Pallas kernels: 7.65 us -> 9.44 us  [the longest x1 6.91 us: restrict(): pl.pallas_call(functools.partial(restrict_kernel, s), in_specs=[pl.BlockS...]
    pallas_call x1, Pallas kernels: 16.4 us -> 18.1 us  [sweeps(): pl.pallas_call(functools.partial(sweeps_kernel, s), in_specs=[pl.BlockSpe...]
    unnamed x16 -> x12, local copies, waits for them, and re-layouts: 2.99 us -> 1.93 us
  transfers between devices with their start and end apart: 14 -> 6, of which waited for: 5 -> 4; matrix products, arithmetic and copies ran while one was open for 2% -> 2% of each run, Pallas kernels for 2% -> 6%
where the time goes in v4:
time: 127 us; the launch traced here: 126 us
  waiting for transfers between devices  56.3 us (44%)
  Pallas kernels  42.2 us (33%)
  starting transfers between devices  22.3 us (18%)
  local copies, waits for them, and re-layouts  4.75 us (4%)
    all_to_all x2, waiting for transfers between devices, exchange(): lax.all_to_all(blocks, AXES, split_axis=0, concat_axis=0, tiled=True)  53.5 us
    pallas_call x1, Pallas kernels, sweeps(): pl.pallas_call(functools.partial(sweeps_kernel, s), in_specs=[pl.BlockSpe...  18.1 us
    all_to_all x2, starting transfers between devices, exchange(): lax.all_to_all(blocks, AXES, split_axis=0, concat_axis=0, tiled=True)  12.1 us
    pallas_call x1, Pallas kernels, restrict(): pl.pallas_call(functools.partial(restrict_kernel, s), in_specs=[pl.BlockS...  6.91 us
    pallas_call x1, Pallas kernels, collect(): pl.pallas_call(functools.partial(collect_kernel, s), in_specs=[pl.BlockSp...  6.79 us
    pallas_call x1, Pallas kernels, prolong(): pl.pallas_call(functools.partial(prolong_kernel, s), in_specs=[vmem_spec(...  5.5 us
    ppermute x1, starting transfers between devices, body(): ahead = lax.ppermute(right, 'col', up)  4.55 us
    ppermute x1, starting transfers between devices, body(): before = lax.ppermute(bottom, 'row', up)  3.04 us
  transfers between devices with their start and end apart: 6, of which 4 were waited for; matrix products, arithmetic and copies ran while one was open for 2% of the time, Pallas kernels for 6%

profile of v4, /device:TPU:0, one launch (start us, length us, event | category | flops | bytes accessed | tf_op | source)
XLA Modules:
  0.0 126.4 jit_solution(11098937970934292527)
XLA Ops:
  0.6 6.9 %restrict.1 = f32[2304,128]{1,0:T(8,128)} custom-call(f32[3,16,49152]{2,1,0:T(8,128)} %bitcast.22, f32[3,3,49152]{2,1,0:T(4,128)} %rest_ref.1, s32[1,49152]{1,0:T(1,128)} %bitcast.25), custom_call_target="tpu_custom_call" | custom-call | tf_op jit(solution)/shard_map/restrict/pallas_call | solution.py:174
  7.5 0.0 copy-start.2
  7.6 0.0 copy-start.3
  7.6 7.3 %all-to-all-start = ((f32[32,72,128]{2,1,0:T(8,128)}), f32[32,72,128]{2,1,0:T(8,128)S(1)}, u32[]{:S(2)}, u32[]{:S(2)}) async-start(f32[32,72,128]{2,1,0:T(8,128)} %bitcast.3), calls=%async_computation | async-start | bytes 2359296 | tf_op jit(solution)/shard_map/all_to_all | solution.py:566
  14.9 0.0 copy-done.2
  14.9 0.0 copy-done.3
  14.9 0.0 copy-start.4
  14.9 0.9 copy-done.4
  15.8 0.0 copy-start.5
  15.8 0.9 prepare.1.coef_ref.own_ref
  16.7 0.0 copy-done.5
  16.8 27.2 %all-to-all-done = f32[32,72,128]{2,1,0:T(8,128)S(1)} async-done(((f32[32,72,128]{2,1,0:T(8,128)}), f32[32,72,128]{2,1,0:T(8,128)S(1)}, u32[]{:S(2)}, u32[]{:S(2)}) %all-to-all-start) | async-done | bytes 1179680 | tf_op jit(solution)/shard_map/all_to_all | solution.py:566
  44.0 2.5 %edges.1 = (f32[6144,128]{1,0:T(8,128)S(1)}, f32[3,96,128]{2,1,0:T(8,128)S(1)}, f32[3,96,128]{2,1,0:T(8,128)S(1)}) custom-call(s32[6144]{0:T(1024)S(1)} %fusion.3.slot_ref, f32[2304,128]{1,0:T(8,128)S(1)} %bitcast.17, f32[48,48,128]{2,1,0:T(8,128)S(1)} %prepare.1.coef_ref.own_ref), custom_call_target="tpu_custom_call" | custom-call | tf_op jit(solution)/shard_map/edges/pallas_call | solution.py:260
  46.5 1.3 %collective-permute-start.1 = (f32[3,96,128]{2,1,0:T(8,128)S(1)}, f32[3,96,128]{2,1,0:T(8,128)S(1)}, u32[]{:S(2)}, u32[]{:S(2)}) collective-permute-start(f32[3,96,128]{2,1,0:T(8,128)S(1)} %get-tuple-element.10.top_ref), channel_id=1, source_target_pairs={{4,0},{8,4},{12,8},{16,12},{20,16},{24,20},{28,24},{5,1},{9,5},{13... | collective-permute-start | bytes 442376 | tf_op jit(solution)/shard_map/ppermute | solution.py:600
  47.8 3.0 %collective-permute-start = (f32[3,96,128]{2,1,0:T(8,128)S(1)}, f32[3,96,128]{2,1,0:T(8,128)S(1)}, u32[]{:S(2)}, u32[]{:S(2)}) collective-permute-start(f32[3,96,128]{2,1,0:T(8,128)S(1)} %get-tuple-element.11.bottom_ref), channel_id=1, source_target_pairs={{0,4},{4,8},{8,12},{12,16},{16,20},{20,24},{24,28},{1,5},{5,9},{9,... | collective-permute-start | bytes 442376 | tf_op jit(solution)/shard_map/ppermute | solution.py:599
  50.9 6.8 %collect.1.body_ref.rhs_ref = f32[48,48,128]{2,1,0:T(8,128)S(1)} custom-call(s32[6144]{0:T(1024)S(1)} %fusion.3.slot_ref, f32[6144,128]{1,0:T(8,128)S(1)} %get-tuple-element.9.lines, f32[3,96,128]{2,1,0:T(8,128)S(1)} %get-tuple-element.10.top_ref, f32[3,96,128]{2,1,0:T(8,128)S(1)} %get-tuple-element.11.bottom_ref), custom_call_target="tpu_custom_call" | custom-call | tf_op jit(solution)/shard_map/collect/pallas_call | solution.py:294
  57.7 0.0 collective-permute-done.1.after_ref
  57.7 0.0 collective-permute-done.before_ref
  57.7 1.5 %pack_edges.1 = (f32[2,96,128]{2,1,0:T(8,128)S(1)}, f32[2,96,128]{2,1,0:T(8,128)S(1)}) custom-call(f32[48,48,128]{2,1,0:T(8,128)S(1)} %collect.1.body_ref.rhs_ref, f32[48,48,128]{2,1,0:T(8,128)S(1)} %prepare.1.coef_ref.own_ref, f32[3,96,128]{2,1,0:T(8,128)S(1)} %collective-permute-done.before_ref, f32[3,96,128]{2,1,0:T(8,128)S(1)} %collective-permute-done.1.after_ref), custom_call_target="tpu_custom_call" | custom-call | tf_op jit(solution)/shard_map/pack_edges/pallas_call | solution.py:352
  59.2 1.3 %collective-permute-start.2 = (f32[2,96,128]{2,1,0:T(8,128)S(1)}, f32[2,96,128]{2,1,0:T(8,128)S(1)}, u32[]{:S(2)}, u32[]{:S(2)}) collective-permute-start(f32[2,96,128]{2,1,0:T(8,128)S(1)} %get-tuple-element.12), channel_id=1, source_target_pairs={{1,0},{2,1},{3,2},{5,4},{6,5},{7,6},{9,8},{10,9},{11,10},{13,12},{... | collective-permute-start | bytes 294920 | tf_op jit(solution)/shard_map/ppermute | solution.py:605
  60.5 4.6 %collective-permute-start.3 = (f32[2,96,128]{2,1,0:T(8,128)S(1)}, f32[2,96,128]{2,1,0:T(8,128)S(1)}, u32[]{:S(2)}, u32[]{:S(2)}) collective-permute-start(f32[2,96,128]{2,1,0:T(8,128)S(1)} %get-tuple-element.13), channel_id=1, source_target_pairs={{0,1},{1,2},{2,3},{4,5},{5,6},{6,7},{8,9},{9,10},{10,11},{12,13},{... | collective-permute-start | bytes 294920 | tf_op jit(solution)/shard_map/ppermute | solution.py:604
  65.0 1.1 collective-permute-done.2.past_ref
  66.1 1.7 %collective-permute-done.3.ahead_ref = f32[2,96,128]{2,1,0:T(8,128)S(1)} collective-permute-done((f32[2,96,128]{2,1,0:T(8,128)S(1)}, f32[2,96,128]{2,1,0:T(8,128)S(1)}, u32[]{:S(2)}, u32[]{:S(2)}) %collective-permute-start.3) | collective-permute-done | bytes 98336 | tf_op jit(solution)/shard_map/ppermute | solution.py:604
  67.9 18.1 %sweeps.1 = (f32[48,48,128]{2,1,0:T(8,128)S(1)}, f32[2304,128]{1,0:T(8,128)}) custom-call(s32[6144]{0:T(1024)S(1)} %fusion.3.slot_ref, f32[48,48,128]{2,1,0:T(8,128)S(1)} %collect.1.body_ref.rhs_ref, f32[48,48,128]{2,1,0:T(8,128)S(1)} %prepare.1.coef_ref.own_ref, f32[3,96,128]{2,1,0:T(8,128)S(1)} %collective-permute-done.before_ref, ...), custom_call_target="tpu_custom_call" | custom-call | tf_op jit(solution)/shard_map/sweeps/pallas_call | solution.py:534
  86.0 0.0 copy-start.1
  86.0 1.0 copy-done.1
  87.0 4.8 %all-to-all-start.1 = ((f32[32,72,128]{2,1,0:T(8,128)}), f32[32,72,128]{2,1,0:T(8,128)S(1)}, u32[]{:S(2)}, u32[]{:S(2)}) async-start(f32[32,72,128]{2,1,0:T(8,128)} %bitcast.10), calls=%async_computation.1 | async-start | bytes 2359296 | tf_op jit(solution)/shard_map/all_to_all | solution.py:566
  91.8 0.0 copy-start
  91.8 2.8 %copy.11 = f32[48,3,16,128]{3,0,1,2:T(8,128)} copy(f32[48,3,16,128]{3,2,1,0:T(8,128)} %bitcast.18) | data formatting | bytes 2359296 | tf_op jit(solution)/shard_map/reshape | solution.py:608
  94.6 26.3 %all-to-all-done.1 = f32[32,72,128]{2,1,0:T(8,128)S(1)} async-done(((f32[32,72,128]{2,1,0:T(8,128)}), f32[32,72,128]{2,1,0:T(8,128)S(1)}, u32[]{:S(2)}, u32[]{:S(2)}) %all-to-all-start.1) | async-done | bytes 1179680 | tf_op jit(solution)/shard_map/all_to_all | solution.py:566
  120.9 0.0 copy-done
  120.9 5.5 %prolong.1 = f32[3,16,49152]{2,1,0:T(8,128)} custom-call(f32[2304,128]{1,0:T(8,128)S(1)} %bitcast.16, f32[3,3,49152]{2,1,0:T(4,128)S(1)} %copy-done, s32[1,49152]{1,0:T(1,128)} %bitcast.26), custom_call_target="tpu_custom_call" | custom-call | tf_op jit(solution)/shard_map/prolong/pallas_call | solution.py:224
  (1 shorter events, 0.0 us)
Async XLA Ops:
  7.5 7.4 %copy-start.2 = (f32[4,3,3,48,128]{4,3,2,1,0:T(8,128)S(1)}, f32[4,3,3,48,128]{4,3,2,1,0:T(8,128)}, u32[]{:S(2)}) copy-start(f32[4,3,3,48,128]{4,3,2,1,0:T(8,128)} %param.12) | copy-start | bytes 2654212
  7.6 7.4 %copy-start.3 = (f32[3,3,48,128]{3,2,1,0:T(8,128)S(1)}, f32[3,3,48,128]{3,2,1,0:T(8,128)}, u32[]{:S(2)}) copy-start(f32[3,3,48,128]{3,2,1,0:T(8,128)} %param.11) | copy-start | bytes 663556
  7.6 36.4 %all-to-all-start = ((f32[32,72,128]{2,1,0:T(8,128)}), f32[32,72,128]{2,1,0:T(8,128)S(1)}, u32[]{:S(2)}, u32[]{:S(2)}) async-start(f32[32,72,128]{2,1,0:T(8,128)} %bitcast.3), calls=%async_computation | async-start | bytes 2359296 | tf_op jit(solution)/shard_map/all_to_all | solution.py:566
  14.9 0.9 copy-start.4
  15.8 0.9 copy-start.5
  46.5 11.1 %collective-permute-start.1 = (f32[3,96,128]{2,1,0:T(8,128)S(1)}, f32[3,96,128]{2,1,0:T(8,128)S(1)}, u32[]{:S(2)}, u32[]{:S(2)}) collective-permute-start(f32[3,96,128]{2,1,0:T(8,128)S(1)} %get-tuple-element.10.top_ref), channel_id=1, source_target_pairs={{4,0},{8,4},{12,8},{16,12},{20,16},{24,20},{28,24},{5,1},{9,5},{13... | collective-permute-start | bytes 442376 | tf_op jit(solution)/shard_map/ppermute | solution.py:600
  47.8 9.8 %collective-permute-start = (f32[3,96,128]{2,1,0:T(8,128)S(1)}, f32[3,96,128]{2,1,0:T(8,128)S(1)}, u32[]{:S(2)}, u32[]{:S(2)}) collective-permute-start(f32[3,96,128]{2,1,0:T(8,128)S(1)} %get-tuple-element.11.bottom_ref), channel_id=1, source_target_pairs={{0,4},{4,8},{8,12},{12,16},{16,20},{20,24},{24,28},{1,5},{5,9},{9,... | collective-permute-start | bytes 442376 | tf_op jit(solution)/shard_map/ppermute | solution.py:599
  59.2 6.9 %collective-permute-start.2 = (f32[2,96,128]{2,1,0:T(8,128)S(1)}, f32[2,96,128]{2,1,0:T(8,128)S(1)}, u32[]{:S(2)}, u32[]{:S(2)}) collective-permute-start(f32[2,96,128]{2,1,0:T(8,128)S(1)} %get-tuple-element.12), channel_id=1, source_target_pairs={{1,0},{2,1},{3,2},{5,4},{6,5},{7,6},{9,8},{10,9},{11,10},{13,12},{... | collective-permute-start | bytes 294920 | tf_op jit(solution)/shard_map/ppermute | solution.py:605
  60.5 7.4 %collective-permute-start.3 = (f32[2,96,128]{2,1,0:T(8,128)S(1)}, f32[2,96,128]{2,1,0:T(8,128)S(1)}, u32[]{:S(2)}, u32[]{:S(2)}) collective-permute-start(f32[2,96,128]{2,1,0:T(8,128)S(1)} %get-tuple-element.13), channel_id=1, source_target_pairs={{0,1},{1,2},{2,3},{4,5},{5,6},{6,7},{8,9},{9,10},{10,11},{12,13},{... | collective-permute-start | bytes 294920 | tf_op jit(solution)/shard_map/ppermute | solution.py:604
  86.0 1.0 copy-start.1
  87.0 33.8 %all-to-all-start.1 = ((f32[32,72,128]{2,1,0:T(8,128)}), f32[32,72,128]{2,1,0:T(8,128)S(1)}, u32[]{:S(2)}, u32[]{:S(2)}) async-start(f32[32,72,128]{2,1,0:T(8,128)} %bitcast.10), calls=%async_computation.1 | async-start | bytes 2359296 | tf_op jit(solution)/shard_map/all_to_all | solution.py:566
  91.8 29.1 %copy-start = (f32[3,3,49152]{2,1,0:T(4,128)S(1)}, f32[3,3,49152]{2,1,0:T(4,128)}, u32[]{:S(2)}) copy-start(f32[3,3,49152]{2,1,0:T(4,128)} %rest_ref.1) | copy-start | bytes 5308420

commit v5 on v4

--- a/solution.py
+++ b/solution.py
@@ -127,6 +127,10 @@
                 out_ref[pl.ds(runs[tile][lane], 8, stride=s.per_peer), :] = value
 
 
+def spread(row):
+    return jnp.broadcast_to(row, (8, LANES))
+
+
 def each_column(s, visit):
     def some(block, carry):
         for step in range(UNROLL):
@@ -154,13 +158,15 @@
             copy.wait()
 
         def column(at, part=part):
-            mask = pat_ref[part, 0:1, at].astype(jnp.float32)
-            value = [x_ref[part, comp, :, at] for comp in range(3)]
+            mask = spread(pat_ref[part, 0:1, at]).astype(jnp.float32)
             for comp in range(3):
-                total = (rest_ref[part, comp, 0:1, at] * mask) * value[0]
-                for source in range(1, 3):
-                    total = total + (rest_ref[part, comp, source : source + 1, at] * mask) * value[source]
-                acc[comp, :, at] = total if part == 0 else acc[comp, :, at] + total
+                factor = [spread(rest_ref[part, comp, k : k + 1, at]) * mask for k in range(3)]
+                for low in range(0, s.q, 8):
+                    loads = slice(low, low + 8)
+                    total = factor[0] * x_ref[part, 0, loads, at]
+                    for source in range(1, 3):
+                        total = total + factor[source] * x_ref[part, source, loads, at]
+                    acc[comp, loads, at] = total if part == 0 else acc[comp, loads, at] + total
 
         each_column(s, column)
 
@@ -202,13 +208,15 @@
     for part in range(FPA):
         def column(at, part=part):
             there = pl.ds(pl.multiple_of(at.start + part * s.agg, LANES), LANES)
-            mask = pat_ref[0:1, there].astype(jnp.float32)
-            value = [agg[comp, :, at] for comp in range(3)]
+            mask = spread(pat_ref[0:1, there]).astype(jnp.float32)
             for comp in range(3):
-                total = (rest_ref[0, comp : comp + 1, there] * mask) * value[0]
-                for source in range(1, 3):
-                    total = total + (rest_ref[source, comp : comp + 1, there] * mask) * value[source]
-                out_ref[part, comp, :, at] = total
+                factor = [spread(rest_ref[k, comp : comp + 1, there]) * mask for k in range(3)]
+                for low in range(0, s.q, 8):
+                    loads = slice(low, low + 8)
+                    total = factor[0] * agg[0, loads, at]
+                    for source in range(1, 3):
+                        total = total + factor[source] * agg[source, loads, at]
+                    out_ref[part, comp, loads, at] = total
 
         each_column(s, column)
         copy = pltpu.make_async_copy(
@@ -239,7 +247,7 @@
 
 def fetch_row(slot_ref, lines, row, held):
     for lane in range(LANES):
-        slot = slot_ref[row * LANES + lane]
+        slot = slot_ref[row, lane]
         held[lane : lane + 1, :] = lines[pl.ds(slot, 1), :]
 
 
@@ -306,20 +314,21 @@
 EDGE = LANES // PACK
 
 
-def pack_lines(line_of, count, left_ref, right_ref, span):
+def pack_lines(line_of, count, left_ref, right_ref, span, start=None):
     for pack in range(left_ref.shape[0]):
-        left = right = None
+        left, right = (None, None) if start is None else (start[0][pack], start[1][pack])
         for member in range(min(PACK, count - pack * PACK)):
             line = line_of(pack * PACK + member)
-            head = pltpu.roll(line, member * EDGE, 1) if member else line
-            turn = (member + 1) * EDGE
-            tail = pltpu.roll(line, turn, 1) if turn < LANES else line
+            if line is None:
+                continue
+            by = (member + 1) * EDGE
+            head, tail = turn(line, by - EDGE), turn(line, by)
             if left is None:
-                here = lax.broadcasted_iota(jnp.int32, line.shape, 1) // EDGE
                 left, right = head, tail
             else:
-                left = jnp.where(here == member, head, left)
-                right = jnp.where(here == member, tail, right)
+                here = lax.broadcasted_iota(jnp.int32, line.shape, 1) // EDGE == member
+                left = jnp.where(here, head, left)
+                right = jnp.where(here, tail, right)
         left_ref[pack, span, :] = left
         right_ref[pack, span, :] = right
 
@@ -334,35 +343,36 @@
     return jnp.where(lane < depth, past, jnp.where(lane >= LANES - depth, ahead, 0.0))
 
 
-def pack_kernel(s, body_ref, coef_ref, before_ref, after_ref, left_ref, right_ref):
-    for own_ref, span in ((body_ref, slice(0, s.comps)), (coef_ref, slice(s.comps, s.comps + COEFS))):
-        def line_of(at, own_ref=own_ref, span=span):
-            if at < s.depth:
-                return before_ref[at, span, :]
-            if at < s.depth + s.rows:
-                return own_ref[at - s.depth]
-            return after_ref[at - s.depth - s.rows, span, :]
-
-        pack_lines(line_of, s.wide, left_ref, right_ref, span)
-
-
-def pack_edges(s, body, coefs, before, after):
-    packs = -(-s.wide // PACK)
-    shape = vmem_result(packs, s.comps + COEFS, LANES)
+def pack_kernel(s, body_ref, left_coef_ref, right_coef_ref, before_ref, after_ref, left_ref, right_ref):
+    def line_of(at, own_ref, span):
+        if at < s.depth:
+            return before_ref[at, span, :]
+        if at < s.depth + s.rows:
+            return None if own_ref is None else own_ref[at - s.depth]
+        return after_ref[at - s.depth - s.rows, span, :]
+
+    loads, coefs = slice(0, s.comps), slice(s.comps, s.comps + COEFS)
+    pack_lines(lambda at: line_of(at, body_ref, loads), s.wide, left_ref, right_ref, loads)
+    start = (left_coef_ref, right_coef_ref)
+    pack_lines(lambda at: line_of(at, None, coefs), s.wide, left_ref, right_ref, coefs, start)
+
+
+def pack_edges(s, body, packs, before, after):
+    shape = vmem_result(-(-s.wide // PACK), s.comps + COEFS, LANES)
     return pl.pallas_call(
         functools.partial(pack_kernel, s),
-        in_specs=[vmem_spec()] * 4,
+        in_specs=[vmem_spec()] * 5,
         out_specs=[vmem_spec()] * 2,
         out_shape=[shape, shape],
         name="pack_edges",
         compiler_params=KERNEL,
-    )(body, coefs, in_vmem(before), in_vmem(after))
+    )(body, *packs, in_vmem(before), in_vmem(after))
 
 
 COEFS = 48
 
 
-def prepare_kernel(s, inv_ref, off_ref, pat_ref, body_ref, flat):
+def prepare_kernel(s, inv_ref, off_ref, pat_ref, body_ref, left_ref, right_ref, flat):
     rows = s.rows
     flat[0 : 9 * rows, :] = inv_ref[...]
     for direction in range(4):
@@ -379,13 +389,18 @@
 
     lax.fori_loop(0, rows, one, 0)
 
+    def line_of(at):
+        return body_ref[at - s.depth] if s.depth <= at < s.depth + rows else None
+
+    pack_lines(line_of, s.wide, left_ref, right_ref, slice(0, COEFS))
+
 
 def prepare(s, inverse, blocks, pattern):
     return pl.pallas_call(
         functools.partial(prepare_kernel, s),
         in_specs=[vmem_spec()] * 3,
-        out_specs=vmem_spec(),
-        out_shape=vmem_result(s.rows, COEFS, LANES),
+        out_specs=[vmem_spec()] * 3,
+        out_shape=[vmem_result(s.rows, COEFS, LANES)] + [vmem_result(-(-s.wide // PACK), COEFS, LANES)] * 2,
         scratch_shapes=[pltpu.VMEM((COEFS * s.rows, LANES), jnp.float32)],
         name="prepare",
         compiler_params=KERNEL,
@@ -393,27 +408,32 @@
 
 
 def sweeps_kernel(
-    s, slot_ref, rhs_ref, own_ref, before_ref, after_ref, past_ref, ahead_ref,
+    s, slot_ref, inside_ref, rhs_ref, own_ref, before_ref, after_ref, past_ref, ahead_ref,
     sol_hbm, out_ref, wide, coef_ref, even, odd, sol_ref, lines, ahead_lines, behind_lines, sem,
 ):
     q = s.q
     halves = range(0, q, 8)
+    lane = lax.broadcasted_iota(jnp.int32, (COEFS, LANES), 1)
+    side = jnp.where(lane < LANES // 2, inside_ref[3], inside_ref[2])
     for held, inner_ref, part in (
         (wide, rhs_ref, slice(0, s.comps)),
         (coef_ref, own_ref, slice(s.comps, s.comps + COEFS)),
     ):
         for at in range(s.wide):
             if at < s.depth:
-                line = before_ref[at, part, :]
+                line, inside = before_ref[at, part, :], inside_ref[0]
             elif at < s.depth + s.rows:
-                line = inner_ref[at - s.depth]
+                line, inside = inner_ref[at - s.depth], None
             else:
-                line = after_ref[at - s.depth - s.rows, part, :]
+                line, inside = after_ref[at - s.depth - s.rows, part, :], inside_ref[1]
             pack, member = divmod(at, PACK)
+            other = beyond(past_ref[pack, part, :], ahead_ref[pack, part, :], member, s.depth)
+            if held is coef_ref:
+                other = other * side
+                if inside is not None:
+                    line, other = line * inside, other * inside
             held[at, :, 0:LANES] = line
-            held[at, :, LANES : 2 * LANES] = beyond(
-                past_ref[pack, part, :], ahead_ref[pack, part, :], member, s.depth
-            )
+            held[at, :, LANES : 2 * LANES] = other
 
     lane = lax.broadcasted_iota(jnp.int32, (8, LANES), 1)
     is_first = lane == 0
@@ -506,7 +526,7 @@
 
     def send(row, held):
         for column in range(LANES):
-            slot = slot_ref[row * LANES + column]
+            slot = slot_ref[row, column]
             lines[pl.ds(slot, 1), :] = held[column : column + 1, :]
 
     finish(0, ahead_lines)
@@ -529,14 +549,14 @@
     copy.wait()
 
 
-def sweeps(s, slots, rhs, coefs, before, after, past, ahead):
+def sweeps(s, slots, inside, rhs, coefs, before, after, past, ahead):
     state = pltpu.VMEM((s.wide, s.comps, 2 * LANES), jnp.float32)
     return pl.pallas_call(
         functools.partial(sweeps_kernel, s),
-        in_specs=[pl.BlockSpec(memory_space=pltpu.SMEM)] + [vmem_spec()] * 6,
+        in_specs=[pl.BlockSpec(memory_space=pltpu.SMEM)] * 2 + [vmem_spec()] * 6,
         out_specs=[pl.BlockSpec(memory_space=pltpu.HBM), vmem_spec()],
         out_shape=[
-            jax.ShapeDtypeStruct((s.rows, s.comps, LANES), jnp.float32),
+            pltpu.HBM((s.rows, s.comps, LANES), jnp.float32),
             jax.ShapeDtypeStruct((s.devices * s.per_peer, LANES), jnp.float32),
         ],
         scratch_shapes=[
@@ -552,12 +572,12 @@
         ],
         name="sweeps",
         compiler_params=KERNEL,
-    )(slots, rhs, coefs, *map(in_vmem, (before, after, past, ahead)))
+    )(slots, inside, rhs, coefs, *map(in_vmem, (before, after, past, ahead)))
 
 
 def ring(axis):
     count = lax.axis_size(axis)
-    up = [(i, i + 1) for i in range(count - 1)]
+    up = [(i, (i + 1) % count) for i in range(count)]
     return up, [(j, i) for i, j in up]
 
 
@@ -591,19 +611,25 @@
     received = exchange(s, outgoing)
     owner = cell_aggregate // s.agg
     local = cell_aggregate % s.agg
-    slots = (local // s.devices * s.devices + owner).reshape(-1)
-    coefs = prepare(s, block_inverse, off_blocks, operator_pattern)
+    slots = local // s.devices * s.devices + owner
+    coefs, *packs = prepare(s, block_inverse, off_blocks, operator_pattern)
+
+    ends = []
+    for axis in AXES:
+        here = lax.axis_index(axis)
+        ends += [here > 0, here < lax.axis_size(axis) - 1]
+    inside = jnp.stack(ends).astype(jnp.float32)
 
     up, down = ring("row")
     lines, top, bottom = edges(s, received, slots, coefs)
     before = lax.ppermute(bottom, "row", up)
     after = lax.ppermute(top, "row", down)
     rhs = collect(s, slots, lines, top, bottom)
-    left, right = pack_edges(s, rhs, coefs, before, after)
+    left, right = pack_edges(s, rhs, packs, before, after)
     up, down = ring("col")
     ahead = lax.ppermute(right, "col", up)
     past = lax.ppermute(left, "col", down)
-    solved, outgoing = sweeps(s, slots, rhs, coefs, before, after, past, ahead)
+    solved, outgoing = sweeps(s, slots, inside, rhs, coefs, before, after, past, ahead)
     correction = prolong(s, exchange(s, outgoing), restriction, pattern)
     coarse = solved.reshape(s.rows, 3, s.loads, LANES).transpose(2, 1, 0, 3)
     return coarse, correction.transpose(1, 0, 2)

time: 127 us -> 123 us (0.969)
  starting transfers between devices: 22.3 us -> 13.5 us
  local copies, waits for them, and re-layouts: 4.75 us -> 7.88 us
  waiting for transfers between devices: 56.3 us -> 58.3 us
    ppermute x1, starting transfers between devices: 4.55 us -> 0.01 us  [body(): ahead = lax.ppermute(right, 'col', up)]
    unnamed x12 -> x18, local copies, waits for them, and re-layouts: 1.93 us -> 5.07 us
    ppermute x1, starting transfers between devices: 3.04 us -> 0.01 us  [body(): before = lax.ppermute(bottom, 'row', up)]
    all_to_all x2, starting transfers between devices: 12.1 us -> 10 us  [exchange(): lax.all_to_all(blocks, AXES, split_axis=0, concat_axis=0, tiled=True)]
    ppermute x1, waiting for transfers between devices: 1.09 us -> 3.11 us  [body(): past = lax.ppermute(left, 'col', down)]
    ppermute x1, starting transfers between devices: 1.29 us -> 2.68 us  [body(): past = lax.ppermute(left, 'col', down)]
    ppermute x1, waiting for transfers between devices: 1.74 us -> 3.12 us  [body(): ahead = lax.ppermute(right, 'col', up)]
    all_to_all x2, waiting for transfers between devices: 53.5 us -> 52.1 us  [exchange(): lax.all_to_all(blocks, AXES, split_axis=0, concat_axis=0, tiled=True)]
  transfers between devices with their start and end apart: 6 -> 6, of which waited for: 4 -> 4; matrix products, arithmetic and copies ran while one was open for 2% -> 2% of each run, Pallas kernels for 6% -> 7%
where the time goes in v5:
time: 123 us; the launch traced here: 122 us
  waiting for transfers between devices  58.3 us (47%)
  Pallas kernels  41.7 us (34%)
  starting transfers between devices  13.5 us (11%)
  local copies, waits for them, and re-layouts  7.88 us (6%)
    all_to_all x2, waiting for transfers between devices, exchange(): lax.all_to_all(blocks, AXES, split_axis=0, concat_axis=0, tiled=True)  52.1 us
    pallas_call x1, Pallas kernels, sweeps(): pl.pallas_call(functools.partial(sweeps_kernel, s), in_specs=[pl.BlockSpe...  18.1 us
    all_to_all x2, starting transfers between devices, exchange(): lax.all_to_all(blocks, AXES, split_axis=0, concat_axis=0, tiled=True)  10 us
    pallas_call x1, Pallas kernels, collect(): pl.pallas_call(functools.partial(collect_kernel, s), in_specs=[pl.BlockSp...  6.79 us
    pallas_call x1, Pallas kernels, restrict(): pl.pallas_call(functools.partial(restrict_kernel, s), in_specs=[pl.BlockS...  6.65 us
    pallas_call x1, Pallas kernels, prolong(): pl.pallas_call(functools.partial(prolong_kernel, s), in_specs=[vmem_spec(...  5.14 us
    unnamed x18, local copies, waits for them, and re-layouts  5.07 us
    ppermute x1, waiting for transfers between devices, body(): ahead = lax.ppermute(right, 'col', up)  3.12 us
  transfers between devices with their start and end apart: 6, of which 4 were waited for; matrix products, arithmetic and copies ran while one was open for 2% of the time, Pallas kernels for 7%

profile of v5, /device:TPU:0, one launch (start us, length us, event | category | flops | bytes accessed | tf_op | source)
XLA Modules:
  0.0 122.3 jit_solution(16127155232484450806)
XLA Ops:
  0.6 6.6 %restrict.1 = f32[2304,128]{1,0:T(8,128)} custom-call(f32[3,16,49152]{2,1,0:T(8,128)} %bitcast.23, f32[3,3,49152]{2,1,0:T(4,128)} %rest_ref.1, s32[1,49152]{1,0:T(1,128)} %bitcast.27), custom_call_target="tpu_custom_call" | custom-call | tf_op jit(solution)/shard_map/restrict/pallas_call | solution.py:180
  7.3 0.0 copy-start.3
  7.3 0.0 copy-start.4
  7.3 0.0 copy-start.8
  7.3 7.3 %all-to-all-start = ((f32[32,72,128]{2,1,0:T(8,128)}), f32[32,72,128]{2,1,0:T(8,128)S(1)}, u32[]{:S(2)}, u32[]{:S(2)}) async-start(f32[32,72,128]{2,1,0:T(8,128)} %bitcast.6), calls=%async_computation | async-start | bytes 2359296 | tf_op jit(solution)/shard_map/all_to_all | solution.py:586
  14.7 0.0 copy-done.3
  14.7 0.0 copy-done.4
  14.7 0.0 copy-start.5
  14.7 0.9 copy-done.5
  15.6 1.6 %prepare.1 = (f32[48,48,128]{2,1,0:T(8,128)S(1)}, f32[2,48,128]{2,1,0:T(8,128)S(1)}, f32[2,48,128]{2,1,0:T(8,128)S(1)}) custom-call(f32[432,128]{1,0:T(8,128)S(1)} %bitcast.21, f32[1728,128]{1,0:T(8,128)S(1)} %bitcast.20, s32[192,128]{1,0:T(8,128)S(1)} %bitcast.22), custom_call_target="tpu_custom_call" | custom-call | tf_op jit(solution)/shard_map/prepare/pallas_call | solution.py:399
  17.2 0.0 copy-start.6
  17.2 0.6 copy-done.6
  17.8 0.0 copy-done.8
  17.9 25.9 %all-to-all-done = f32[32,72,128]{2,1,0:T(8,128)S(1)} async-done(((f32[32,72,128]{2,1,0:T(8,128)}), f32[32,72,128]{2,1,0:T(8,128)S(1)}, u32[]{:S(2)}, u32[]{:S(2)}) %all-to-all-start) | async-done | bytes 1179680 | tf_op jit(solution)/shard_map/all_to_all | solution.py:586
  43.7 2.5 %edges.1 = (f32[6144,128]{1,0:T(8,128)S(1)}, f32[3,96,128]{2,1,0:T(8,128)S(1)}, f32[3,96,128]{2,1,0:T(8,128)S(1)}) custom-call(s32[48,128]{1,0:T(8,128)S(1)} %fusion.2.slot_ref, f32[2304,128]{1,0:T(8,128)S(1)} %bitcast.19, f32[48,48,128]{2,1,0:T(8,128)S(1)} %get-tuple-element.12.coef_ref.own_ref), custom_call_target="tpu_custom_call" | custom-call | tf_op jit(solution)/shard_map/edges/pallas_call | solution.py:268
  46.3 0.0 copy-start.1
  46.3 1.7 %copy-done.1 = f32[6144,128]{1,0:T(8,128)} copy-done((f32[6144,128]{1,0:T(8,128)}, f32[6144,128]{1,0:T(8,128)S(1)}, u32[]{:S(2)}) %copy-start.1) | copy-done | bytes 3145752
  47.9 0.8 collective-permute-start.1
  48.7 0.0 collective-permute-start
  48.7 0.0 copy-start.2
  48.7 1.9 %copy-done.2 = f32[6144,128]{1,0:T(8,128)S(1)} copy-done((f32[6144,128]{1,0:T(8,128)S(1)}, f32[6144,128]{1,0:T(8,128)}, u32[]{:S(2)}) %copy-start.2) | copy-done | bytes 3145752
  50.6 0.0 copy-start.7
  50.6 6.8 %collect.1.body_ref.rhs_ref = f32[48,48,128]{2,1,0:T(8,128)S(1)} custom-call(s32[48,128]{1,0:T(8,128)S(1)} %fusion.2.slot_ref, f32[6144,128]{1,0:T(8,128)S(1)} %copy-done.2, f32[3,96,128]{2,1,0:T(8,128)S(1)} %get-tuple-element.14.top_ref, f32[3,96,128]{2,1,0:T(8,128)S(1)} %get-tuple-element.15.bottom_ref), custom_call_target="tpu_custom_call" | custom-call | tf_op jit(solution)/shard_map/collect/pallas_call | solution.py:302
  57.4 0.0 collective-permute-done.1.after_ref
  57.4 0.0 collective-permute-done.before_ref
  57.4 0.0 copy-done.7
  57.4 0.8 pack_edges.1
  58.3 2.7 %collective-permute-start.2 = (f32[2,96,128]{2,1,0:T(8,128)S(1)}, f32[2,96,128]{2,1,0:T(8,128)S(1)}, u32[]{:S(2)}, u32[]{:S(2)}) collective-permute-start(f32[2,96,128]{2,1,0:T(8,128)S(1)} %get-tuple-element.18), channel_id=1, source_target_pairs={{1,0},{2,1},{3,2},{0,3},{5,4},{6,5},{7,6},{4,7},{9,8},{10,9},{11,1... | collective-permute-start | bytes 294920 | tf_op jit(solution)/shard_map/ppermute | solution.py:631
  61.0 0.0 collective-permute-start.3
  61.0 0.1 add_convert_fusion.inside_ref
  61.1 3.1 %collective-permute-done.2.past_ref = f32[2,96,128]{2,1,0:T(8,128)S(1)} collective-permute-done((f32[2,96,128]{2,1,0:T(8,128)S(1)}, f32[2,96,128]{2,1,0:T(8,128)S(1)}, u32[]{:S(2)}, u32[]{:S(2)}) %collective-permute-start.2) | collective-permute-done | bytes 98336 | tf_op jit(solution)/shard_map/ppermute | solution.py:631
  64.2 3.1 %collective-permute-done.3.ahead_ref = f32[2,96,128]{2,1,0:T(8,128)S(1)} collective-permute-done((f32[2,96,128]{2,1,0:T(8,128)S(1)}, f32[2,96,128]{2,1,0:T(8,128)S(1)}, u32[]{:S(2)}, u32[]{:S(2)}) %collective-permute-start.3) | collective-permute-done | bytes 98336 | tf_op jit(solution)/shard_map/ppermute | solution.py:630
  67.3 18.1 %sweeps.1 = (f32[48,48,128]{2,1,0:T(8,128)}, f32[2304,128]{1,0:T(8,128)}) custom-call(s32[48,128]{1,0:T(8,128)S(1)} %fusion.2.slot_ref, f32[4]{0:T(128)S(1)} %add_convert_fusion.inside_ref, f32[48,48,128]{2,1,0:T(8,128)S(1)} %collect.1.body_ref.rhs_ref, f32[48,48,128]{2,1,0:T(8,128)S(1)} %get-tuple-element.12.coef_ref.own_ref, ...), custom_call_target="tpu_custom_call" | custom-call | tf_op jit(solution)/shard_map/sweeps/pallas_call | solution.py:554
  85.4 2.7 %all-to-all-start.1 = ((f32[32,72,128]{2,1,0:T(8,128)}), f32[32,72,128]{2,1,0:T(8,128)S(1)}, u32[]{:S(2)}, u32[]{:S(2)}) async-start(f32[32,72,128]{2,1,0:T(8,128)} %bitcast.13), calls=%async_computation.1 | async-start | bytes 2359296 | tf_op jit(solution)/shard_map/all_to_all | solution.py:586
  88.1 0.0 copy-start
  88.1 2.8 %copy.11 = f32[48,3,16,128]{3,0,1,2:T(8,128)} copy(f32[48,3,16,128]{3,2,1,0:T(8,128)} %bitcast.25) | data formatting | bytes 2359296 | tf_op jit(solution)/shard_map/reshape | solution.py:634
  90.9 26.3 %all-to-all-done.1 = f32[32,72,128]{2,1,0:T(8,128)S(1)} async-done(((f32[32,72,128]{2,1,0:T(8,128)}), f32[32,72,128]{2,1,0:T(8,128)S(1)}, u32[]{:S(2)}, u32[]{:S(2)}) %all-to-all-start.1) | async-done | bytes 1179680 | tf_op jit(solution)/shard_map/all_to_all | solution.py:586
  117.2 0.0 copy-done
  117.2 5.1 %prolong.1 = f32[3,16,49152]{2,1,0:T(8,128)} custom-call(f32[2304,128]{1,0:T(8,128)S(1)} %bitcast.18, f32[3,3,49152]{2,1,0:T(4,128)S(1)} %copy-done, s32[1,49152]{1,0:T(1,128)} %bitcast.28), custom_call_target="tpu_custom_call" | custom-call | tf_op jit(solution)/shard_map/prolong/pallas_call | solution.py:232
  (1 shorter events, 0.0 us)
Async XLA Ops:
  7.3 7.4 %copy-start.3 = (f32[4,3,3,48,128]{4,3,2,1,0:T(8,128)S(1)}, f32[4,3,3,48,128]{4,3,2,1,0:T(8,128)}, u32[]{:S(2)}) copy-start(f32[4,3,3,48,128]{4,3,2,1,0:T(8,128)} %param.12) | copy-start | bytes 2654212
  7.3 7.4 %copy-start.4 = (f32[3,3,48,128]{3,2,1,0:T(8,128)S(1)}, f32[3,3,48,128]{3,2,1,0:T(8,128)}, u32[]{:S(2)}) copy-start(f32[3,3,48,128]{3,2,1,0:T(8,128)} %param.11) | copy-start | bytes 663556
  7.3 10.5 %copy-start.8 = (s32[48,128]{1,0:T(8,128)S(1)}, s32[48,128]{1,0:T(8,128)}, u32[]{:S(2)}) copy-start(s32[48,128]{1,0:T(8,128)} %param.10) | copy-start | bytes 73732
  7.3 36.4 %all-to-all-start = ((f32[32,72,128]{2,1,0:T(8,128)}), f32[32,72,128]{2,1,0:T(8,128)S(1)}, u32[]{:S(2)}, u32[]{:S(2)}) async-start(f32[32,72,128]{2,1,0:T(8,128)} %bitcast.6), calls=%async_computation | async-start | bytes 2359296 | tf_op jit(solution)/shard_map/all_to_all | solution.py:586
  14.7 0.9 copy-start.5
  17.2 0.6 copy-start.6
  46.3 1.7 %copy-start.1 = (f32[6144,128]{1,0:T(8,128)}, f32[6144,128]{1,0:T(8,128)S(1)}, u32[]{:S(2)}) copy-start(f32[6144,128]{1,0:T(8,128)S(1)} %get-tuple-element.13.lines) | copy-start | bytes 9437188
  47.9 9.5 %collective-permute-start.1 = (f32[3,96,128]{2,1,0:T(8,128)S(1)}, f32[3,96,128]{2,1,0:T(8,128)S(1)}, u32[]{:S(2)}, u32[]{:S(2)}) collective-permute-start(f32[3,96,128]{2,1,0:T(8,128)S(1)} %get-tuple-element.14.top_ref), channel_id=1, source_target_pairs={{4,0},{8,4},{12,8},{16,12},{20,16},{24,20},{28,24},{0,28},{5,1},{9... | collective-permute-start | bytes 442376 | tf_op jit(solution)/shard_map/ppermute | solution.py:626
  48.7 8.7 %collective-permute-start = (f32[3,96,128]{2,1,0:T(8,128)S(1)}, f32[3,96,128]{2,1,0:T(8,128)S(1)}, u32[]{:S(2)}, u32[]{:S(2)}) collective-permute-start(f32[3,96,128]{2,1,0:T(8,128)S(1)} %get-tuple-element.15.bottom_ref), channel_id=1, source_target_pairs={{0,4},{4,8},{8,12},{12,16},{16,20},{20,24},{24,28},{28,0},{1,5},{5... | collective-permute-start | bytes 442376 | tf_op jit(solution)/shard_map/ppermute | solution.py:625
  48.7 1.9 %copy-start.2 = (f32[6144,128]{1,0:T(8,128)S(1)}, f32[6144,128]{1,0:T(8,128)}, u32[]{:S(2)}) copy-start(f32[6144,128]{1,0:T(8,128)} %copy-done.1) | copy-start | bytes 9437188
  50.6 6.8 %copy-start.7 = (f32[2,48,128]{2,1,0:T(8,128)S(1)}, f32[2,48,128]{2,1,0:T(8,128)}, u32[]{:S(2)}) copy-start(f32[2,48,128]{2,1,0:T(8,128)} %copy-done.6) | copy-start | bytes 147460
  58.3 5.9 %collective-permute-start.2 = (f32[2,96,128]{2,1,0:T(8,128)S(1)}, f32[2,96,128]{2,1,0:T(8,128)S(1)}, u32[]{:S(2)}, u32[]{:S(2)}) collective-permute-start(f32[2,96,128]{2,1,0:T(8,128)S(1)} %get-tuple-element.18), channel_id=1, source_target_pairs={{1,0},{2,1},{3,2},{0,3},{5,4},{6,5},{7,6},{4,7},{9,8},{10,9},{11,1... | collective-permute-start | bytes 294920 | tf_op jit(solution)/shard_map/ppermute | solution.py:631
  61.0 6.3 %collective-permute-start.3 = (f32[2,96,128]{2,1,0:T(8,128)S(1)}, f32[2,96,128]{2,1,0:T(8,128)S(1)}, u32[]{:S(2)}, u32[]{:S(2)}) collective-permute-start(f32[2,96,128]{2,1,0:T(8,128)S(1)} %get-tuple-element.19), channel_id=1, source_target_pairs={{0,1},{1,2},{2,3},{3,0},{4,5},{5,6},{6,7},{7,4},{8,9},{9,10},{10,1... | collective-permute-start | bytes 294920 | tf_op jit(solution)/shard_map/ppermute | solution.py:630
  85.4 31.8 %all-to-all-start.1 = ((f32[32,72,128]{2,1,0:T(8,128)}), f32[32,72,128]{2,1,0:T(8,128)S(1)}, u32[]{:S(2)}, u32[]{:S(2)}) async-start(f32[32,72,128]{2,1,0:T(8,128)} %bitcast.13), calls=%async_computation.1 | async-start | bytes 2359296 | tf_op jit(solution)/shard_map/all_to_all | solution.py:586
  88.1 29.1 %copy-start = (f32[3,3,49152]{2,1,0:T(4,128)S(1)}, f32[3,3,49152]{2,1,0:T(4,128)}, u32[]{:S(2)}) copy-start(f32[3,3,49152]{2,1,0:T(4,128)} %rest_ref.1) | copy-start | bytes 5308420

commit v6 on v5

--- a/solution.py
+++ b/solution.py
@@ -333,16 +333,6 @@
         right_ref[pack, span, :] = right
 
 
-def beyond(past, ahead, member, depth):
-    if member:
-        past = pltpu.roll(past, LANES - member * EDGE, 1)
-    turn = (member + 1) * EDGE
-    if turn < LANES:
-        ahead = pltpu.roll(ahead, LANES - turn, 1)
-    lane = lax.broadcasted_iota(jnp.int32, past.shape, 1)
-    return jnp.where(lane < depth, past, jnp.where(lane >= LANES - depth, ahead, 0.0))
-
-
 def pack_kernel(s, body_ref, left_coef_ref, right_coef_ref, before_ref, after_ref, left_ref, right_ref):
     def line_of(at, own_ref, span):
         if at < s.depth:
@@ -407,122 +397,172 @@
     )(inverse.reshape(-1, LANES), blocks.reshape(-1, LANES), pattern.reshape(-1, LANES))
 
 
-def sweeps_kernel(
-    s, slot_ref, inside_ref, rhs_ref, own_ref, before_ref, after_ref, past_ref, ahead_ref,
-    sol_hbm, out_ref, wide, coef_ref, even, odd, sol_ref, lines, ahead_lines, behind_lines, sem,
-):
-    q = s.q
-    halves = range(0, q, 8)
-    lane = lax.broadcasted_iota(jnp.int32, (COEFS, LANES), 1)
-    side = jnp.where(lane < LANES // 2, inside_ref[3], inside_ref[2])
-    for held, inner_ref, part in (
-        (wide, rhs_ref, slice(0, s.comps)),
-        (coef_ref, own_ref, slice(s.comps, s.comps + COEFS)),
-    ):
-        for at in range(s.wide):
-            if at < s.depth:
-                line, inside = before_ref[at, part, :], inside_ref[0]
-            elif at < s.depth + s.rows:
-                line, inside = inner_ref[at - s.depth], None
-            else:
-                line, inside = after_ref[at - s.depth - s.rows, part, :], inside_ref[1]
-            pack, member = divmod(at, PACK)
-            other = beyond(past_ref[pack, part, :], ahead_ref[pack, part, :], member, s.depth)
-            if held is coef_ref:
-                other = other * side
-                if inside is not None:
-                    line, other = line * inside, other * inside
-            held[at, :, 0:LANES] = line
-            held[at, :, LANES : 2 * LANES] = other
-
-    lane = lax.broadcasted_iota(jnp.int32, (8, LANES), 1)
-    is_first = lane == 0
-    is_last = lane == LANES - 1
-    columns = (slice(0, LANES), slice(LANES, 2 * LANES))
-
-    def span(comp, low):
-        return slice(comp * q + low, comp * q + low + 8)
-
-    def invert(at, total, column):
+class Jacobi:
+    def __init__(self, s, rhs_ref, coef_ref):
+        self.q, self.rhs, self.coef = s.q, rhs_ref, coef_ref
+        self.halves = range(0, s.q, 8)
+
+    def span(self, comp, low):
+        return slice(comp * self.q + low, comp * self.q + low + 8)
+
+    def read(self, ref, at):
+        return [[ref[at, self.span(comp, low), :] for low in self.halves] for comp in range(3)]
+
+    def write(self, ref, at, fresh):
+        for comp in range(3):
+            for half, low in enumerate(self.halves):
+                ref[at, self.span(comp, low), :] = fresh[comp][half]
+
+    def factor(self, at, index):
+        return self.coef[at, index : index + 1, :]
+
+    def invert(self, at, total):
         fresh = []
         for comp in range(3):
-            value = [None] * len(halves)
+            value = [None] * len(self.halves)
             for source in range(3):
-                index = comp * 3 + source
-                factor = coef_ref[at, index : index + 1, column]
-                for half in range(len(halves)):
+                factor = self.factor(at, comp * 3 + source)
+                for half in range(len(self.halves)):
                     term = factor * total[source][half]
                     value[half] = term if source == 0 else value[half] + term
             fresh.append(value)
         return fresh
 
-    def put(target, at, fresh, column):
+    def first(self, at):
+        return self.invert(at, self.read(self.rhs, at))
+
+    def next(self, old, at):
+        here = self.read(old, at)
+        pieces = [
+            self.read(old, at - 1),
+            self.read(old, at + 1),
+            [[turn(x, 1) for x in each] for each in here],
+            [[turn(x, -1) for x in each] for each in here],
+        ]
+        total = self.read(self.rhs, at)
         for comp in range(3):
-            for half, low in enumerate(halves):
-                target[at, span(comp, low), column] = fresh[comp][half]
-
-    def first(at, carry):
-        for column in columns:
-            total = [[wide[at, span(comp, low), column] for low in halves] for comp in range(3)]
-            put(even, at, invert(at, total, column), column)
+            for direction in range(4):
+                for source in range(3):
+                    factor = self.factor(at, 9 + (direction * 3 + comp) * 3 + source)
+                    for half in range(len(self.halves)):
+                        total[comp][half] = total[comp][half] - factor * pieces[direction][source][half]
+        return self.invert(at, total)
+
+    def run(self, s, even, odd):
+        def first(k, carry):
+            for at in (2 * k, 2 * k + 1):
+                self.write(even, at, self.first(at))
+            return carry
+
+        lax.fori_loop(0, s.wide // 2, first, 0)
+        old, new = even, odd
+        for inner in range(1, s.depth):
+            def middle(k, carry, old=old, new=new, inner=inner):
+                for step in range(2):
+                    at = inner + 2 * k + step
+                    self.write(new, at, self.next(old, at))
+                return carry
+
+            lax.fori_loop(0, (s.wide - 2 * inner) // 2, middle, 0)
+            old, new = new, old
+        return old
+
+
+HALF = LANES // 2
+
+
+def inside_of(axis):
+    here = lax.axis_index(axis)
+    return [jnp.where(x, 1.0, 0.0) for x in (here > 0, here < lax.axis_size(axis) - 1)]
+
+
+def inner_kernel(
+    s, rhs_ref, own_ref, before_ref, after_ref,
+    sol_ref, rhs_strip_ref, coef_strip_ref, wide, coef_ref, even, odd,
+):
+    inside = inside_of("row")
+    lane = lax.broadcasted_iota(jnp.int32, (COEFS, LANES), 1)
+    for held, own, strip, part in (
+        (wide, rhs_ref, rhs_strip_ref, slice(0, s.comps)),
+        (coef_ref, own_ref, coef_strip_ref, slice(s.comps, s.comps + COEFS)),
+    ):
+        for at in range(s.wide):
+            row = at - s.depth
+            if row < 0:
+                line, side = before_ref[at, part, :], inside[0]
+            elif row < s.rows:
+                line, side = own[row], None
+            else:
+                line, side = after_ref[row - s.rows, part, :], inside[1]
+            if held is coef_ref and side is not None:
+                line = line * side
+            held[at] = line
+            strip[at] = jnp.where(lane < LANES // 4, line, turn(line, HALF))
+
+    jacobi = Jacobi(s, wide, coef_ref)
+    old = jacobi.run(s, even, odd)
+
+    def last(k, carry):
+        for row in (2 * k, 2 * k + 1):
+            jacobi.write(sol_ref, row, jacobi.next(old, row + s.depth))
         return carry
 
-    lax.fori_loop(0, s.wide, first, 0)
-
-    def turned(old, at):
-        west = ([], [])
-        east = ([], [])
+    lax.fori_loop(0, s.rows // 2, last, 0)
+
+
+def inner(s, rhs, coefs, before, after):
+    strip = (s.wide, s.comps, LANES)
+    coef_strip = (s.wide, COEFS, LANES)
+    state = pltpu.VMEM(strip, jnp.float32)
+    return pl.pallas_call(
+        functools.partial(inner_kernel, s),
+        in_specs=[vmem_spec()] * 4,
+        out_specs=[vmem_spec()] * 3,
+        out_shape=[vmem_result(s.rows, s.comps, LANES), vmem_result(*strip), vmem_result(*coef_strip)],
+        scratch_shapes=[state, pltpu.VMEM(coef_strip, jnp.float32), state, state],
+        name="inner",
+        compiler_params=KERNEL,
+    )(rhs, coefs, in_vmem(before), in_vmem(after))
+
+
+def outer_kernel(
+    s, slot_ref, inner_ref, rhs_strip_ref, coef_strip_ref, past_ref, ahead_ref,
+    sol_hbm, out_ref, wide, coef_ref, even, odd, sol_ref, lines, ahead_lines, behind_lines, sem,
+):
+    lane = lax.broadcasted_iota(jnp.int32, (COEFS, LANES), 1)
+    left, right = lane >= LANES - s.depth, (lane >= HALF) & (lane < HALF + s.depth)
+    rows = inside_of("row")
+    columns = inside_of("col")
+    for held, own, part in (
+        (wide, rhs_strip_ref, slice(0, s.comps)),
+        (coef_ref, coef_strip_ref, slice(s.comps, s.comps + COEFS)),
+    ):
+        for pack in range(past_ref.shape[0]):
+            past, ahead = past_ref[pack, part, :], ahead_ref[pack, part, :]
+            if held is coef_ref:
+                past, ahead = past * columns[1], ahead * columns[0]
+            for member in range(min(PACK, s.wide - pack * PACK)):
+                at = pack * PACK + member
+                far, near = turn(past, HALF - member * EDGE), turn(ahead, -(member + 1) * EDGE)
+                if held is coef_ref and not s.depth <= at < s.depth + s.rows:
+                    side = rows[0] if at < s.depth else rows[1]
+                    far, near = far * side, near * side
+                held[at] = jnp.where(right, far, jnp.where(left, near, own[at]))
+
+    jacobi = Jacobi(s, wide, coef_ref)
+    old = jacobi.run(s, even, odd)
+    place = lax.broadcasted_iota(jnp.int32, (8, LANES), 1)
+
+    def finish(row, held):
+        fresh = jacobi.next(old, row + s.depth)
+        main = jacobi.read(inner_ref, row)
         for comp in range(3):
-            for side in west + east:
-                side.append([])
-            for low in halves:
-                here = [old[at, span(comp, low), column] for column in columns]
-                up = [pltpu.roll(x, 1, 1) for x in here]
-                down = [pltpu.roll(x, LANES - 1, 1) for x in here]
-                for v in range(2):
-                    west[v][-1].append(jnp.where(is_first, up[1 - v], up[v]))
-                    east[v][-1].append(jnp.where(is_last, down[1 - v], down[v]))
-        return west, east
-
-    def sweep(old, at, count):
-        west, east = turned(old, at)
-        result = []
-        for v in range(count):
-            column = columns[v]
-            pieces = []
-            for where in (at - 1, at + 1):
-                pieces.append([[old[where, span(comp, low), column] for low in halves] for comp in range(3)])
-            pieces += [west[v], east[v]]
-            total = []
-            for comp in range(3):
-                value = [wide[at, span(comp, low), column] for low in halves]
-                for direction in range(4):
-                    for source in range(3):
-                        index = 9 + (direction * 3 + comp) * 3 + source
-                        factor = coef_ref[at, index : index + 1, column]
-                        for half in range(len(halves)):
-                            value[half] = value[half] - factor * pieces[direction][source][half]
-                total.append(value)
-            result.append(invert(at, total, column))
-        return result
-
-    old, new = even, odd
-    for inner in range(1, s.depth):
-        def middle(k, carry, old=old, new=new, inner=inner):
-            for step in range(2):
-                at = inner + 2 * k + step
-                for column, fresh in zip(columns, sweep(old, at, 2)):
-                    put(new, at, fresh, column)
-            return carry
-
-        lax.fori_loop(0, (s.wide - 2 * inner) // 2, middle, 0)
-        old, new = new, old
-
-    def finish(row, held):
-        (fresh,) = sweep(old, row + s.depth, 1)
-        put(sol_ref, row, fresh, columns[0])
-        parts = [fresh[comp][half] for comp in range(3) for half in range(len(halves))]
-        held[:, 0 : s.comps] = jnp.concatenate(parts, axis=0).T
+            for half in range(len(fresh[comp])):
+                strip = fresh[comp][half]
+                value = jnp.where(place < s.depth, strip, main[comp][half])
+                fresh[comp][half] = jnp.where(place >= LANES - s.depth, turn(strip, HALF), value)
+        jacobi.write(sol_ref, row, fresh)
+        held[:, 0 : s.comps] = jnp.concatenate([x for each in fresh for x in each], axis=0).T
 
     def send(row, held):
         for column in range(LANES):
@@ -549,11 +589,11 @@
     copy.wait()
 
 
-def sweeps(s, slots, inside, rhs, coefs, before, after, past, ahead):
-    state = pltpu.VMEM((s.wide, s.comps, 2 * LANES), jnp.float32)
-    return pl.pallas_call(
-        functools.partial(sweeps_kernel, s),
-        in_specs=[pl.BlockSpec(memory_space=pltpu.SMEM)] * 2 + [vmem_spec()] * 6,
+def outer(s, slots, main, rhs_strip, coef_strip, past, ahead):
+    state = pltpu.VMEM((s.wide, s.comps, LANES), jnp.float32)
+    return pl.pallas_call(
+        functools.partial(outer_kernel, s),
+        in_specs=[pl.BlockSpec(memory_space=pltpu.SMEM)] + [vmem_spec()] * 5,
         out_specs=[pl.BlockSpec(memory_space=pltpu.HBM), vmem_spec()],
         out_shape=[
             pltpu.HBM((s.rows, s.comps, LANES), jnp.float32),
@@ -561,7 +601,7 @@
         ],
         scratch_shapes=[
             state,
-            pltpu.VMEM((s.wide, COEFS, 2 * LANES), jnp.float32),
+            pltpu.VMEM((s.wide, COEFS, LANES), jnp.float32),
             state,
             state,
             pltpu.VMEM((s.rows, s.comps, LANES), jnp.float32),
@@ -570,9 +610,9 @@
             pltpu.VMEM((LANES, LANES), jnp.float32),
             pltpu.SemaphoreType.DMA,
         ],
-        name="sweeps",
-        compiler_params=KERNEL,
-    )(slots, inside, rhs, coefs, *map(in_vmem, (before, after, past, ahead)))
+        name="outer",
+        compiler_params=KERNEL,
+    )(slots, main, rhs_strip, coef_strip, in_vmem(past), in_vmem(ahead))
 
 
 def ring(axis):
@@ -614,12 +654,6 @@
     slots = local // s.devices * s.devices + owner
     coefs, *packs = prepare(s, block_inverse, off_blocks, operator_pattern)
 
-    ends = []
-    for axis in AXES:
-        here = lax.axis_index(axis)
-        ends += [here > 0, here < lax.axis_size(axis) - 1]
-    inside = jnp.stack(ends).astype(jnp.float32)
-
     up, down = ring("row")
     lines, top, bottom = edges(s, received, slots, coefs)
     before = lax.ppermute(bottom, "row", up)
@@ -629,7 +663,8 @@
     up, down = ring("col")
     ahead = lax.ppermute(right, "col", up)
     past = lax.ppermute(left, "col", down)
-    solved, outgoing = sweeps(s, slots, inside, rhs, coefs, before, after, past, ahead)
+    main, *strips = inner(s, rhs, coefs, before, after)
+    solved, outgoing = outer(s, slots, main, *strips, past, ahead)
     correction = prolong(s, exchange(s, outgoing), restriction, pattern)
     coarse = solved.reshape(s.rows, 3, s.loads, LANES).transpose(2, 1, 0, 3)
     return coarse, correction.transpose(1, 0, 2)

time: 123 us -> 123 us (level)
  Pallas kernels: 41.7 us -> 49.2 us
  waiting for transfers between devices: 58.3 us -> 51.4 us
  local copies, waits for them, and re-layouts: 7.88 us -> 4.34 us
  starting transfers between devices: 13.5 us -> 16.6 us
    pallas_call x1 -> x2, Pallas kernels: 18.1 us -> 25.6 us  [the longest x1 16.6 us: outer(): pl.pallas_call(functools.partial(outer_kernel, s), in_specs=[pl.BlockSpec...]
    unnamed x18 -> x12, local copies, waits for them, and re-layouts: 5.07 us -> 1.53 us
    ppermute x1, waiting for transfers between devices: 3.12 us -> 0.01 us  [body(): ahead = lax.ppermute(right, 'col', up)]
    ppermute x1, waiting for transfers between devices: 3.11 us -> 0.01 us  [body(): past = lax.ppermute(left, 'col', down)]
    all_to_all x2, starting transfers between devices: 10 us -> 13 us  [exchange(): lax.all_to_all(blocks, AXES, split_axis=0, concat_axis=0, tiled=True)]
  transfers between devices with their start and end apart: 6 -> 6, of which waited for: 4 -> 2; matrix products, arithmetic and copies ran while one was open for 2% -> 3% of each run, Pallas kernels for 7% -> 14%
where the time goes in v6:
time: 123 us
  waiting for transfers between devices  51.4 us (42%)
  Pallas kernels  49.2 us (40%)
  starting transfers between devices  16.6 us (13%)
  local copies, waits for them, and re-layouts  4.34 us (4%)
    all_to_all x2, waiting for transfers between devices, exchange(): lax.all_to_all(blocks, AXES, split_axis=0, concat_axis=0, tiled=True)  51.4 us
    pallas_call x1, Pallas kernels, outer(): pl.pallas_call(functools.partial(outer_kernel, s), in_specs=[pl.BlockSpec...  16.6 us
    all_to_all x2, starting transfers between devices, exchange(): lax.all_to_all(blocks, AXES, split_axis=0, concat_axis=0, tiled=True)  13 us
    pallas_call x1, Pallas kernels, inner(): pl.pallas_call(functools.partial(inner_kernel, s), in_specs=[vmem_spec()]...  9.04 us
    pallas_call x1, Pallas kernels, collect(): pl.pallas_call(functools.partial(collect_kernel, s), in_specs=[pl.BlockSp...  6.79 us
    pallas_call x1, Pallas kernels, restrict(): pl.pallas_call(functools.partial(restrict_kernel, s), in_specs=[pl.BlockS...  6.65 us
    pallas_call x1, Pallas kernels, prolong(): pl.pallas_call(functools.partial(prolong_kernel, s), in_specs=[vmem_spec(...  5.14 us
    reshape x1, local copies, waits for them, and re-layouts, body(): coarse = solved.reshape(s.rows, 3, s.loads, LANES).transpose(2, 1, 0, 3)  2.82 us
  transfers between devices with their start and end apart: 6, of which 2 were waited for; matrix products, arithmetic and copies ran while one was open for 3% of the time, Pallas kernels for 14%

profile of v6, /device:TPU:0, one launch (start us, length us, event | category | flops | bytes accessed | tf_op | source)
XLA Modules:
  0.0 123.1 jit_solution(4264655323409526878)
XLA Ops:
  0.6 6.6 %restrict.1 = f32[2304,128]{1,0:T(8,128)} custom-call(f32[3,16,49152]{2,1,0:T(8,128)} %bitcast.19, f32[3,3,49152]{2,1,0:T(4,128)} %rest_ref.1, s32[1,49152]{1,0:T(1,128)} %bitcast.23), custom_call_target="tpu_custom_call" | custom-call | tf_op jit(solution)/shard_map/restrict/pallas_call | solution.py:180
  7.3 0.0 copy-start.1
  7.3 0.0 copy-start.2
  7.3 7.3 %all-to-all-start = ((f32[32,72,128]{2,1,0:T(8,128)}), f32[32,72,128]{2,1,0:T(8,128)S(1)}, u32[]{:S(2)}, u32[]{:S(2)}) async-start(f32[32,72,128]{2,1,0:T(8,128)} %bitcast.2), calls=%async_computation | async-start | bytes 2359296 | tf_op jit(solution)/shard_map/all_to_all | solution.py:626
  14.6 0.0 copy-done.1
  14.7 0.0 copy-done.2
  14.7 0.0 copy-start.3
  14.7 0.9 copy-done.3
  15.6 1.7 %prepare.1 = (f32[48,48,128]{2,1,0:T(8,128)S(1)}, f32[2,48,128]{2,1,0:T(8,128)S(1)}, f32[2,48,128]{2,1,0:T(8,128)S(1)}) custom-call(f32[432,128]{1,0:T(8,128)S(1)} %bitcast.17, f32[1728,128]{1,0:T(8,128)S(1)} %bitcast.16, s32[192,128]{1,0:T(8,128)S(1)} %bitcast.18), custom_call_target="tpu_custom_call" | custom-call | tf_op jit(solution)/shard_map/prepare/pallas_call | solution.py:389
  17.2 0.0 copy-start.4
  17.2 0.6 copy-done.4
  17.8 0.8 fusion.2.slot_ref
  18.6 25.1 %all-to-all-done = f32[32,72,128]{2,1,0:T(8,128)S(1)} async-done(((f32[32,72,128]{2,1,0:T(8,128)}), f32[32,72,128]{2,1,0:T(8,128)S(1)}, u32[]{:S(2)}, u32[]{:S(2)}) %all-to-all-start) | async-done | bytes 1179680 | tf_op jit(solution)/shard_map/all_to_all | solution.py:626
  43.7 2.5 %edges.1 = (f32[6144,128]{1,0:T(8,128)S(1)}, f32[3,96,128]{2,1,0:T(8,128)S(1)}, f32[3,96,128]{2,1,0:T(8,128)S(1)}) custom-call(s32[48,128]{1,0:T(8,128)S(1)} %fusion.2.slot_ref, f32[2304,128]{1,0:T(8,128)S(1)} %bitcast.15, f32[48,48,128]{2,1,0:T(8,128)S(1)} %get-tuple-element.15.coef_ref.own_ref), custom_call_target="tpu_custom_call" | custom-call | tf_op jit(solution)/shard_map/edges/pallas_call | solution.py:268
  46.3 0.8 collective-permute-start.1
  47.1 0.0 collective-permute-start
  47.1 0.0 copy-start.5
  47.1 6.8 %collect.1.rhs_ref.body_ref = f32[48,48,128]{2,1,0:T(8,128)S(1)} custom-call(s32[48,128]{1,0:T(8,128)S(1)} %fusion.2.slot_ref, f32[6144,128]{1,0:T(8,128)S(1)} %get-tuple-element.16.lines, f32[3,96,128]{2,1,0:T(8,128)S(1)} %get-tuple-element.17.top_ref, f32[3,96,128]{2,1,0:T(8,128)S(1)} %get-tuple-element.18.bottom_ref), custom_call_target="tpu_custom_call" | custom-call | tf_op jit(solution)/shard_map/collect/pallas_call | solution.py:302
  53.9 0.0 collective-permute-done.1.after_ref
  53.9 0.0 collective-permute-done.before_ref
  53.9 0.0 copy-done.5
  53.9 0.8 pack_edges.1
  54.8 2.7 %collective-permute-start.2 = (f32[2,96,128]{2,1,0:T(8,128)S(1)}, f32[2,96,128]{2,1,0:T(8,128)S(1)}, u32[]{:S(2)}, u32[]{:S(2)}) collective-permute-start(f32[2,96,128]{2,1,0:T(8,128)S(1)} %get-tuple-element.24), channel_id=1, source_target_pairs={{1,0},{2,1},{3,2},{0,3},{5,4},{6,5},{7,6},{4,7},{9,8},{10,9},{11,1... | collective-permute-start | bytes 294920 | tf_op jit(solution)/shard_map/ppermute | solution.py:665
  57.5 0.0 collective-permute-start.3
  57.5 9.0 %inner.1 = (f32[48,48,128]{2,1,0:T(8,128)S(1)}, f32[54,48,128]{2,1,0:T(8,128)S(1)}, f32[54,48,128]{2,1,0:T(8,128)S(1)}) custom-call(f32[48,48,128]{2,1,0:T(8,128)S(1)} %collect.1.rhs_ref.body_ref, f32[48,48,128]{2,1,0:T(8,128)S(1)} %get-tuple-element.15.coef_ref.own_ref, f32[3,96,128]{2,1,0:T(8,128)S(1)} %collective-permute-done.before_ref, ...), custom_call_target="tpu_custom_call" | custom-call | tf_op jit(solution)/shard_map/inner/pallas_call | solution.py:517
  66.5 0.0 collective-permute-done.2.past_ref
  66.5 0.0 collective-permute-done.3.ahead_ref
  66.5 16.6 %outer.1 = (f32[48,48,128]{2,1,0:T(8,128)}, f32[2304,128]{1,0:T(8,128)}) custom-call(s32[48,128]{1,0:T(8,128)S(1)} %fusion.2.slot_ref, f32[48,48,128]{2,1,0:T(8,128)S(1)} %get-tuple-element.19.inner_ref, f32[54,48,128]{2,1,0:T(8,128)S(1)} %get-tuple-element.20.rhs_strip_ref, f32[54,48,128]{2,1,0:T(8,128)S(1)} %get-tuple-element.21.coef_strip_ref, ...), custom_call_target="tpu_custom_call" | custom-call | tf_op jit(solution)/shard_map/outer/pallas_call | solution.py:594
  83.1 5.7 %all-to-all-start.1 = ((f32[32,72,128]{2,1,0:T(8,128)}), f32[32,72,128]{2,1,0:T(8,128)S(1)}, u32[]{:S(2)}, u32[]{:S(2)}) async-start(f32[32,72,128]{2,1,0:T(8,128)} %bitcast.9), calls=%async_computation.1 | async-start | bytes 2359296 | tf_op jit(solution)/shard_map/all_to_all | solution.py:626
  88.8 0.0 copy-start
  88.9 2.8 %copy.11 = f32[48,3,16,128]{3,0,1,2:T(8,128)} copy(f32[48,3,16,128]{3,2,1,0:T(8,128)} %bitcast.22) | data formatting | bytes 2359296 | tf_op jit(solution)/shard_map/reshape | solution.py:669
  91.7 26.3 %all-to-all-done.1 = f32[32,72,128]{2,1,0:T(8,128)S(1)} async-done(((f32[32,72,128]{2,1,0:T(8,128)}), f32[32,72,128]{2,1,0:T(8,128)S(1)}, u32[]{:S(2)}, u32[]{:S(2)}) %all-to-all-start.1) | async-done | bytes 1179680 | tf_op jit(solution)/shard_map/all_to_all | solution.py:626
  117.9 0.0 copy-done
  117.9 5.1 %prolong.1 = f32[3,16,49152]{2,1,0:T(8,128)} custom-call(f32[2304,128]{1,0:T(8,128)S(1)} %bitcast.14, f32[3,3,49152]{2,1,0:T(4,128)S(1)} %copy-done, s32[1,49152]{1,0:T(1,128)} %bitcast.24), custom_call_target="tpu_custom_call" | custom-call | tf_op jit(solution)/shard_map/prolong/pallas_call | solution.py:232
Async XLA Ops:
  7.3 7.4 %copy-start.1 = (f32[4,3,3,48,128]{4,3,2,1,0:T(8,128)S(1)}, f32[4,3,3,48,128]{4,3,2,1,0:T(8,128)}, u32[]{:S(2)}) copy-start(f32[4,3,3,48,128]{4,3,2,1,0:T(8,128)} %param.12) | copy-start | bytes 2654212
  7.3 7.4 %copy-start.2 = (f32[3,3,48,128]{3,2,1,0:T(8,128)S(1)}, f32[3,3,48,128]{3,2,1,0:T(8,128)}, u32[]{:S(2)}) copy-start(f32[3,3,48,128]{3,2,1,0:T(8,128)} %param.11) | copy-start | bytes 663556
  7.3 36.4 %all-to-all-start = ((f32[32,72,128]{2,1,0:T(8,128)}), f32[32,72,128]{2,1,0:T(8,128)S(1)}, u32[]{:S(2)}, u32[]{:S(2)}) async-start(f32[32,72,128]{2,1,0:T(8,128)} %bitcast.2), calls=%async_computation | async-start | bytes 2359296 | tf_op jit(solution)/shard_map/all_to_all | solution.py:626
  14.7 0.9 copy-start.3
  17.2 0.6 copy-start.4
  46.3 7.6 %collective-permute-start.1 = (f32[3,96,128]{2,1,0:T(8,128)S(1)}, f32[3,96,128]{2,1,0:T(8,128)S(1)}, u32[]{:S(2)}, u32[]{:S(2)}) collective-permute-start(f32[3,96,128]{2,1,0:T(8,128)S(1)} %get-tuple-element.17.top_ref), channel_id=1, source_target_pairs={{4,0},{8,4},{12,8},{16,12},{20,16},{24,20},{28,24},{0,28},{5,1},{9... | collective-permute-start | bytes 442376 | tf_op jit(solution)/shard_map/ppermute | solution.py:660
  47.1 6.8 %collective-permute-start = (f32[3,96,128]{2,1,0:T(8,128)S(1)}, f32[3,96,128]{2,1,0:T(8,128)S(1)}, u32[]{:S(2)}, u32[]{:S(2)}) collective-permute-start(f32[3,96,128]{2,1,0:T(8,128)S(1)} %get-tuple-element.18.bottom_ref), channel_id=1, source_target_pairs={{0,4},{4,8},{8,12},{12,16},{16,20},{20,24},{24,28},{28,0},{1,5},{5... | collective-permute-start | bytes 442376 | tf_op jit(solution)/shard_map/ppermute | solution.py:659
  47.1 6.8 %copy-start.5 = (f32[2,48,128]{2,1,0:T(8,128)S(1)}, f32[2,48,128]{2,1,0:T(8,128)}, u32[]{:S(2)}) copy-start(f32[2,48,128]{2,1,0:T(8,128)} %copy-done.4) | copy-start | bytes 147460
  54.8 11.7 %collective-permute-start.2 = (f32[2,96,128]{2,1,0:T(8,128)S(1)}, f32[2,96,128]{2,1,0:T(8,128)S(1)}, u32[]{:S(2)}, u32[]{:S(2)}) collective-permute-start(f32[2,96,128]{2,1,0:T(8,128)S(1)} %get-tuple-element.24), channel_id=1, source_target_pairs={{1,0},{2,1},{3,2},{0,3},{5,4},{6,5},{7,6},{4,7},{9,8},{10,9},{11,1... | collective-permute-start | bytes 294920 | tf_op jit(solution)/shard_map/ppermute | solution.py:665
  57.5 9.1 %collective-permute-start.3 = (f32[2,96,128]{2,1,0:T(8,128)S(1)}, f32[2,96,128]{2,1,0:T(8,128)S(1)}, u32[]{:S(2)}, u32[]{:S(2)}) collective-permute-start(f32[2,96,128]{2,1,0:T(8,128)S(1)} %get-tuple-element.25), channel_id=1, source_target_pairs={{0,1},{1,2},{2,3},{3,0},{4,5},{5,6},{6,7},{7,4},{8,9},{9,10},{10,1... | collective-permute-start | bytes 294920 | tf_op jit(solution)/shard_map/ppermute | solution.py:664
  83.1 34.8 %all-to-all-start.1 = ((f32[32,72,128]{2,1,0:T(8,128)}), f32[32,72,128]{2,1,0:T(8,128)S(1)}, u32[]{:S(2)}, u32[]{:S(2)}) async-start(f32[32,72,128]{2,1,0:T(8,128)} %bitcast.9), calls=%async_computation.1 | async-start | bytes 2359296 | tf_op jit(solution)/shard_map/all_to_all | solution.py:626
  88.8 29.1 %copy-start = (f32[3,3,49152]{2,1,0:T(4,128)S(1)}, f32[3,3,49152]{2,1,0:T(4,128)}, u32[]{:S(2)}) copy-start(f32[3,3,49152]{2,1,0:T(4,128)} %rest_ref.1) | copy-start | bytes 5308420

commit v7 on v6

--- a/solution.py
+++ b/solution.py
@@ -360,9 +360,21 @@
 
 
 COEFS = 48
-
-
-def prepare_kernel(s, inv_ref, off_ref, pat_ref, body_ref, left_ref, right_ref, flat):
+HALF = LANES // 2
+SHIFT = LANES // 4
+
+
+def own_strip(line):
+    lane = lax.broadcasted_iota(jnp.int32, line.shape, 1)
+    return jnp.where(lane < SHIFT, line, turn(line, HALF))
+
+
+def second(shape):
+    lane = lax.broadcasted_iota(jnp.int32, shape, 1)
+    return (lane + SHIFT // 2) // SHIFT % 2 == 1
+
+
+def prepare_kernel(s, inv_ref, off_ref, pat_ref, body_ref, left_ref, right_ref, strip_ref, flat):
     rows = s.rows
     flat[0 : 9 * rows, :] = inv_ref[...]
     for direction in range(4):
@@ -374,7 +386,9 @@
 
     def one(row, carry):
         for low in range(0, COEFS, 8):
-            body_ref[row, low : low + 8, :] = flat[pl.ds(low * rows + row, 8, stride=rows), :]
+            line = flat[pl.ds(low * rows + row, 8, stride=rows), :]
+            body_ref[row, low : low + 8, :] = line
+            strip_ref[row, low : low + 8, :] = own_strip(line)
         return carry
 
     lax.fori_loop(0, rows, one, 0)
@@ -389,8 +403,13 @@
     return pl.pallas_call(
         functools.partial(prepare_kernel, s),
         in_specs=[vmem_spec()] * 3,
-        out_specs=[vmem_spec()] * 3,
-        out_shape=[vmem_result(s.rows, COEFS, LANES)] + [vmem_result(-(-s.wide // PACK), COEFS, LANES)] * 2,
+        out_specs=[vmem_spec()] * 4,
+        out_shape=[
+            vmem_result(s.rows, COEFS, LANES),
+            vmem_result(-(-s.wide // PACK), COEFS, LANES),
+            vmem_result(-(-s.wide // PACK), COEFS, LANES),
+            vmem_result(s.rows, COEFS, LANES),
+        ],
         scratch_shapes=[pltpu.VMEM((COEFS * s.rows, LANES), jnp.float32)],
         name="prepare",
         compiler_params=KERNEL,
@@ -398,9 +417,9 @@
 
 
 class Jacobi:
-    def __init__(self, s, rhs_ref, coef_ref):
-        self.q, self.rhs, self.coef = s.q, rhs_ref, coef_ref
-        self.halves = range(0, s.q, 8)
+    def __init__(self, loads, rhs_ref, coef_ref):
+        self.q, self.rhs, self.coef = loads, rhs_ref, coef_ref
+        self.halves = range(0, loads, 8)
 
     def span(self, comp, low):
         return slice(comp * self.q + low, comp * self.q + low + 8)
@@ -468,100 +487,107 @@
         return old
 
 
-HALF = LANES // 2
-
-
 def inside_of(axis):
     here = lax.axis_index(axis)
     return [jnp.where(x, 1.0, 0.0) for x in (here > 0, here < lax.axis_size(axis) - 1)]
 
 
-def inner_kernel(
-    s, rhs_ref, own_ref, before_ref, after_ref,
-    sol_ref, rhs_strip_ref, coef_strip_ref, wide, coef_ref, even, odd,
-):
+def inner_kernel(s, rhs_ref, own_ref, before_ref, after_ref, wide, coef_ref, even, strip_ref, odd):
     inside = inside_of("row")
-    lane = lax.broadcasted_iota(jnp.int32, (COEFS, LANES), 1)
-    for held, own, strip, part in (
-        (wide, rhs_ref, rhs_strip_ref, slice(0, s.comps)),
-        (coef_ref, own_ref, coef_strip_ref, slice(s.comps, s.comps + COEFS)),
-    ):
-        for at in range(s.wide):
-            row = at - s.depth
-            if row < 0:
-                line, side = before_ref[at, part, :], inside[0]
-            elif row < s.rows:
-                line, side = own[row], None
-            else:
-                line, side = after_ref[row - s.rows, part, :], inside[1]
-            if held is coef_ref and side is not None:
-                line = line * side
-            held[at] = line
-            strip[at] = jnp.where(lane < LANES // 4, line, turn(line, HALF))
-
-    jacobi = Jacobi(s, wide, coef_ref)
-    old = jacobi.run(s, even, odd)
-
-    def last(k, carry):
-        for row in (2 * k, 2 * k + 1):
-            jacobi.write(sol_ref, row, jacobi.next(old, row + s.depth))
-        return carry
-
-    lax.fori_loop(0, s.rows // 2, last, 0)
+    loads, coefs = slice(0, s.comps), slice(s.comps, s.comps + COEFS)
+    upper = second((8, LANES))
+    for at in range(s.wide):
+        row = at - s.depth
+        if row < 0:
+            line, factor = before_ref[at, loads, :], before_ref[at, coefs, :] * inside[0]
+        elif row < s.rows:
+            line, factor = rhs_ref[row], own_ref[row]
+        else:
+            line, factor = after_ref[row - s.rows, loads, :], after_ref[row - s.rows, coefs, :] * inside[1]
+        wide[at] = line
+        coef_ref[at] = factor
+        for comp in range(3):
+            low = comp * s.q
+            first, other = own_strip(line[low : low + 8]), own_strip(line[low + 8 : low + 16])
+            strip_ref[at, comp * 8 : comp * 8 + 8, :] = jnp.where(upper, turn(other, SHIFT), first)
+    Jacobi(s.q, wide, coef_ref).run(s, even, odd)
 
 
 def inner(s, rhs, coefs, before, after):
-    strip = (s.wide, s.comps, LANES)
-    coef_strip = (s.wide, COEFS, LANES)
-    state = pltpu.VMEM(strip, jnp.float32)
+    tile = (s.wide, s.comps, LANES)
     return pl.pallas_call(
         functools.partial(inner_kernel, s),
         in_specs=[vmem_spec()] * 4,
-        out_specs=[vmem_spec()] * 3,
-        out_shape=[vmem_result(s.rows, s.comps, LANES), vmem_result(*strip), vmem_result(*coef_strip)],
-        scratch_shapes=[state, pltpu.VMEM(coef_strip, jnp.float32), state, state],
+        out_specs=[vmem_spec()] * 4,
+        out_shape=[
+            vmem_result(*tile),
+            vmem_result(s.wide, COEFS, LANES),
+            vmem_result(*tile),
+            vmem_result(s.wide, 24, LANES),
+        ],
+        scratch_shapes=[pltpu.VMEM(tile, jnp.float32)],
         name="inner",
         compiler_params=KERNEL,
     )(rhs, coefs, in_vmem(before), in_vmem(after))
 
 
 def outer_kernel(
-    s, slot_ref, inner_ref, rhs_strip_ref, coef_strip_ref, past_ref, ahead_ref,
+    s, slot_ref, main_rhs_ref, main_coef_ref, main_ref, rhs_strip_ref, coef_strip_ref, past_ref, ahead_ref,
     sol_hbm, out_ref, wide, coef_ref, even, odd, sol_ref, lines, ahead_lines, behind_lines, sem,
 ):
-    lane = lax.broadcasted_iota(jnp.int32, (COEFS, LANES), 1)
-    left, right = lane >= LANES - s.depth, (lane >= HALF) & (lane < HALF + s.depth)
+    columns = inside_of("col")
     rows = inside_of("row")
-    columns = inside_of("col")
-    for held, own, part in (
-        (wide, rhs_strip_ref, slice(0, s.comps)),
-        (coef_ref, coef_strip_ref, slice(s.comps, s.comps + COEFS)),
-    ):
-        for pack in range(past_ref.shape[0]):
-            past, ahead = past_ref[pack, part, :], ahead_ref[pack, part, :]
-            if held is coef_ref:
-                past, ahead = past * columns[1], ahead * columns[0]
-            for member in range(min(PACK, s.wide - pack * PACK)):
-                at = pack * PACK + member
-                far, near = turn(past, HALF - member * EDGE), turn(ahead, -(member + 1) * EDGE)
-                if held is coef_ref and not s.depth <= at < s.depth + s.rows:
-                    side = rows[0] if at < s.depth else rows[1]
-                    far, near = far * side, near * side
-                held[at] = jnp.where(right, far, jnp.where(left, near, own[at]))
-
-    jacobi = Jacobi(s, wide, coef_ref)
-    old = jacobi.run(s, even, odd)
+
+    def sides(shape, by):
+        lane = lax.broadcasted_iota(jnp.int32, shape, 1)
+        right = (lane >= HALF + by) & (lane < HALF + by + s.depth)
+        end = by if by else LANES
+        return right, (lane >= end - s.depth) & (lane < end)
+
+    upper = second((COEFS, LANES))
+    factor_sides = sides((COEFS, LANES), 0)
+    load_sides = [sides((8, LANES), 0), sides((8, LANES), SHIFT)]
+    coefs = slice(s.comps, s.comps + COEFS)
+    for at in range(s.wide):
+        pack, member = divmod(at, PACK)
+        row = at - s.depth
+        far = turn(past_ref[pack, coefs, :], HALF - member * EDGE) * columns[1]
+        near = turn(ahead_ref[pack, coefs, :], -(member + 1) * EDGE) * columns[0]
+        if 0 <= row < s.rows:
+            own = coef_strip_ref[row]
+        else:
+            own = own_strip(main_coef_ref[at])
+            side = rows[0] if row < 0 else rows[1]
+            far, near = far * side, near * side
+        right, left = factor_sides
+        factor = jnp.where(right, far, jnp.where(left, near, own))
+        coef_ref[at] = jnp.where(upper, turn(factor, SHIFT), factor)
+        for comp in range(3):
+            value = rhs_strip_ref[at, comp * 8 : comp * 8 + 8, :]
+            for half in range(2):
+                part = slice(comp * s.q + half * 8, comp * s.q + half * 8 + 8)
+                by = half * SHIFT
+                right, left = load_sides[half]
+                far = turn(past_ref[pack, part, :], HALF + by - member * EDGE)
+                near = turn(ahead_ref[pack, part, :], by - (member + 1) * EDGE)
+                value = jnp.where(right, far, jnp.where(left, near, value))
+            wide[at, comp * 8 : comp * 8 + 8, :] = value
+
+    strips = Jacobi(8, wide, coef_ref)
+    old = strips.run(s, even, odd)
+    main = Jacobi(s.q, main_rhs_ref, main_coef_ref)
     place = lax.broadcasted_iota(jnp.int32, (8, LANES), 1)
 
     def finish(row, held):
-        fresh = jacobi.next(old, row + s.depth)
-        main = jacobi.read(inner_ref, row)
+        fresh = main.next(main_ref, row + s.depth)
+        ends = strips.next(old, row + s.depth)
         for comp in range(3):
-            for half in range(len(fresh[comp])):
-                strip = fresh[comp][half]
-                value = jnp.where(place < s.depth, strip, main[comp][half])
-                fresh[comp][half] = jnp.where(place >= LANES - s.depth, turn(strip, HALF), value)
-        jacobi.write(sol_ref, row, fresh)
+            (strip,) = ends[comp]
+            for half in range(2):
+                by = half * SHIFT
+                value = jnp.where(place < s.depth, turn(strip, -by), fresh[comp][half])
+                fresh[comp][half] = jnp.where(place >= LANES - s.depth, turn(strip, HALF - by), value)
+        main.write(sol_ref, row, fresh)
         held[:, 0 : s.comps] = jnp.concatenate([x for each in fresh for x in each], axis=0).T
 
     def send(row, held):
@@ -589,11 +615,11 @@
     copy.wait()
 
 
-def outer(s, slots, main, rhs_strip, coef_strip, past, ahead):
-    state = pltpu.VMEM((s.wide, s.comps, LANES), jnp.float32)
+def outer(s, slots, tile, coef_strip, past, ahead):
+    state = pltpu.VMEM((s.wide, 24, LANES), jnp.float32)
     return pl.pallas_call(
         functools.partial(outer_kernel, s),
-        in_specs=[pl.BlockSpec(memory_space=pltpu.SMEM)] + [vmem_spec()] * 5,
+        in_specs=[pl.BlockSpec(memory_space=pltpu.SMEM)] + [vmem_spec()] * 7,
         out_specs=[pl.BlockSpec(memory_space=pltpu.HBM), vmem_spec()],
         out_shape=[
             pltpu.HBM((s.rows, s.comps, LANES), jnp.float32),
@@ -612,7 +638,7 @@
         ],
         name="outer",
         compiler_params=KERNEL,
-    )(slots, main, rhs_strip, coef_strip, in_vmem(past), in_vmem(ahead))
+    )(slots, *tile, coef_strip, in_vmem(past), in_vmem(ahead))
 
 
 def ring(axis):
@@ -652,7 +678,8 @@
     owner = cell_aggregate // s.agg
     local = cell_aggregate % s.agg
     slots = local // s.devices * s.devices + owner
-    coefs, *packs = prepare(s, block_inverse, off_blocks, operator_pattern)
+    slots, block_inverse = lax.optimization_barrier((slots, block_inverse))
+    coefs, *packs, coef_strip = prepare(s, block_inverse, off_blocks, operator_pattern)
 
     up, down = ring("row")
     lines, top, bottom = edges(s, received, slots, coefs)
@@ -663,8 +690,8 @@
     up, down = ring("col")
     ahead = lax.ppermute(right, "col", up)
     past = lax.ppermute(left, "col", down)
-    main, *strips = inner(s, rhs, coefs, before, after)
-    solved, outgoing = outer(s, slots, main, *strips, past, ahead)
+    tile = inner(s, rhs, coefs, before, after)
+    solved, outgoing = outer(s, slots, tile, coef_strip, past, ahead)
     correction = prolong(s, exchange(s, outgoing), restriction, pattern)
     coarse = solved.reshape(s.rows, 3, s.loads, LANES).transpose(2, 1, 0, 3)
     return coarse, correction.transpose(1, 0, 2)

time: 123 us -> 134 us (1.089)
  Pallas kernels: 49.2 us -> 62 us
  waiting for transfers between devices: 51.4 us -> 45.6 us
  local copies, waits for them, and re-layouts: 4.34 us -> 7.79 us
    all_to_all x2, waiting for transfers between devices: 51.4 us -> 45.6 us  [exchange(): lax.all_to_all(blocks, AXES, split_axis=0, concat_axis=0, tiled=True)]
    pallas_call x1, Pallas kernels: 9.04 us -> 14.3 us  [inner(): pl.pallas_call(functools.partial(inner_kernel, s), in_specs=[vmem_spec()]...]
    pallas_call x1, Pallas kernels: 16.6 us -> 20.9 us  [outer(): pl.pallas_call(functools.partial(outer_kernel, s), in_specs=[pl.BlockSpec...]
    unnamed x12 -> x20, local copies, waits for them, and re-layouts: 1.53 us -> 4.97 us
    pallas_call x1, Pallas kernels: 1.65 us -> 4.81 us  [prepare(): pl.pallas_call(functools.partial(prepare_kernel, s), in_specs=[vmem_spec(...]
  transfers between devices with their start and end apart: 6 -> 6, of which waited for: 2 -> 2; matrix products, arithmetic and copies ran while one was open for 3% -> 3% of each run, Pallas kernels for 14% -> 19%
where the time goes in v7:
time: 134 us; the launch traced here: 133 us
  Pallas kernels  62 us (46%)
  waiting for transfers between devices  45.6 us (34%)
  starting transfers between devices  16.6 us (12%)
  local copies, waits for them, and re-layouts  7.79 us (6%)
    all_to_all x2, waiting for transfers between devices, exchange(): lax.all_to_all(blocks, AXES, split_axis=0, concat_axis=0, tiled=True)  45.6 us
    pallas_call x1, Pallas kernels, outer(): pl.pallas_call(functools.partial(outer_kernel, s), in_specs=[pl.BlockSpec...  20.9 us
    pallas_call x1, Pallas kernels, inner(): pl.pallas_call(functools.partial(inner_kernel, s), in_specs=[vmem_spec()]...  14.3 us
    all_to_all x2, starting transfers between devices, exchange(): lax.all_to_all(blocks, AXES, split_axis=0, concat_axis=0, tiled=True)  13 us
    pallas_call x1, Pallas kernels, collect(): pl.pallas_call(functools.partial(collect_kernel, s), in_specs=[pl.BlockSp...  6.79 us
    pallas_call x1, Pallas kernels, restrict(): pl.pallas_call(functools.partial(restrict_kernel, s), in_specs=[pl.BlockS...  6.65 us
    pallas_call x1, Pallas kernels, prolong(): pl.pallas_call(functools.partial(prolong_kernel, s), in_specs=[vmem_spec(...  5.14 us
    unnamed x20, local copies, waits for them, and re-layouts  4.97 us
  transfers between devices with their start and end apart: 6, of which 2 were waited for; matrix products, arithmetic and copies ran while one was open for 3% of the time, Pallas kernels for 19%

profile of v7, /device:TPU:0, one launch (start us, length us, event | category | flops | bytes accessed | tf_op | source)
XLA Modules:
  0.0 133.4 jit_solution(9131448811432012249)
XLA Ops:
  0.6 6.6 %restrict.1 = f32[2304,128]{1,0:T(8,128)} custom-call(f32[3,16,49152]{2,1,0:T(8,128)} %bitcast.19, f32[3,3,49152]{2,1,0:T(4,128)} %rest_ref.1, s32[1,49152]{1,0:T(1,128)} %bitcast.23), custom_call_target="tpu_custom_call" | custom-call | tf_op jit(solution)/shard_map/restrict/pallas_call | solution.py:180
  7.3 0.0 copy-start.9
  7.3 7.3 %all-to-all-start = ((f32[32,72,128]{2,1,0:T(8,128)}), f32[32,72,128]{2,1,0:T(8,128)S(1)}, u32[]{:S(2)}, u32[]{:S(2)}) async-start(f32[32,72,128]{2,1,0:T(8,128)} %bitcast.2), calls=%async_computation | async-start | bytes 2359296 | tf_op jit(solution)/shard_map/all_to_all | solution.py:652
  14.6 0.0 copy-done.9
  14.6 0.6 fusion.2.slot_ref
  15.3 0.0 copy-start.1
  15.3 1.2 copy-done.1
  16.5 0.0 copy-start.3
  16.5 0.9 copy-done.3
  17.4 0.0 copy-start.4
  17.4 0.9 copy-done.4
  18.3 4.8 %prepare.1 = (f32[48,48,128]{2,1,0:T(8,128)S(1)}, f32[2,48,128]{2,1,0:T(8,128)S(1)}, f32[2,48,128]{2,1,0:T(8,128)S(1)}, f32[48,48,128]{2,1,0:T(8,128)S(1)}) custom-call(f32[432,128]{1,0:T(8,128)S(1)} %bitcast.17, f32[1728,128]{1,0:T(8,128)S(1)} %bitcast.16, s32[192,128]{1,0:T(8,128)S(1)} %bitcast.18), custom_call_target="tpu_custom_call" | custom-call | tf_op jit(solution)/shard_map/prepare/pallas_call | solution.py:403
  23.1 0.0 copy-start.5
  23.1 0.6 copy-done.5
  23.7 0.0 copy-start.7
  23.7 0.6 copy-done.7
  24.3 19.4 %all-to-all-done = f32[32,72,128]{2,1,0:T(8,128)S(1)} async-done(((f32[32,72,128]{2,1,0:T(8,128)}), f32[32,72,128]{2,1,0:T(8,128)S(1)}, u32[]{:S(2)}, u32[]{:S(2)}) %all-to-all-start) | async-done | bytes 1179680 | tf_op jit(solution)/shard_map/all_to_all | solution.py:652
  43.7 0.0 copy-start.2
  43.7 0.7 copy-done.2
  44.5 2.5 %edges.1 = (f32[6144,128]{1,0:T(8,128)S(1)}, f32[3,96,128]{2,1,0:T(8,128)S(1)}, f32[3,96,128]{2,1,0:T(8,128)S(1)}) custom-call(s32[48,128]{1,0:T(8,128)S(1)} %copy-done.2, f32[2304,128]{1,0:T(8,128)S(1)} %bitcast.15, f32[48,48,128]{2,1,0:T(8,128)S(1)} %get-tuple-element.21.coef_ref.own_ref), custom_call_target="tpu_custom_call" | custom-call | tf_op jit(solution)/shard_map/edges/pallas_call | solution.py:268
  47.0 0.8 collective-permute-start.1
  47.8 0.0 collective-permute-start
  47.8 0.0 copy-start.6
  47.8 0.0 copy-start.8
  47.8 6.8 %collect.1.rhs_ref.body_ref = f32[48,48,128]{2,1,0:T(8,128)S(1)} custom-call(s32[48,128]{1,0:T(8,128)S(1)} %copy-done.2, f32[6144,128]{1,0:T(8,128)S(1)} %get-tuple-element.22.lines, f32[3,96,128]{2,1,0:T(8,128)S(1)} %get-tuple-element.23.top_ref, f32[3,96,128]{2,1,0:T(8,128)S(1)} %get-tuple-element.24.bottom_ref), custom_call_target="tpu_custom_call" | custom-call | tf_op jit(solution)/shard_map/collect/pallas_call | solution.py:302
  54.6 0.0 collective-permute-done.1.after_ref
  54.6 0.0 collective-permute-done.before_ref
  54.6 0.0 copy-done.6
  54.7 0.0 copy-done.8
  54.7 0.8 pack_edges.1
  55.5 2.7 %collective-permute-start.2 = (f32[2,96,128]{2,1,0:T(8,128)S(1)}, f32[2,96,128]{2,1,0:T(8,128)S(1)}, u32[]{:S(2)}, u32[]{:S(2)}) collective-permute-start(f32[2,96,128]{2,1,0:T(8,128)S(1)} %get-tuple-element.32), channel_id=1, source_target_pairs={{1,0},{2,1},{3,2},{0,3},{5,4},{6,5},{7,6},{4,7},{9,8},{10,9},{11,1... | collective-permute-start | bytes 294920 | tf_op jit(solution)/shard_map/ppermute | solution.py:692
  58.2 0.0 collective-permute-start.3
  58.2 14.3 %inner.1 = (f32[54,48,128]{2,1,0:T(8,128)S(1)}, f32[54,48,128]{2,1,0:T(8,128)S(1)}, f32[54,48,128]{2,1,0:T(8,128)S(1)}, f32[54,24,128]{2,1,0:T(8,128)S(1)}) custom-call(f32[48,48,128]{2,1,0:T(8,128)S(1)} %collect.1.rhs_ref.body_ref, f32[48,48,128]{2,1,0:T(8,128)S(1)} %get-tuple-element.21.coef_ref.own_ref, ...), custom_call_target="tpu_custom_call" | custom-call | tf_op jit(solution)/shard_map/inner/pallas_call | solution.py:518
  72.5 0.0 collective-permute-done.2.past_ref
  72.5 0.0 collective-permute-done.3.ahead_ref
  72.5 20.9 %outer.1 = (f32[48,48,128]{2,1,0:T(8,128)}, f32[2304,128]{1,0:T(8,128)}) custom-call(s32[48,128]{1,0:T(8,128)S(1)} %copy-done.2, f32[54,48,128]{2,1,0:T(8,128)S(1)} %get-tuple-element.25.main_rhs_ref, f32[54,48,128]{2,1,0:T(8,128)S(1)} %get-tuple-element.26.main_coef_ref, f32[54,48,128]{2,1,0:T(8,128)S(1)} %get-tuple-element.27.main_ref, ...), custom_call_target="tpu_custom_call" | custom-call | tf_op jit(solution)/shard_map/outer/pallas_call | solution.py:620
  93.4 5.7 %all-to-all-start.1 = ((f32[32,72,128]{2,1,0:T(8,128)}), f32[32,72,128]{2,1,0:T(8,128)S(1)}, u32[]{:S(2)}, u32[]{:S(2)}) async-start(f32[32,72,128]{2,1,0:T(8,128)} %bitcast.9), calls=%async_computation.1 | async-start | bytes 2359296 | tf_op jit(solution)/shard_map/all_to_all | solution.py:652
  99.1 0.0 copy-start
  99.2 2.8 %copy.11 = f32[48,3,16,128]{3,0,1,2:T(8,128)} copy(f32[48,3,16,128]{3,2,1,0:T(8,128)} %bitcast.21) | data formatting | bytes 2359296 | tf_op jit(solution)/shard_map/reshape | solution.py:696
  102.0 26.3 %all-to-all-done.1 = f32[32,72,128]{2,1,0:T(8,128)S(1)} async-done(((f32[32,72,128]{2,1,0:T(8,128)}), f32[32,72,128]{2,1,0:T(8,128)S(1)}, u32[]{:S(2)}, u32[]{:S(2)}) %all-to-all-start.1) | async-done | bytes 1179680 | tf_op jit(solution)/shard_map/all_to_all | solution.py:652
  128.2 0.0 copy-done
  128.2 5.1 %prolong.1 = f32[3,16,49152]{2,1,0:T(8,128)} custom-call(f32[2304,128]{1,0:T(8,128)S(1)} %bitcast.14, f32[3,3,49152]{2,1,0:T(4,128)S(1)} %copy-done, s32[1,49152]{1,0:T(1,128)} %bitcast.24), custom_call_target="tpu_custom_call" | custom-call | tf_op jit(solution)/shard_map/prolong/pallas_call | solution.py:232
Async XLA Ops:
  7.3 7.4 %copy-start.9 = (s32[48,128]{1,0:T(8,128)S(1)}, s32[48,128]{1,0:T(8,128)}, u32[]{:S(2)}) copy-start(s32[48,128]{1,0:T(8,128)} %param.10) | copy-start | bytes 73732
  7.3 36.4 %all-to-all-start = ((f32[32,72,128]{2,1,0:T(8,128)}), f32[32,72,128]{2,1,0:T(8,128)S(1)}, u32[]{:S(2)}, u32[]{:S(2)}) async-start(f32[32,72,128]{2,1,0:T(8,128)} %bitcast.2), calls=%async_computation | async-start | bytes 2359296 | tf_op jit(solution)/shard_map/all_to_all | solution.py:652
  15.3 1.2 copy-start.1
  16.5 0.9 copy-start.3
  17.4 0.9 copy-start.4
  23.1 0.6 copy-start.5
  23.7 0.6 copy-start.7
  43.7 0.7 copy-start.2
  47.0 7.6 %collective-permute-start.1 = (f32[3,96,128]{2,1,0:T(8,128)S(1)}, f32[3,96,128]{2,1,0:T(8,128)S(1)}, u32[]{:S(2)}, u32[]{:S(2)}) collective-permute-start(f32[3,96,128]{2,1,0:T(8,128)S(1)} %get-tuple-element.23.top_ref), channel_id=1, source_target_pairs={{4,0},{8,4},{12,8},{16,12},{20,16},{24,20},{28,24},{0,28},{5,1},{9... | collective-permute-start | bytes 442376 | tf_op jit(solution)/shard_map/ppermute | solution.py:687
  47.8 6.8 %collective-permute-start = (f32[3,96,128]{2,1,0:T(8,128)S(1)}, f32[3,96,128]{2,1,0:T(8,128)S(1)}, u32[]{:S(2)}, u32[]{:S(2)}) collective-permute-start(f32[3,96,128]{2,1,0:T(8,128)S(1)} %get-tuple-element.24.bottom_ref), channel_id=1, source_target_pairs={{0,4},{4,8},{8,12},{12,16},{16,20},{20,24},{24,28},{28,0},{1,5},{5... | collective-permute-start | bytes 442376 | tf_op jit(solution)/shard_map/ppermute | solution.py:686
  47.8 6.8 %copy-start.6 = (f32[2,48,128]{2,1,0:T(8,128)S(1)}, f32[2,48,128]{2,1,0:T(8,128)}, u32[]{:S(2)}) copy-start(f32[2,48,128]{2,1,0:T(8,128)} %copy-done.5) | copy-start | bytes 147460
  47.8 6.8 %copy-start.8 = (f32[2,48,128]{2,1,0:T(8,128)S(1)}, f32[2,48,128]{2,1,0:T(8,128)}, u32[]{:S(2)}) copy-start(f32[2,48,128]{2,1,0:T(8,128)} %copy-done.7) | copy-start | bytes 147460
  55.5 17.0 %collective-permute-start.2 = (f32[2,96,128]{2,1,0:T(8,128)S(1)}, f32[2,96,128]{2,1,0:T(8,128)S(1)}, u32[]{:S(2)}, u32[]{:S(2)}) collective-permute-start(f32[2,96,128]{2,1,0:T(8,128)S(1)} %get-tuple-element.32), channel_id=1, source_target_pairs={{1,0},{2,1},{3,2},{0,3},{5,4},{6,5},{7,6},{4,7},{9,8},{10,9},{11,1... | collective-permute-start | bytes 294920 | tf_op jit(solution)/shard_map/ppermute | solution.py:692
  58.2 14.3 %collective-permute-start.3 = (f32[2,96,128]{2,1,0:T(8,128)S(1)}, f32[2,96,128]{2,1,0:T(8,128)S(1)}, u32[]{:S(2)}, u32[]{:S(2)}) collective-permute-start(f32[2,96,128]{2,1,0:T(8,128)S(1)} %get-tuple-element.33), channel_id=1, source_target_pairs={{0,1},{1,2},{2,3},{3,0},{4,5},{5,6},{6,7},{7,4},{8,9},{9,10},{10,1... | collective-permute-start | bytes 294920 | tf_op jit(solution)/shard_map/ppermute | solution.py:691
  93.4 34.8 %all-to-all-start.1 = ((f32[32,72,128]{2,1,0:T(8,128)}), f32[32,72,128]{2,1,0:T(8,128)S(1)}, u32[]{:S(2)}, u32[]{:S(2)}) async-start(f32[32,72,128]{2,1,0:T(8,128)} %bitcast.9), calls=%async_computation.1 | async-start | bytes 2359296 | tf_op jit(solution)/shard_map/all_to_all | solution.py:652
  99.1 29.1 %copy-start = (f32[3,3,49152]{2,1,0:T(4,128)S(1)}, f32[3,3,49152]{2,1,0:T(4,128)}, u32[]{:S(2)}) copy-start(f32[3,3,49152]{2,1,0:T(4,128)} %rest_ref.1) | copy-start | bytes 5308420

commit v8 on v5

--- a/solution.py
+++ b/solution.py
@@ -407,25 +407,31 @@
     )(inverse.reshape(-1, LANES), blocks.reshape(-1, LANES), pattern.reshape(-1, LANES))
 
 
+def inside_of(axis):
+    here = lax.axis_index(axis)
+    return [jnp.where(x, 1.0, 0.0) for x in (here > 0, here < lax.axis_size(axis) - 1)]
+
+
 def sweeps_kernel(
-    s, slot_ref, inside_ref, rhs_ref, own_ref, before_ref, after_ref, past_ref, ahead_ref,
+    s, slot_ref, rhs_ref, own_ref, before_ref, after_ref, past_ref, ahead_ref,
     sol_hbm, out_ref, wide, coef_ref, even, odd, sol_ref, lines, ahead_lines, behind_lines, sem,
 ):
     q = s.q
     halves = range(0, q, 8)
     lane = lax.broadcasted_iota(jnp.int32, (COEFS, LANES), 1)
-    side = jnp.where(lane < LANES // 2, inside_ref[3], inside_ref[2])
+    rows, columns = inside_of("row"), inside_of("col")
+    side = jnp.where(lane < LANES // 2, columns[1], columns[0])
     for held, inner_ref, part in (
         (wide, rhs_ref, slice(0, s.comps)),
         (coef_ref, own_ref, slice(s.comps, s.comps + COEFS)),
     ):
         for at in range(s.wide):
             if at < s.depth:
-                line, inside = before_ref[at, part, :], inside_ref[0]
+                line, inside = before_ref[at, part, :], rows[0]
             elif at < s.depth + s.rows:
                 line, inside = inner_ref[at - s.depth], None
             else:
-                line, inside = after_ref[at - s.depth - s.rows, part, :], inside_ref[1]
+                line, inside = after_ref[at - s.depth - s.rows, part, :], rows[1]
             pack, member = divmod(at, PACK)
             other = beyond(past_ref[pack, part, :], ahead_ref[pack, part, :], member, s.depth)
             if held is coef_ref:
@@ -549,11 +555,11 @@
     copy.wait()
 
 
-def sweeps(s, slots, inside, rhs, coefs, before, after, past, ahead):
+def sweeps(s, slots, rhs, coefs, before, after, past, ahead):
     state = pltpu.VMEM((s.wide, s.comps, 2 * LANES), jnp.float32)
     return pl.pallas_call(
         functools.partial(sweeps_kernel, s),
-        in_specs=[pl.BlockSpec(memory_space=pltpu.SMEM)] * 2 + [vmem_spec()] * 6,
+        in_specs=[pl.BlockSpec(memory_space=pltpu.SMEM)] + [vmem_spec()] * 6,
         out_specs=[pl.BlockSpec(memory_space=pltpu.HBM), vmem_spec()],
         out_shape=[
             pltpu.HBM((s.rows, s.comps, LANES), jnp.float32),
@@ -572,7 +578,7 @@
         ],
         name="sweeps",
         compiler_params=KERNEL,
-    )(slots, inside, rhs, coefs, *map(in_vmem, (before, after, past, ahead)))
+    )(slots, rhs, coefs, *map(in_vmem, (before, after, past, ahead)))
 
 
 def ring(axis):
@@ -614,12 +620,6 @@
     slots = local // s.devices * s.devices + owner
     coefs, *packs = prepare(s, block_inverse, off_blocks, operator_pattern)
 
-    ends = []
-    for axis in AXES:
-        here = lax.axis_index(axis)
-        ends += [here > 0, here < lax.axis_size(axis) - 1]
-    inside = jnp.stack(ends).astype(jnp.float32)
-
     up, down = ring("row")
     lines, top, bottom = edges(s, received, slots, coefs)
     before = lax.ppermute(bottom, "row", up)
@@ -629,7 +629,7 @@
     up, down = ring("col")
     ahead = lax.ppermute(right, "col", up)
     past = lax.ppermute(left, "col", down)
-    solved, outgoing = sweeps(s, slots, inside, rhs, coefs, before, after, past, ahead)
+    solved, outgoing = sweeps(s, slots, rhs, coefs, before, after, past, ahead)
     correction = prolong(s, exchange(s, outgoing), restriction, pattern)
     coarse = solved.reshape(s.rows, 3, s.loads, LANES).transpose(2, 1, 0, 3)
     return coarse, correction.transpose(1, 0, 2)

time: 123 us -> 119 us (0.967)
  local copies, waits for them, and re-layouts: 7.88 us -> 4.34 us
    unnamed x18 -> x12, local copies, waits for them, and re-layouts: 5.07 us -> 1.53 us
  transfers between devices with their start and end apart: 6 -> 6, of which waited for: 4 -> 4; matrix products, arithmetic and copies ran while one was open for 2% -> 3% of each run, Pallas kernels for 7% -> 7%
where the time goes in v8:
time: 119 us
  waiting for transfers between devices  57.7 us (48%)
  Pallas kernels  41.7 us (35%)
  starting transfers between devices  13.5 us (11%)
  local copies, waits for them, and re-layouts  4.34 us (4%)
    all_to_all x2, waiting for transfers between devices, exchange(): lax.all_to_all(blocks, AXES, split_axis=0, concat_axis=0, tiled=True)  51.4 us
    pallas_call x1, Pallas kernels, sweeps(): pl.pallas_call(functools.partial(sweeps_kernel, s), in_specs=[pl.BlockSpe...  18.1 us
    all_to_all x2, starting transfers between devices, exchange(): lax.all_to_all(blocks, AXES, split_axis=0, concat_axis=0, tiled=True)  10 us
    pallas_call x1, Pallas kernels, collect(): pl.pallas_call(functools.partial(collect_kernel, s), in_specs=[pl.BlockSp...  6.79 us
    pallas_call x1, Pallas kernels, restrict(): pl.pallas_call(functools.partial(restrict_kernel, s), in_specs=[pl.BlockS...  6.65 us
    pallas_call x1, Pallas kernels, prolong(): pl.pallas_call(functools.partial(prolong_kernel, s), in_specs=[vmem_spec(...  5.14 us
    ppermute x1, waiting for transfers between devices, body(): past = lax.ppermute(left, 'col', down)  3.18 us
    ppermute x1, waiting for transfers between devices, body(): ahead = lax.ppermute(right, 'col', up)  3.12 us
  transfers between devices with their start and end apart: 6, of which 4 were waited for; matrix products, arithmetic and copies ran while one was open for 3% of the time, Pallas kernels for 7%

profile of v8, /device:TPU:0, one launch (start us, length us, event | category | flops | bytes accessed | tf_op | source)
XLA Modules:
  0.0 118.8 jit_solution(4416105926893973524)
XLA Ops:
  0.6 6.6 %restrict.1 = f32[2304,128]{1,0:T(8,128)} custom-call(f32[3,16,49152]{2,1,0:T(8,128)} %bitcast.19, f32[3,3,49152]{2,1,0:T(4,128)} %rest_ref.1, s32[1,49152]{1,0:T(1,128)} %bitcast.23), custom_call_target="tpu_custom_call" | custom-call | tf_op jit(solution)/shard_map/restrict/pallas_call | solution.py:180
  7.3 0.0 copy-start.1
  7.3 0.0 copy-start.2
  7.3 7.3 %all-to-all-start = ((f32[32,72,128]{2,1,0:T(8,128)}), f32[32,72,128]{2,1,0:T(8,128)S(1)}, u32[]{:S(2)}, u32[]{:S(2)}) async-start(f32[32,72,128]{2,1,0:T(8,128)} %bitcast.2), calls=%async_computation | async-start | bytes 2359296 | tf_op jit(solution)/shard_map/all_to_all | solution.py:592
  14.6 0.0 copy-done.1
  14.7 0.0 copy-done.2
  14.7 0.0 copy-start.3
  14.7 0.9 copy-done.3
  15.6 1.6 %prepare.1 = (f32[48,48,128]{2,1,0:T(8,128)S(1)}, f32[2,48,128]{2,1,0:T(8,128)S(1)}, f32[2,48,128]{2,1,0:T(8,128)S(1)}) custom-call(f32[432,128]{1,0:T(8,128)S(1)} %bitcast.17, f32[1728,128]{1,0:T(8,128)S(1)} %bitcast.16, s32[192,128]{1,0:T(8,128)S(1)} %bitcast.18), custom_call_target="tpu_custom_call" | custom-call | tf_op jit(solution)/shard_map/prepare/pallas_call | solution.py:399
  17.2 0.0 copy-start.4
  17.2 0.6 copy-done.4
  17.8 0.8 fusion.2.slot_ref
  18.6 25.1 %all-to-all-done = f32[32,72,128]{2,1,0:T(8,128)S(1)} async-done(((f32[32,72,128]{2,1,0:T(8,128)}), f32[32,72,128]{2,1,0:T(8,128)S(1)}, u32[]{:S(2)}, u32[]{:S(2)}) %all-to-all-start) | async-done | bytes 1179680 | tf_op jit(solution)/shard_map/all_to_all | solution.py:592
  43.7 2.5 %edges.1 = (f32[6144,128]{1,0:T(8,128)S(1)}, f32[3,96,128]{2,1,0:T(8,128)S(1)}, f32[3,96,128]{2,1,0:T(8,128)S(1)}) custom-call(s32[48,128]{1,0:T(8,128)S(1)} %fusion.2.slot_ref, f32[2304,128]{1,0:T(8,128)S(1)} %bitcast.15, f32[48,48,128]{2,1,0:T(8,128)S(1)} %get-tuple-element.12.coef_ref.own_ref), custom_call_target="tpu_custom_call" | custom-call | tf_op jit(solution)/shard_map/edges/pallas_call | solution.py:268
  46.3 0.8 collective-permute-start.1
  47.1 0.0 collective-permute-start
  47.1 0.0 copy-start.5
  47.1 6.8 %collect.1.body_ref.rhs_ref = f32[48,48,128]{2,1,0:T(8,128)S(1)} custom-call(s32[48,128]{1,0:T(8,128)S(1)} %fusion.2.slot_ref, f32[6144,128]{1,0:T(8,128)S(1)} %get-tuple-element.13.lines, f32[3,96,128]{2,1,0:T(8,128)S(1)} %get-tuple-element.14.top_ref, f32[3,96,128]{2,1,0:T(8,128)S(1)} %get-tuple-element.15.bottom_ref), custom_call_target="tpu_custom_call" | custom-call | tf_op jit(solution)/shard_map/collect/pallas_call | solution.py:302
  53.9 0.0 collective-permute-done.1.after_ref
  53.9 0.0 collective-permute-done.before_ref
  53.9 0.0 copy-done.5
  53.9 0.8 pack_edges.1
  54.8 2.7 %collective-permute-start.2 = (f32[2,96,128]{2,1,0:T(8,128)S(1)}, f32[2,96,128]{2,1,0:T(8,128)S(1)}, u32[]{:S(2)}, u32[]{:S(2)}) collective-permute-start(f32[2,96,128]{2,1,0:T(8,128)S(1)} %get-tuple-element.18), channel_id=1, source_target_pairs={{1,0},{2,1},{3,2},{0,3},{5,4},{6,5},{7,6},{4,7},{9,8},{10,9},{11,1... | collective-permute-start | bytes 294920 | tf_op jit(solution)/shard_map/ppermute | solution.py:631
  57.5 0.0 collective-permute-start.3
  57.5 3.2 %collective-permute-done.2.past_ref = f32[2,96,128]{2,1,0:T(8,128)S(1)} collective-permute-done((f32[2,96,128]{2,1,0:T(8,128)S(1)}, f32[2,96,128]{2,1,0:T(8,128)S(1)}, u32[]{:S(2)}, u32[]{:S(2)}) %collective-permute-start.2) | collective-permute-done | bytes 98336 | tf_op jit(solution)/shard_map/ppermute | solution.py:631
  60.6 3.1 %collective-permute-done.3.ahead_ref = f32[2,96,128]{2,1,0:T(8,128)S(1)} collective-permute-done((f32[2,96,128]{2,1,0:T(8,128)S(1)}, f32[2,96,128]{2,1,0:T(8,128)S(1)}, u32[]{:S(2)}, u32[]{:S(2)}) %collective-permute-start.3) | collective-permute-done | bytes 98336 | tf_op jit(solution)/shard_map/ppermute | solution.py:630
  63.8 18.1 %sweeps.1 = (f32[48,48,128]{2,1,0:T(8,128)}, f32[2304,128]{1,0:T(8,128)}) custom-call(s32[48,128]{1,0:T(8,128)S(1)} %fusion.2.slot_ref, f32[48,48,128]{2,1,0:T(8,128)S(1)} %collect.1.body_ref.rhs_ref, f32[48,48,128]{2,1,0:T(8,128)S(1)} %get-tuple-element.12.coef_ref.own_ref, f32[3,96,128]{2,1,0:T(8,128)S(1)} %collective-permute-done.before_ref, ...), custom_call_target="tpu_custom_call" | custom-call | tf_op jit(solution)/shard_map/sweeps/pallas_call | solution.py:560
  81.9 2.7 %all-to-all-start.1 = ((f32[32,72,128]{2,1,0:T(8,128)}), f32[32,72,128]{2,1,0:T(8,128)S(1)}, u32[]{:S(2)}, u32[]{:S(2)}) async-start(f32[32,72,128]{2,1,0:T(8,128)} %bitcast.9), calls=%async_computation.1 | async-start | bytes 2359296 | tf_op jit(solution)/shard_map/all_to_all | solution.py:592
  84.6 0.0 copy-start
  84.6 2.8 %copy.11 = f32[48,3,16,128]{3,0,1,2:T(8,128)} copy(f32[48,3,16,128]{3,2,1,0:T(8,128)} %bitcast.22) | data formatting | bytes 2359296 | tf_op jit(solution)/shard_map/reshape | solution.py:634
  87.4 26.3 %all-to-all-done.1 = f32[32,72,128]{2,1,0:T(8,128)S(1)} async-done(((f32[32,72,128]{2,1,0:T(8,128)}), f32[32,72,128]{2,1,0:T(8,128)S(1)}, u32[]{:S(2)}, u32[]{:S(2)}) %all-to-all-start.1) | async-done | bytes 1179680 | tf_op jit(solution)/shard_map/all_to_all | solution.py:592
  113.7 0.0 copy-done
  113.7 5.1 %prolong.1 = f32[3,16,49152]{2,1,0:T(8,128)} custom-call(f32[2304,128]{1,0:T(8,128)S(1)} %bitcast.14, f32[3,3,49152]{2,1,0:T(4,128)S(1)} %copy-done, s32[1,49152]{1,0:T(1,128)} %bitcast.24), custom_call_target="tpu_custom_call" | custom-call | tf_op jit(solution)/shard_map/prolong/pallas_call | solution.py:232
Async XLA Ops:
  7.3 7.4 %copy-start.1 = (f32[4,3,3,48,128]{4,3,2,1,0:T(8,128)S(1)}, f32[4,3,3,48,128]{4,3,2,1,0:T(8,128)}, u32[]{:S(2)}) copy-start(f32[4,3,3,48,128]{4,3,2,1,0:T(8,128)} %param.12) | copy-start | bytes 2654212
  7.3 7.4 %copy-start.2 = (f32[3,3,48,128]{3,2,1,0:T(8,128)S(1)}, f32[3,3,48,128]{3,2,1,0:T(8,128)}, u32[]{:S(2)}) copy-start(f32[3,3,48,128]{3,2,1,0:T(8,128)} %param.11) | copy-start | bytes 663556
  7.3 36.4 %all-to-all-start = ((f32[32,72,128]{2,1,0:T(8,128)}), f32[32,72,128]{2,1,0:T(8,128)S(1)}, u32[]{:S(2)}, u32[]{:S(2)}) async-start(f32[32,72,128]{2,1,0:T(8,128)} %bitcast.2), calls=%async_computation | async-start | bytes 2359296 | tf_op jit(solution)/shard_map/all_to_all | solution.py:592
  14.7 0.9 copy-start.3
  17.2 0.6 copy-start.4
  46.3 7.6 %collective-permute-start.1 = (f32[3,96,128]{2,1,0:T(8,128)S(1)}, f32[3,96,128]{2,1,0:T(8,128)S(1)}, u32[]{:S(2)}, u32[]{:S(2)}) collective-permute-start(f32[3,96,128]{2,1,0:T(8,128)S(1)} %get-tuple-element.14.top_ref), channel_id=1, source_target_pairs={{4,0},{8,4},{12,8},{16,12},{20,16},{24,20},{28,24},{0,28},{5,1},{9... | collective-permute-start | bytes 442376 | tf_op jit(solution)/shard_map/ppermute | solution.py:626
  47.1 6.8 %collective-permute-start = (f32[3,96,128]{2,1,0:T(8,128)S(1)}, f32[3,96,128]{2,1,0:T(8,128)S(1)}, u32[]{:S(2)}, u32[]{:S(2)}) collective-permute-start(f32[3,96,128]{2,1,0:T(8,128)S(1)} %get-tuple-element.15.bottom_ref), channel_id=1, source_target_pairs={{0,4},{4,8},{8,12},{12,16},{16,20},{20,24},{24,28},{28,0},{1,5},{5... | collective-permute-start | bytes 442376 | tf_op jit(solution)/shard_map/ppermute | solution.py:625
  47.1 6.8 %copy-start.5 = (f32[2,48,128]{2,1,0:T(8,128)S(1)}, f32[2,48,128]{2,1,0:T(8,128)}, u32[]{:S(2)}) copy-start(f32[2,48,128]{2,1,0:T(8,128)} %copy-done.4) | copy-start | bytes 147460
  54.8 5.9 %collective-permute-start.2 = (f32[2,96,128]{2,1,0:T(8,128)S(1)}, f32[2,96,128]{2,1,0:T(8,128)S(1)}, u32[]{:S(2)}, u32[]{:S(2)}) collective-permute-start(f32[2,96,128]{2,1,0:T(8,128)S(1)} %get-tuple-element.18), channel_id=1, source_target_pairs={{1,0},{2,1},{3,2},{0,3},{5,4},{6,5},{7,6},{4,7},{9,8},{10,9},{11,1... | collective-permute-start | bytes 294920 | tf_op jit(solution)/shard_map/ppermute | solution.py:631
  57.5 6.3 %collective-permute-start.3 = (f32[2,96,128]{2,1,0:T(8,128)S(1)}, f32[2,96,128]{2,1,0:T(8,128)S(1)}, u32[]{:S(2)}, u32[]{:S(2)}) collective-permute-start(f32[2,96,128]{2,1,0:T(8,128)S(1)} %get-tuple-element.19), channel_id=1, source_target_pairs={{0,1},{1,2},{2,3},{3,0},{4,5},{5,6},{6,7},{7,4},{8,9},{9,10},{10,1... | collective-permute-start | bytes 294920 | tf_op jit(solution)/shard_map/ppermute | solution.py:630
  81.9 31.8 %all-to-all-start.1 = ((f32[32,72,128]{2,1,0:T(8,128)}), f32[32,72,128]{2,1,0:T(8,128)S(1)}, u32[]{:S(2)}, u32[]{:S(2)}) async-start(f32[32,72,128]{2,1,0:T(8,128)} %bitcast.9), calls=%async_computation.1 | async-start | bytes 2359296 | tf_op jit(solution)/shard_map/all_to_all | solution.py:592
  84.6 29.1 %copy-start = (f32[3,3,49152]{2,1,0:T(4,128)S(1)}, f32[3,3,49152]{2,1,0:T(4,128)}, u32[]{:S(2)}) copy-start(f32[3,3,49152]{2,1,0:T(4,128)} %rest_ref.1) | copy-start | bytes 5308420

commit v9 on v8

--- a/solution.py
+++ b/solution.py
@@ -251,8 +251,11 @@
         held[lane : lane + 1, :] = lines[pl.ds(slot, 1), :]
 
 
-def edges_kernel(s, slot_ref, in_ref, coef_ref, lines, top_ref, bottom_ref, *held):
+def edges_kernel(s, slot_vmem, in_ref, coef_ref, lines, top_ref, bottom_ref, slot_ref, sem, *held):
+    fetch = pltpu.make_async_copy(slot_vmem, slot_ref, sem)
+    fetch.start()
     lines_from_tiles(s, in_ref, lines)
+    fetch.wait()
     places = []
     for at in range(s.depth):
         places += [(at, top_ref, at), (s.rows - s.depth + at, bottom_ref, at)]
@@ -263,17 +266,21 @@
         target[at, s.comps :, :] = coef_ref[row]
 
 
+def slot_scratch(s):
+    return [pltpu.SMEM((s.rows, LANES), jnp.int32), pltpu.SemaphoreType.DMA]
+
+
 def edges(s, received, slots, coefs):
     edge = vmem_result(s.depth, s.comps + COEFS, LANES)
     return pl.pallas_call(
         functools.partial(edges_kernel, s),
-        in_specs=[pl.BlockSpec(memory_space=pltpu.SMEM)] + [vmem_spec()] * 2,
+        in_specs=[vmem_spec()] * 3,
         out_specs=[vmem_spec()] * 3,
         out_shape=[vmem_result(s.agg, LANES), edge, edge],
-        scratch_shapes=[pltpu.VMEM((LANES, LANES), jnp.float32)] * (2 * s.depth),
+        scratch_shapes=slot_scratch(s) + [pltpu.VMEM((LANES, LANES), jnp.float32)] * (2 * s.depth),
         name="edges",
         compiler_params=KERNEL,
-    )(slots, in_vmem(received), coefs)
+    )(in_vmem(slots), in_vmem(received), coefs)
 
 
 def collect_kernel(s, slot_ref, lines, top_ref, bottom_ref, out_ref, even, odd):
@@ -413,11 +420,13 @@
 
 
 def sweeps_kernel(
-    s, slot_ref, rhs_ref, own_ref, before_ref, after_ref, past_ref, ahead_ref,
-    sol_hbm, out_ref, wide, coef_ref, even, odd, sol_ref, lines, ahead_lines, behind_lines, sem,
+    s, slot_vmem, rhs_ref, own_ref, before_ref, after_ref, past_ref, ahead_ref,
+    sol_hbm, out_ref, wide, coef_ref, even, odd, sol_ref, lines, ahead_lines, behind_lines, sem, slot_ref, slot_sem,
 ):
     q = s.q
     halves = range(0, q, 8)
+    fetch = pltpu.make_async_copy(slot_vmem, slot_ref, slot_sem)
+    fetch.start()
     lane = lax.broadcasted_iota(jnp.int32, (COEFS, LANES), 1)
     rows, columns = inside_of("row"), inside_of("col")
     side = jnp.where(lane < LANES // 2, columns[1], columns[0])
@@ -467,13 +476,14 @@
             for half, low in enumerate(halves):
                 target[at, span(comp, low), column] = fresh[comp][half]
 
-    def first(at, carry):
-        for column in columns:
-            total = [[wide[at, span(comp, low), column] for low in halves] for comp in range(3)]
-            put(even, at, invert(at, total, column), column)
+    def first(k, carry):
+        for at in (2 * k, 2 * k + 1):
+            for column in columns:
+                total = [[wide[at, span(comp, low), column] for low in halves] for comp in range(3)]
+                put(even, at, invert(at, total, column), column)
         return carry
 
-    lax.fori_loop(0, s.wide, first, 0)
+    lax.fori_loop(0, s.wide // 2, first, 0)
 
     def turned(old, at):
         west = ([], [])
@@ -537,6 +547,7 @@
 
     finish(0, ahead_lines)
     finish(1, behind_lines)
+    fetch.wait()
 
     def two(k, carry):
         row = 2 * k
@@ -559,7 +570,7 @@
     state = pltpu.VMEM((s.wide, s.comps, 2 * LANES), jnp.float32)
     return pl.pallas_call(
         functools.partial(sweeps_kernel, s),
-        in_specs=[pl.BlockSpec(memory_space=pltpu.SMEM)] + [vmem_spec()] * 6,
+        in_specs=[vmem_spec()] * 7,
         out_specs=[pl.BlockSpec(memory_space=pltpu.HBM), vmem_spec()],
         out_shape=[
             pltpu.HBM((s.rows, s.comps, LANES), jnp.float32),
@@ -575,10 +586,11 @@
             pltpu.VMEM((LANES, LANES), jnp.float32),
             pltpu.VMEM((LANES, LANES), jnp.float32),
             pltpu.SemaphoreType.DMA,
+            *slot_scratch(s),
         ],
         name="sweeps",
         compiler_params=KERNEL,
-    )(slots, rhs, coefs, *map(in_vmem, (before, after, past, ahead)))
+    )(in_vmem(slots), rhs, coefs, *map(in_vmem, (before, after, past, ahead)))
 
 
 def ring(axis):

time: 119 us -> 118 us (level)
  no operation moved by 1% of the time
where the time goes in v9:
time: 118 us
  waiting for transfers between devices  57.7 us (49%)
  Pallas kernels  40.6 us (34%)
  starting transfers between devices  13.5 us (11%)
  local copies, waits for them, and re-layouts  4.34 us (4%)
    all_to_all x2, waiting for transfers between devices, exchange(): lax.all_to_all(blocks, AXES, split_axis=0, concat_axis=0, tiled=True)  51.4 us
    pallas_call x1, Pallas kernels, sweeps(): pl.pallas_call(functools.partial(sweeps_kernel, s), in_specs=[vmem_spec()...  17 us
    all_to_all x2, starting transfers between devices, exchange(): lax.all_to_all(blocks, AXES, split_axis=0, concat_axis=0, tiled=True)  10 us
    pallas_call x1, Pallas kernels, collect(): pl.pallas_call(functools.partial(collect_kernel, s), in_specs=[pl.BlockSp...  6.79 us
    pallas_call x1, Pallas kernels, restrict(): pl.pallas_call(functools.partial(restrict_kernel, s), in_specs=[pl.BlockS...  6.65 us
    pallas_call x1, Pallas kernels, prolong(): pl.pallas_call(functools.partial(prolong_kernel, s), in_specs=[vmem_spec(...  5.14 us
    ppermute x1, waiting for transfers between devices, body(): past = lax.ppermute(left, 'col', down)  3.18 us
    ppermute x1, waiting for transfers between devices, body(): ahead = lax.ppermute(right, 'col', up)  3.13 us
  transfers between devices with their start and end apart: 6, of which 4 were waited for; matrix products, arithmetic and copies ran while one was open for 3% of the time, Pallas kernels for 7%

profile of v9, /device:TPU:0, one launch (start us, length us, event | category | flops | bytes accessed | tf_op | source)
XLA Modules:
  0.0 117.7 jit_solution(1406586857820729478)
XLA Ops:
  0.6 6.6 %restrict.1 = f32[2304,128]{1,0:T(8,128)} custom-call(f32[3,16,49152]{2,1,0:T(8,128)} %bitcast.19, f32[3,3,49152]{2,1,0:T(4,128)} %rest_ref.1, s32[1,49152]{1,0:T(1,128)} %bitcast.23), custom_call_target="tpu_custom_call" | custom-call | tf_op jit(solution)/shard_map/restrict/pallas_call | solution.py:180
  7.3 0.0 copy-start.1
  7.3 0.0 copy-start.2
  7.3 7.3 %all-to-all-start = ((f32[32,72,128]{2,1,0:T(8,128)}), f32[32,72,128]{2,1,0:T(8,128)S(1)}, u32[]{:S(2)}, u32[]{:S(2)}) async-start(f32[32,72,128]{2,1,0:T(8,128)} %bitcast.2), calls=%async_computation | async-start | bytes 2359296 | tf_op jit(solution)/shard_map/all_to_all | solution.py:604
  14.6 0.0 copy-done.1
  14.7 0.0 copy-done.2
  14.7 0.0 copy-start.3
  14.7 0.9 copy-done.3
  15.6 1.6 %prepare.1 = (f32[48,48,128]{2,1,0:T(8,128)S(1)}, f32[2,48,128]{2,1,0:T(8,128)S(1)}, f32[2,48,128]{2,1,0:T(8,128)S(1)}) custom-call(f32[432,128]{1,0:T(8,128)S(1)} %bitcast.17, f32[1728,128]{1,0:T(8,128)S(1)} %bitcast.16, s32[192,128]{1,0:T(8,128)S(1)} %bitcast.18), custom_call_target="tpu_custom_call" | custom-call | tf_op jit(solution)/shard_map/prepare/pallas_call | solution.py:406
  17.2 0.0 copy-start.4
  17.2 0.6 copy-done.4
  17.8 0.8 fusion.2.slot_vmem.slot_ref
  18.6 25.1 %all-to-all-done = f32[32,72,128]{2,1,0:T(8,128)S(1)} async-done(((f32[32,72,128]{2,1,0:T(8,128)}), f32[32,72,128]{2,1,0:T(8,128)S(1)}, u32[]{:S(2)}, u32[]{:S(2)}) %all-to-all-start) | async-done | bytes 1179680 | tf_op jit(solution)/shard_map/all_to_all | solution.py:604
  43.7 2.5 %edges.1 = (f32[6144,128]{1,0:T(8,128)S(1)}, f32[3,96,128]{2,1,0:T(8,128)S(1)}, f32[3,96,128]{2,1,0:T(8,128)S(1)}) custom-call(s32[48,128]{1,0:T(8,128)S(1)} %fusion.2.slot_vmem.slot_ref, f32[2304,128]{1,0:T(8,128)S(1)} %bitcast.15, f32[48,48,128]{2,1,0:T(8,128)S(1)} %get-tuple-element.12.coef_ref.own_ref), custom_call_target="tpu_custom_call" | custom-call | tf_op jit(solution)/shard_map/edges/pallas_call | solution.py:275
  46.2 0.8 collective-permute-start.1
  47.1 0.0 collective-permute-start
  47.1 0.0 copy-start.5
  47.1 6.8 %collect.1.body_ref.rhs_ref = f32[48,48,128]{2,1,0:T(8,128)S(1)} custom-call(s32[48,128]{1,0:T(8,128)S(1)} %fusion.2.slot_vmem.slot_ref, f32[6144,128]{1,0:T(8,128)S(1)} %get-tuple-element.13.lines, f32[3,96,128]{2,1,0:T(8,128)S(1)} %get-tuple-element.14.top_ref, f32[3,96,128]{2,1,0:T(8,128)S(1)} %get-tuple-element.15.bottom_ref), custom_call_target="tpu_custom_call" | custom-call | tf_op jit(solution)/shard_map/collect/pallas_call | solution.py:309
  53.9 0.0 collective-permute-done.1.after_ref
  53.9 0.0 collective-permute-done.before_ref
  53.9 0.0 copy-done.5
  53.9 0.8 pack_edges.1
  54.7 2.7 %collective-permute-start.2 = (f32[2,96,128]{2,1,0:T(8,128)S(1)}, f32[2,96,128]{2,1,0:T(8,128)S(1)}, u32[]{:S(2)}, u32[]{:S(2)}) collective-permute-start(f32[2,96,128]{2,1,0:T(8,128)S(1)} %get-tuple-element.18), channel_id=1, source_target_pairs={{1,0},{2,1},{3,2},{0,3},{5,4},{6,5},{7,6},{4,7},{9,8},{10,9},{11,1... | collective-permute-start | bytes 294920 | tf_op jit(solution)/shard_map/ppermute | solution.py:643
  57.4 0.0 collective-permute-start.3
  57.4 3.2 %collective-permute-done.2.past_ref = f32[2,96,128]{2,1,0:T(8,128)S(1)} collective-permute-done((f32[2,96,128]{2,1,0:T(8,128)S(1)}, f32[2,96,128]{2,1,0:T(8,128)S(1)}, u32[]{:S(2)}, u32[]{:S(2)}) %collective-permute-start.2) | collective-permute-done | bytes 98336 | tf_op jit(solution)/shard_map/ppermute | solution.py:643
  60.6 3.1 %collective-permute-done.3.ahead_ref = f32[2,96,128]{2,1,0:T(8,128)S(1)} collective-permute-done((f32[2,96,128]{2,1,0:T(8,128)S(1)}, f32[2,96,128]{2,1,0:T(8,128)S(1)}, u32[]{:S(2)}, u32[]{:S(2)}) %collective-permute-start.3) | collective-permute-done | bytes 98336 | tf_op jit(solution)/shard_map/ppermute | solution.py:642
  63.7 17.0 %sweeps.1 = (f32[48,48,128]{2,1,0:T(8,128)}, f32[2304,128]{1,0:T(8,128)}) custom-call(s32[48,128]{1,0:T(8,128)S(1)} %fusion.2.slot_vmem.slot_ref, f32[48,48,128]{2,1,0:T(8,128)S(1)} %collect.1.body_ref.rhs_ref, f32[48,48,128]{2,1,0:T(8,128)S(1)} %get-tuple-element.12.coef_ref.own_ref, f32[3,96,128]{2,1,0:T(8,128)S(1)} %collective-permute-done.before_ref, ...), custom_call_target="tpu_custom_call" | custom-call | tf_op jit(solution)/shard_map/sweeps/pallas_call | solution.py:571
  80.8 2.7 %all-to-all-start.1 = ((f32[32,72,128]{2,1,0:T(8,128)}), f32[32,72,128]{2,1,0:T(8,128)S(1)}, u32[]{:S(2)}, u32[]{:S(2)}) async-start(f32[32,72,128]{2,1,0:T(8,128)} %bitcast.9), calls=%async_computation.1 | async-start | bytes 2359296 | tf_op jit(solution)/shard_map/all_to_all | solution.py:604
  83.5 0.0 copy-start
  83.5 2.8 %copy.11 = f32[48,3,16,128]{3,0,1,2:T(8,128)} copy(f32[48,3,16,128]{3,2,1,0:T(8,128)} %bitcast.22) | data formatting | bytes 2359296 | tf_op jit(solution)/shard_map/reshape | solution.py:646
  86.3 26.3 %all-to-all-done.1 = f32[32,72,128]{2,1,0:T(8,128)S(1)} async-done(((f32[32,72,128]{2,1,0:T(8,128)}), f32[32,72,128]{2,1,0:T(8,128)S(1)}, u32[]{:S(2)}, u32[]{:S(2)}) %all-to-all-start.1) | async-done | bytes 1179680 | tf_op jit(solution)/shard_map/all_to_all | solution.py:604
  112.5 0.0 copy-done
  112.5 5.1 %prolong.1 = f32[3,16,49152]{2,1,0:T(8,128)} custom-call(f32[2304,128]{1,0:T(8,128)S(1)} %bitcast.14, f32[3,3,49152]{2,1,0:T(4,128)S(1)} %copy-done, s32[1,49152]{1,0:T(1,128)} %bitcast.24), custom_call_target="tpu_custom_call" | custom-call | tf_op jit(solution)/shard_map/prolong/pallas_call | solution.py:232
Async XLA Ops:
  7.3 7.4 %copy-start.1 = (f32[4,3,3,48,128]{4,3,2,1,0:T(8,128)S(1)}, f32[4,3,3,48,128]{4,3,2,1,0:T(8,128)}, u32[]{:S(2)}) copy-start(f32[4,3,3,48,128]{4,3,2,1,0:T(8,128)} %param.12) | copy-start | bytes 2654212
  7.3 7.4 %copy-start.2 = (f32[3,3,48,128]{3,2,1,0:T(8,128)S(1)}, f32[3,3,48,128]{3,2,1,0:T(8,128)}, u32[]{:S(2)}) copy-start(f32[3,3,48,128]{3,2,1,0:T(8,128)} %param.11) | copy-start | bytes 663556
  7.3 36.4 %all-to-all-start = ((f32[32,72,128]{2,1,0:T(8,128)}), f32[32,72,128]{2,1,0:T(8,128)S(1)}, u32[]{:S(2)}, u32[]{:S(2)}) async-start(f32[32,72,128]{2,1,0:T(8,128)} %bitcast.2), calls=%async_computation | async-start | bytes 2359296 | tf_op jit(solution)/shard_map/all_to_all | solution.py:604
  14.7 0.9 copy-start.3
  17.2 0.6 copy-start.4
  46.2 7.6 %collective-permute-start.1 = (f32[3,96,128]{2,1,0:T(8,128)S(1)}, f32[3,96,128]{2,1,0:T(8,128)S(1)}, u32[]{:S(2)}, u32[]{:S(2)}) collective-permute-start(f32[3,96,128]{2,1,0:T(8,128)S(1)} %get-tuple-element.14.top_ref), channel_id=1, source_target_pairs={{4,0},{8,4},{12,8},{16,12},{20,16},{24,20},{28,24},{0,28},{5,1},{9... | collective-permute-start | bytes 442376 | tf_op jit(solution)/shard_map/ppermute | solution.py:638
  47.1 6.8 %collective-permute-start = (f32[3,96,128]{2,1,0:T(8,128)S(1)}, f32[3,96,128]{2,1,0:T(8,128)S(1)}, u32[]{:S(2)}, u32[]{:S(2)}) collective-permute-start(f32[3,96,128]{2,1,0:T(8,128)S(1)} %get-tuple-element.15.bottom_ref), channel_id=1, source_target_pairs={{0,4},{4,8},{8,12},{12,16},{16,20},{20,24},{24,28},{28,0},{1,5},{5... | collective-permute-start | bytes 442376 | tf_op jit(solution)/shard_map/ppermute | solution.py:637
  47.1 6.8 %copy-start.5 = (f32[2,48,128]{2,1,0:T(8,128)S(1)}, f32[2,48,128]{2,1,0:T(8,128)}, u32[]{:S(2)}) copy-start(f32[2,48,128]{2,1,0:T(8,128)} %copy-done.4) | copy-start | bytes 147460
  54.7 5.9 %collective-permute-start.2 = (f32[2,96,128]{2,1,0:T(8,128)S(1)}, f32[2,96,128]{2,1,0:T(8,128)S(1)}, u32[]{:S(2)}, u32[]{:S(2)}) collective-permute-start(f32[2,96,128]{2,1,0:T(8,128)S(1)} %get-tuple-element.18), channel_id=1, source_target_pairs={{1,0},{2,1},{3,2},{0,3},{5,4},{6,5},{7,6},{4,7},{9,8},{10,9},{11,1... | collective-permute-start | bytes 294920 | tf_op jit(solution)/shard_map/ppermute | solution.py:643
  57.4 6.3 %collective-permute-start.3 = (f32[2,96,128]{2,1,0:T(8,128)S(1)}, f32[2,96,128]{2,1,0:T(8,128)S(1)}, u32[]{:S(2)}, u32[]{:S(2)}) collective-permute-start(f32[2,96,128]{2,1,0:T(8,128)S(1)} %get-tuple-element.19), channel_id=1, source_target_pairs={{0,1},{1,2},{2,3},{3,0},{4,5},{5,6},{6,7},{7,4},{8,9},{9,10},{10,1... | collective-permute-start | bytes 294920 | tf_op jit(solution)/shard_map/ppermute | solution.py:642
  80.8 31.8 %all-to-all-start.1 = ((f32[32,72,128]{2,1,0:T(8,128)}), f32[32,72,128]{2,1,0:T(8,128)S(1)}, u32[]{:S(2)}, u32[]{:S(2)}) async-start(f32[32,72,128]{2,1,0:T(8,128)} %bitcast.9), calls=%async_computation.1 | async-start | bytes 2359296 | tf_op jit(solution)/shard_map/all_to_all | solution.py:604
  83.5 29.1 %copy-start = (f32[3,3,49152]{2,1,0:T(4,128)S(1)}, f32[3,3,49152]{2,1,0:T(4,128)}, u32[]{:S(2)}) copy-start(f32[3,3,49152]{2,1,0:T(4,128)} %rest_ref.1) | copy-start | bytes 5308420
